TPU v7x, 32 devices: a whole 2x2x4 slice. The times are simulated.
32 devices in a mesh: gx: 4 (over y, core), yz: 8 (over z, x).
Axes of the slice: x: 2, y: 2, z: 4, core: 2. Of those that a mesh axis runs over, the one named last changes fastest.
Arguments:
- gas_state: float32 [5, 64, 128, 256], P(None, 'gx', 'yz'), may hold values from -6 to 6
- parcel_speed: float32 [4, 8, 32, 4, 3, 128], P('gx', 'yz'), may hold values from -6 to 6
- parcel_mass: float32 [4, 8, 32, 4, 128], P('gx', 'yz'), may hold values from 0.3 to 3
- offsets: float32 [4, 8, 32, 4, 3, 128], P('gx', 'yz'), may hold values from 0 to 1
- cell_base: int32 [4, 8, 32, 4, 3, 128], P('gx', 'yz'), may hold values from 0 to 6, as said below
- block_tile: int32 [4, 8, 32, 4], P('gx', 'yz'), may hold values from 0 to 511
- block_count: int32 [4, 8, 32], P('gx', 'yz'), may hold values from 0 to 4, as said below
Outputs:
- gas_next: float32 [5, 64, 128, 256], P(None, 'gx', 'yz')
- speed_next: float32 [4, 8, 32, 4, 3, 128], P('gx', 'yz')
- mass_next: float32 [4, 8, 32, 4, 128], P('gx', 'yz')
Inputs may be any that keep to these rules, and one draw needn't show every extreme that they name: `block_count`: A device's live blocks for an owner are its first ones; in every draw some owner receives 4 live blocks from every device. `cell_base`: component 0, 1, 2 is at most 2, 2, 6, so that the base cell and the next cell along each dimension lie in the tile.
All inputs are finite; a program needn't handle non-finite values.
Results may differ from a plain program's by a relative error of at most 0.0003.
Values sent between devices are 32-bit elements; how exact they have to be, the bound alone decides.
No kernel may reach another device: no remote copies, remote signals or barrier semaphores. Data moves between devices by JAX's collectives and lax.ppermute only.
A program may use at most 128 MiB of HBM per device.

v0:
```python
import math

import jax
import jax.numpy as jnp
from jax import lax
from jax.sharding import PartitionSpec as P

TILE_X = 4
TILE_Y = 4
TILE_Z = 8


DIFFUSION = 0.1
CELL_MASS = 4.0
DRAG_RATE = 0.5
EVAPORATION = 0.3
LATENT_HEAT = 2.0


def extended(cells, sides, width):
    for axis, dim in sides:
        count = lax.axis_size(axis)
        ends = count - 1
        head = lax.slice_in_dim(cells, 0, width, axis=dim)
        tail = lax.slice_in_dim(cells, cells.shape[dim] - width, cells.shape[dim], axis=dim)
        cells = jnp.concatenate(
            [
                lax.ppermute(tail, axis, [(i, (i + 1) % count) for i in range(ends)]),
                cells,
                lax.ppermute(head, axis, [((i + 1) % count, i) for i in range(ends)]),
            ],
            axis=dim,
        )
    return cells


def split_tiles(block):
    fields, extent_x, extent_y, extent_z = block.shape
    grid = block.reshape(
        fields, extent_x // TILE_X, TILE_X, extent_y // TILE_Y, TILE_Y, extent_z // TILE_Z, TILE_Z
    )
    grid = grid.transpose(1, 3, 5, 0, 2, 4, 6)
    return grid.reshape(-1, fields, TILE_X * TILE_Y * TILE_Z)


def join_tiles(tile_data, extent_x, extent_y, extent_z):
    fields = tile_data.shape[1]
    grid = tile_data.reshape(
        extent_x // TILE_X, extent_y // TILE_Y, extent_z // TILE_Z, fields, TILE_X, TILE_Y, TILE_Z
    )
    return grid.transpose(3, 0, 4, 1, 5, 2, 6).reshape(fields, extent_x, extent_y, extent_z)


def laplace(padded):
    framed = jnp.pad(padded, ((0, 0), (0, 0), (0, 0), (1, 1)))
    centre = framed[:, 1:-1, 1:-1, 1:-1]
    beside_all = framed[:, 2:, 1:-1, 1:-1] + framed[:, :-2, 1:-1, 1:-1]
    beside_all = beside_all + framed[:, 1:-1, 2:, 1:-1] + framed[:, 1:-1, :-2, 1:-1]
    beside_all = beside_all + framed[:, 1:-1, 1:-1, 2:] + framed[:, 1:-1, 1:-1, :-2]
    return beside_all - 6.0 * centre


def weights_along(fraction, base_cell, extent):
    positions = jnp.arange(extent, dtype=jnp.int32)
    lower_hit = (base_cell[..., None] == positions).astype(jnp.float32)
    upper_hit = (base_cell[..., None] + 1 == positions).astype(jnp.float32)
    return (1.0 - fraction)[..., None] * lower_hit + fraction[..., None] * upper_hit


def parcel_update(tile_data, velocity, shifts, cells, mass_old, live):
    along_x = weights_along(shifts[:, 0], cells[:, 0], TILE_X)
    along_y = weights_along(shifts[:, 1], cells[:, 1], TILE_Y)
    along_z = weights_along(shifts[:, 2], cells[:, 2], TILE_Z)
    stencil = (
        along_x[:, :, :, None, None] * along_y[:, :, None, :, None] * along_z[:, :, None, None, :]
    )
    stencil = stencil.reshape(mass_old.shape + (TILE_X * TILE_Y * TILE_Z,))
    sampled = jnp.einsum("scq,spq->scp", tile_data, stencil, precision=lax.Precision.HIGHEST)
    radius = jnp.cbrt(mass_old)
    factor = DRAG_RATE / (radius * radius)
    alive = live > 0.5
    moved = (velocity + factor[:, None, :] * sampled[:, 0:3]) / (1.0 + factor[:, None, :])
    velocity_new = jnp.where(alive[:, None, None], moved, velocity)
    evap_loss = EVAPORATION * jax.nn.softplus(sampled[:, 3] - sampled[:, 4]) / radius
    mass_new = jnp.where(alive[:, None], mass_old / (1.0 + evap_loss), mass_old)
    vapour = mass_old - mass_new
    momentum = mass_old[:, None, :] * (velocity - velocity_new) + vapour[:, None, :] * velocity_new
    source = jnp.concatenate(
        [momentum, -LATENT_HEAT * vapour[:, None, :], vapour[:, None, :]], axis=1
    )
    source = source * live[:, None, None]
    deposit = jnp.einsum("scp,spq->scq", source, stencil, precision=lax.Precision.HIGHEST)
    return (velocity_new, mass_new, deposit)


def in_groups(tile_data, velocity, shifts, cells, mass_old, live):
    leading = live.shape
    slot_total = leading[0] * leading[1]
    group_size = math.gcd(slot_total, 64)

    def grouped(member):
        return member.reshape((slot_total // group_size, group_size) + member.shape[2:])

    def process(packed):
        return parcel_update(*packed)

    outcome = lax.map(
        process,
        tuple((grouped(member) for member in (tile_data, velocity, shifts, cells, mass_old, live))),
    )
    return tuple((member.reshape(leading + member.shape[2:]) for member in outcome))


def shards(gas_state, parcel_speed, parcel_mass, offsets, cell_base, block_tile, block_count):
    fields, extent_x, extent_y, extent_z = gas_state.shape
    devices, capacity = (block_tile.shape[2], block_tile.shape[3])
    slot_total = devices * capacity
    table = split_tiles(gas_state)
    tile_rows = table.shape[0]
    padded = extended(gas_state, (("gx", 1), ("yz", 2)), 1)
    diffused = laplace(padded)
    velocity = parcel_speed.reshape(devices, capacity, 3, -1)
    mass_old = parcel_mass.reshape(devices, capacity, -1)
    shifts = offsets.reshape(devices, capacity, 3, -1)
    cells = cell_base.reshape(devices, capacity, 3, -1)
    tile_index = block_tile.reshape(devices, capacity)
    counted = block_count.reshape(devices)
    live = lax.broadcasted_iota(jnp.int32, (devices, capacity), 1) < counted[:, None]
    wanted = lax.all_to_all(tile_index, ("gx", "yz"), split_axis=0, concat_axis=0, tiled=True)
    fetched = lax.all_to_all(table[wanted], ("gx", "yz"), split_axis=0, concat_axis=0, tiled=True)
    velocity_new, mass_new, deposit = in_groups(
        fetched, velocity, shifts, cells, mass_old, live.astype(jnp.float32)
    )
    arrived = lax.all_to_all(deposit, ("gx", "yz"), split_axis=0, concat_axis=0, tiled=True)
    summed = jax.ops.segment_sum(
        arrived.reshape(slot_total, fields, -1), wanted.reshape(-1), num_segments=tile_rows
    )
    source_field = join_tiles(summed, extent_x, extent_y, extent_z)
    gas_next = gas_state + DIFFUSION * diffused + source_field / CELL_MASS
    return (gas_next, velocity_new.reshape(parcel_speed.shape), mass_new.reshape(parcel_mass.shape))


def solution(mesh):
    in_specs = (
        P(None, "gx", "yz", None),
        P("gx", "yz", None, None, None, None),
        P("gx", "yz", None, None, None),
        P("gx", "yz", None, None, None, None),
        P("gx", "yz", None, None, None, None),
        P("gx", "yz", None, None),
        P("gx", "yz", None),
    )
    out_specs = (
        P(None, "gx", "yz", None),
        P("gx", "yz", None, None, None, None),
        P("gx", "yz", None, None, None),
    )
    return jax.shard_map(shards, mesh=mesh, in_specs=in_specs, out_specs=out_specs, check_vma=False)
```

profile of v0, /device:TPU:0, one launch (start us, length us, event | category | flops | bytes accessed | tf_op | source)
XLA Modules:
  0.0 171.6 jit_solution(17278127564476708110)
XLA Ops:
  0.6 1.4 copy.93
  2.0 7.3 %all-to-all-start = ((s32[32,1,4]{2,1,0:T(1,128)}), s32[32,1,4]{2,1,0:T(1,128)S(1)}, u32[]{:S(2)}, u32[]{:S(2)}) async-start(s32[32,1,4]{2,1,0:T(1,128)} %copy.93), calls=%async_computation | async-start | bytes 32768 | tf_op jit(solution)/shard_map/all_to_all | solution.py:129
  9.3 14.5 %reshape.245 = f32[5,4,4,4,4,32,8]{6,5,4,3,2,1,0:T(8,128)} reshape(f32[5,16,16,256]{3,2,1,0:T(8,128)} %param.9) | data formatting | bytes 2621440 | tf_op jit(solution)/shard_map/reshape | solution.py:39
  23.9 14.1 %copy.95 = f32[4,4,32,5,4,4,8]{2,1,0,6,5,4,3:T(4,128)} copy(f32[4,4,32,5,4,4,8]{6,2,5,1,4,0,3:T(8,128)} %bitcast.143) | data formatting | bytes 2621440 | tf_op jit(solution)/shard_map/transpose | solution.py:42
  37.9 6.5 %reshape.246 = f32[512,5,128]{0,2,1:T(8,128)S(1)} reshape(f32[4,4,32,5,4,4,8]{2,1,0,6,5,4,3:T(4,128)} %copy.95) | data formatting | bytes 2621440 | tf_op jit(solution)/shard_map/reshape | solution.py:43
  44.4 1.0 copy.98
  45.8 1.6 gather_fusion
  47.3 1.9 %copy.100 = f32[32,4,5,128]{3,1,2,0:T(4,128)} copy(f32[32,4,5,128]{3,2,1,0:T(8,128)} %bitcast.153) | data formatting | bytes 655360 | tf_op jit(solution)/shard_map/gather | solution.py:130
  49.2 5.9 %all-to-all-start.1 = ((f32[32,4,5,128]{3,1,2,0:T(4,128)}), f32[32,4,5,128]{3,1,2,0:T(4,128)}, u32[]{:S(2)}, u32[]{:S(2)}) async-start(f32[32,4,5,128]{3,1,2,0:T(4,128)} %copy.100), calls=%async_computation.1 | async-start | bytes 655360 | tf_op jit(solution)/shard_map/all_to_all | solution.py:130
  55.2 0.6 fusion.34
  55.8 2.1 %collective-permute-start.1 = (f32[5,1,16,256]{3,2,1,0:T(8,128)S(1)}, f32[5,1,16,256]{3,2,1,0:T(8,128)S(1)}, u32[]{:S(2)}, u32[]{:S(2)}) collective-permute-start(f32[5,1,16,256]{3,2,1,0:T(8,128)S(1)} %get-tuple-element.171), channel_id=1, source_target_pairs={{0,8},{8,16},{16,24},{1,9},{9,17},{17,25},{2,10},{10,18},{18,26},{... | collective-permute-start | bytes 245768 | tf_op jit(solution)/shard_map/ppermute | solution.py:28
  57.9 1.5 collective-permute-start
  59.4 0.6 broadcast.276
  60.0 0.7 reduce.7
  61.1 0.7 copy.102
  61.9 0.7 copy.103
  63.2 4.0 %all-to-all-done.1 = f32[32,4,5,128]{3,1,2,0:T(4,128)} async-done(((f32[32,4,5,128]{3,1,2,0:T(4,128)}), f32[32,4,5,128]{3,1,2,0:T(4,128)}, u32[]{:S(2)}, u32[]{:S(2)}) %all-to-all-start.1) | async-done | bytes 327712 | tf_op jit(solution)/shard_map/all_to_all | solution.py:130
  67.2 1.0 copy.101
  68.2 30.0 %while.14 = (s32[]{:T(128)}, f32[2,64,3,128]{3,2,1,0:T(4,128)}, f32[2,64,128]{2,1,0:T(8,128)}, f32[2,64,5,128]{3,2,1,0:T(8,128)}, f32[2,64]{1,0:T(2,128)S(1)}, /...) while((s32[]{:T(128)}, f32[2,64,3,128]{3,2,1,0:T(4,128)}, ...), condition=%wide.region_1.2_spmd, body=%wide.region_0.1_spmd.sunk | while | flops 128278592 | bytes 23332864 | solution.py:107
  68.3 0.9 dynamic-slice_bitcast_fusion.4
  69.2 0.9 dynamic-slice_bitcast_fusion.5
  70.5 0.6 broadcast_multiply_fusion.7
  71.2 3.7 %fusion.45 = f32[64,5,128]{2,1,0:T(8,128)S(1)} fusion(f32[64,128,128]{1,2,0:T(8,128)S(1)} %bitcast.141, f32[1,64,5,128]{3,1,0,2:T(8,128)S(1)} %constant_dynamic-slice_fusion.5), kind=kOutput, calls=%fused_computation.11.clone.1 | convolution fusion | flops 62914560 | bytes 4521984 | tf_op jit(solution)/shard_map/while/body/eval_jaxpr/scq,spq->scp/dot_general | solution.py:78
  75.8 6.6 %fusion.48 = f32[2,64,5,128]{3,2,1,0:T(8,128)S(1)} fusion(f32[2,64,5,128]{3,2,1,0:T(8,128)S(1)} %copy-done.3, s32[]{:T(128)S(6)} %copy.139, f32[64,128,128]{1,2,0:T(8,128)S(1)} %bitcast.142, f32[64,1,128]{2,1,0:T(1,128)S(1)} %get-tuple-element.272, f32[64,1,128]{2,1,0:T(1,128)S(1)} %get-tuple-element.276, f32[64,3,128]{2,1,0:T(4,128)S(1)} %get-tuple-element.277, ...), kind=kOutput, calls=%fused_computation.4.clone.1 | convolution fusion | flops 63037440 | bytes 4653572 | tf_op jit(solution)/shard_map/while/body/eval_jaxpr/scp,spq->scq/dot_general | solution.py:92
  82.5 0.8 copy-done.4
  83.3 0.9 dynamic-slice_bitcast_fusion.4
  84.2 0.9 dynamic-slice_bitcast_fusion.5
  85.5 0.6 broadcast_multiply_fusion.7
  86.2 3.7 %fusion.45 = f32[64,5,128]{2,1,0:T(8,128)S(1)} fusion(f32[64,128,128]{1,2,0:T(8,128)S(1)} %bitcast.141, f32[1,64,5,128]{3,1,0,2:T(8,128)S(1)} %constant_dynamic-slice_fusion.5), kind=kOutput, calls=%fused_computation.11.clone.1 | convolution fusion | flops 62914560 | bytes 4521984 | tf_op jit(solution)/shard_map/while/body/eval_jaxpr/scq,spq->scp/dot_general | solution.py:78
  90.8 6.6 %fusion.48 = f32[2,64,5,128]{3,2,1,0:T(8,128)S(1)} fusion(f32[2,64,5,128]{3,2,1,0:T(8,128)S(1)} %copy-done.3, s32[]{:T(128)S(6)} %copy.139, f32[64,128,128]{1,2,0:T(8,128)S(1)} %bitcast.142, f32[64,1,128]{2,1,0:T(1,128)S(1)} %get-tuple-element.272, f32[64,1,128]{2,1,0:T(1,128)S(1)} %get-tuple-element.276, f32[64,3,128]{2,1,0:T(4,128)S(1)} %get-tuple-element.277, ...), kind=kOutput, calls=%fused_computation.4.clone.1 | convolution fusion | flops 63037440 | bytes 4653572 | tf_op jit(solution)/shard_map/while/body/eval_jaxpr/scp,spq->scq/dot_general | solution.py:92
  97.5 0.8 copy-done.4
  98.2 1.9 %copy.108 = f32[32,4,5,128]{3,1,2,0:T(4,128)} copy(f32[32,4,5,128]{3,2,1,0:T(8,128)} %bitcast.155) | data formatting | bytes 655360 | tf_op jit(solution)/shard_map/reshape | solution.py:111
  100.1 4.0 %all-to-all-start.2 = ((f32[32,4,5,128]{3,1,2,0:T(4,128)}), f32[32,4,5,128]{3,1,2,0:T(4,128)S(1)}, u32[]{:S(2)}, u32[]{:S(2)}) async-start(f32[32,4,5,128]{3,1,2,0:T(4,128)} %copy.108), calls=%async_computation.2 | async-start | bytes 655360 | tf_op jit(solution)/shard_map/all_to_all | solution.py:134
  104.7 1.3 collective-permute-start.2
  106.0 4.8 %collective-permute-start.3 = (f32[5,18,1,256]{3,2,1,0:T(1,128)S(1)}, f32[5,18,1,256]{3,2,1,0:T(1,128)S(1)}, u32[]{:S(2)}, u32[]{:S(2)}) collective-permute-start(f32[5,18,1,256]{3,2,1,0:T(1,128)S(1)} %get-tuple-element.168), channel_id=1, source_target_pairs={{0,1},{1,2},{2,3},{3,4},{4,5},{5,6},{6,7},{8,9},{9,10},{10,11},{11... | collective-permute-start | bytes 276488 | tf_op jit(solution)/shard_map/ppermute | solution.py:28
  110.8 0.7 reduce.6
  111.6 1.2 collective-permute-done.2
  112.9 1.9 %collective-permute-done.3 = f32[5,18,1,256]{3,2,1,0:T(1,128)S(1)} collective-permute-done((f32[5,18,1,256]{3,2,1,0:T(1,128)S(1)}, f32[5,18,1,256]{3,2,1,0:T(1,128)S(1)}, u32[]{:S(2)}, u32[]{:S(2)}) %collective-permute-start.3) | collective-permute-done | bytes 92192 | tf_op jit(solution)/shard_map/ppermute | solution.py:28
  114.8 3.5 %select_maximum_fusion = f32[5,18,18,258]{3,2,1,0:T(8,128)} fusion(f32[5,18,1,256]{3,2,1,0:T(1,128)S(1)} %collective-permute-done.2, f32[5,18,16,256]{3,2,1,0:T(8,128)S(1)} %constant_dynamic-update-slice_fusion, f32[5,18,1,256]{3,2,1,0:T(1,128)S(1)} %collective-permute-done.3), kind=kLoop, calls=%fused_computation.73 | loop fusion | flops 3343680 | bytes 3330720 | tf_op jit(solution)/shard_map/concatenate | solution.py:26
  118.3 0.7 copy.115
  119.1 1.0 copy.110
  120.2 9.5 %scatter_fusion = f32[512,5,128]{2,1,0:T(8,128)S(1)} fusion(f32[512,5,128]{2,1,0:T(8,128)S(1)} %broadcast_in_dim.33, s32[128]{0:T(128)S(1)} %reshape.260, f32[128,5,128]{2,1,0:T(8,128)} %copy.110), kind=kCustom, calls=%fused_computation.1 | custom fusion | flops 81920 | bytes 983552 | tf_op jit(solution)/shard_map/scatter-add | solution.py:135
  129.7 1.3 copy_multiply_fusion
  131.0 1.7 copy.112
  132.7 4.3 %div.48 = f32[4,4,32,5,4,4,8]{2,1,0,6,5,4,3:T(4,128)} reshape(f32[512,5,128]{0,2,1:T(8,128)S(1)} %copy.112) | data formatting | bytes 2621440 | tf_op jit(solution)/shard_map/div | solution.py:139
  137.0 13.0 %copy.113 = f32[5,4,4,4,4,32,8]{6,5,4,3,2,1,0:T(8,128)} copy(f32[5,4,4,4,4,32,8]{5,3,1,6,4,2,0:T(4,128)} %bitcast.144) | data formatting | bytes 2621440 | tf_op jit(solution)/shard_map/div | solution.py:139
  150.0 16.6 %div.50 = f32[5,16,16,256]{3,2,1,0:T(8,128)} reshape(f32[5,4,4,4,4,32,8]{6,5,4,3,2,1,0:T(8,128)} %copy.113) | data formatting | bytes 2621440 | tf_op jit(solution)/shard_map/div | solution.py:139
  166.6 5.0 %fusion.27 = f32[5,16,16,256]{3,2,1,0:T(8,128)} fusion(f32[5,16,16,256]{3,2,1,0:T(8,128)} %div.50, f32[5,16,16,256]{3,2,1,0:T(8,128)S(1)} %copy-done, f32[5,18,18,258]{3,2,1,0:T(8,128)} %select_maximum_fusion, f32[5,18,16,256]{3,2,1,0:T(8,128)S(1)} %copy-done.2, f32[5,18,1,256]{3,2,1,0:T(1,128)S(1)} %copy-done.7, ...), kind=kLoop, calls=%fused_computation.80 | loop fusion | flops 4587520 | bytes 8376320 | tf_op jit(solution)/shard_map/add | solution.py:139
  (108 shorter events, 4.8 us)
Async XLA Ops:
  2.0 43.4 %all-to-all-start = ((s32[32,1,4]{2,1,0:T(1,128)}), s32[32,1,4]{2,1,0:T(1,128)S(1)}, u32[]{:S(2)}, u32[]{:S(2)}) async-start(s32[32,1,4]{2,1,0:T(1,128)} %copy.93), calls=%async_computation | async-start | bytes 32768 | tf_op jit(solution)/shard_map/all_to_all | solution.py:129
  45.4 9.7 %copy-start = (f32[5,16,16,256]{3,2,1,0:T(8,128)S(1)}, f32[5,16,16,256]{3,2,1,0:T(8,128)}, u32[]{:S(2)}) copy-start(f32[5,16,16,256]{3,2,1,0:T(8,128)} %param.9) | copy-start | bytes 3932164
  45.5 14.4 %copy-start.20 = (s32[1,1,32]{2,1,0:T(1,128)S(1)}, s32[1,1,32]{2,1,0:T(1,128)}, u32[]{:S(2)}) copy-start(s32[1,1,32]{2,1,0:T(1,128)} %param.15) | copy-start | bytes 388
  47.3 13.7 %copy-start.15 = (f32[1,1,32,4,3,128]{5,3,4,2,1,0:T(4,128)S(1)}, f32[1,1,32,4,3,128]{5,3,4,2,1,0:T(4,128)}, u32[]{:S(2)}) copy-start(f32[1,1,32,4,3,128]{5,3,4,2,1,0:T(4,128)} %param.10) | copy-start | bytes 589828
  47.3 13.8 %copy-start.16 = (s32[1,1,32,4,3,128]{5,3,4,2,1,0:T(4,128)S(1)}, s32[1,1,32,4,3,128]{5,3,4,2,1,0:T(4,128)}, u32[]{:S(2)}) copy-start(s32[1,1,32,4,3,128]{5,3,4,2,1,0:T(4,128)} %param.13) | copy-start | bytes 589828
  47.3 14.6 %copy-start.17 = (f32[1,1,32,4,3,128]{5,3,4,2,1,0:T(4,128)S(1)}, f32[1,1,32,4,3,128]{5,3,4,2,1,0:T(4,128)}, u32[]{:S(2)}) copy-start(f32[1,1,32,4,3,128]{5,3,4,2,1,0:T(4,128)} %param.12) | copy-start | bytes 589828
  49.2 18.0 %all-to-all-start.1 = ((f32[32,4,5,128]{3,1,2,0:T(4,128)}), f32[32,4,5,128]{3,1,2,0:T(4,128)}, u32[]{:S(2)}, u32[]{:S(2)}) async-start(f32[32,4,5,128]{3,1,2,0:T(4,128)} %copy.100), calls=%async_computation.1 | async-start | bytes 655360 | tf_op jit(solution)/shard_map/all_to_all | solution.py:130
  55.8 6.7 %collective-permute-start.1 = (f32[5,1,16,256]{3,2,1,0:T(8,128)S(1)}, f32[5,1,16,256]{3,2,1,0:T(8,128)S(1)}, u32[]{:S(2)}, u32[]{:S(2)}) collective-permute-start(f32[5,1,16,256]{3,2,1,0:T(8,128)S(1)} %get-tuple-element.171), channel_id=1, source_target_pairs={{0,8},{8,16},{16,24},{1,9},{9,17},{17,25},{2,10},{10,18},{18,26},{... | collective-permute-start | bytes 245768 | tf_op jit(solution)/shard_map/ppermute | solution.py:28
  57.9 46.2 %collective-permute-start = (f32[5,1,16,256]{3,2,1,0:T(8,128)}, f32[5,1,16,256]{3,2,1,0:T(8,128)S(1)}, u32[]{:S(2)}, u32[]{:S(2)}) collective-permute-start(f32[5,1,16,256]{3,2,1,0:T(8,128)} %get-tuple-element.170), channel_id=1, source_target_pairs={{8,0},{16,8},{24,16},{9,1},{17,9},{25,17},{10,2},{18,10},{26,18},{... | collective-permute-start | bytes 245768 | tf_op jit(solution)/shard_map/ppermute | solution.py:30
  62.6 0.6 copy-start.8
  62.6 5.6 %copy-start.5 = (f32[1,1,32,4,128]{4,3,2,1,0:T(4,128)S(1)}, f32[1,1,32,4,128]{4,3,2,1,0:T(4,128)}, u32[]{:S(2)}) copy-start(f32[1,1,32,4,128]{4,3,2,1,0:T(4,128)} %param.11) | copy-start | bytes 196612
  71.2 4.4 %copy-start.12 = (f32[2,64,3,128]{3,2,1,0:T(4,128)S(1)}, f32[2,64,3,128]{3,2,1,0:T(4,128)}, u32[]{:S(2)}) copy-start(f32[2,64,3,128]{3,2,1,0:T(4,128)} %get-tuple-element.291) | copy-start | bytes 589828 | tf_op jit(solution)/shard_map/while
  71.2 4.5 %copy-start.18 = (f32[2,64,128]{2,1,0:T(8,128)S(1)}, f32[2,64,128]{2,1,0:T(8,128)}, u32[]{:S(2)}) copy-start(f32[2,64,128]{2,1,0:T(8,128)} %get-tuple-element.292) | copy-start | bytes 196612 | tf_op jit(solution)/shard_map/while
  71.2 4.6 %copy-start.3 = (f32[2,64,5,128]{3,2,1,0:T(8,128)S(1)}, f32[2,64,5,128]{3,2,1,0:T(8,128)}, u32[]{:S(2)}) copy-start(f32[2,64,5,128]{3,2,1,0:T(8,128)} %get-tuple-element.293) | copy-start | bytes 983044 | tf_op jit(solution)/shard_map/while
  75.7 6.8 %copy-start.13 = (f32[2,64,3,128]{3,2,1,0:T(4,128)}, f32[2,64,3,128]{3,2,1,0:T(4,128)S(1)}, u32[]{:S(2)}) copy-start(f32[2,64,3,128]{3,2,1,0:T(4,128)S(1)} %bitcast_dynamic-update-slice_fusion.2) | copy-start | bytes 589828 | tf_op jit(solution)/shard_map/while
  75.8 6.7 %copy-start.19 = (f32[2,64,128]{2,1,0:T(8,128)}, f32[2,64,128]{2,1,0:T(8,128)S(1)}, u32[]{:S(2)}) copy-start(f32[2,64,128]{2,1,0:T(8,128)S(1)} %fusion.47) | copy-start | bytes 196612 | tf_op jit(solution)/shard_map/while
  82.4 0.8 copy-start.4
  86.2 4.4 %copy-start.12 = (f32[2,64,3,128]{3,2,1,0:T(4,128)S(1)}, f32[2,64,3,128]{3,2,1,0:T(4,128)}, u32[]{:S(2)}) copy-start(f32[2,64,3,128]{3,2,1,0:T(4,128)} %get-tuple-element.291) | copy-start | bytes 589828 | tf_op jit(solution)/shard_map/while
  86.2 4.5 %copy-start.18 = (f32[2,64,128]{2,1,0:T(8,128)S(1)}, f32[2,64,128]{2,1,0:T(8,128)}, u32[]{:S(2)}) copy-start(f32[2,64,128]{2,1,0:T(8,128)} %get-tuple-element.292) | copy-start | bytes 196612 | tf_op jit(solution)/shard_map/while
  86.2 4.6 %copy-start.3 = (f32[2,64,5,128]{3,2,1,0:T(8,128)S(1)}, f32[2,64,5,128]{3,2,1,0:T(8,128)}, u32[]{:S(2)}) copy-start(f32[2,64,5,128]{3,2,1,0:T(8,128)} %get-tuple-element.293) | copy-start | bytes 983044 | tf_op jit(solution)/shard_map/while
  90.7 6.8 %copy-start.13 = (f32[2,64,3,128]{3,2,1,0:T(4,128)}, f32[2,64,3,128]{3,2,1,0:T(4,128)S(1)}, u32[]{:S(2)}) copy-start(f32[2,64,3,128]{3,2,1,0:T(4,128)S(1)} %bitcast_dynamic-update-slice_fusion.2) | copy-start | bytes 589828 | tf_op jit(solution)/shard_map/while
  90.8 6.7 %copy-start.19 = (f32[2,64,128]{2,1,0:T(8,128)}, f32[2,64,128]{2,1,0:T(8,128)S(1)}, u32[]{:S(2)}) copy-start(f32[2,64,128]{2,1,0:T(8,128)S(1)} %fusion.47) | copy-start | bytes 196612 | tf_op jit(solution)/shard_map/while
  97.4 0.8 copy-start.4
  100.1 18.9 %all-to-all-start.2 = ((f32[32,4,5,128]{3,1,2,0:T(4,128)}), f32[32,4,5,128]{3,1,2,0:T(4,128)S(1)}, u32[]{:S(2)}, u32[]{:S(2)}) async-start(f32[32,4,5,128]{3,1,2,0:T(4,128)} %copy.108), calls=%async_computation.2 | async-start | bytes 655360 | tf_op jit(solution)/shard_map/all_to_all | solution.py:134
  104.1 0.6 copy-start.10
  104.1 14.1 %copy-start.1 = (f32[5,18,16,256]{3,2,1,0:T(8,128)}, f32[5,18,16,256]{3,2,1,0:T(8,128)S(1)}, u32[]{:S(2)}) copy-start(f32[5,18,16,256]{3,2,1,0:T(8,128)S(1)} %constant_dynamic-update-slice_fusion) | copy-start | bytes 4423684
  104.7 8.1 %collective-permute-start.2 = (f32[5,18,1,256]{3,2,1,0:T(1,128)S(1)}, f32[5,18,1,256]{3,2,1,0:T(1,128)S(1)}, u32[]{:S(2)}, u32[]{:S(2)}) collective-permute-start(f32[5,18,1,256]{3,2,1,0:T(1,128)S(1)} %get-tuple-element.169), channel_id=1, source_target_pairs={{1,0},{2,1},{3,2},{4,3},{5,4},{6,5},{7,6},{9,8},{10,9},{11,10},{12... | collective-permute-start | bytes 276488 | tf_op jit(solution)/shard_map/ppermute | solution.py:30
  106.0 8.8 %collective-permute-start.3 = (f32[5,18,1,256]{3,2,1,0:T(1,128)S(1)}, f32[5,18,1,256]{3,2,1,0:T(1,128)S(1)}, u32[]{:S(2)}, u32[]{:S(2)}) collective-permute-start(f32[5,18,1,256]{3,2,1,0:T(1,128)S(1)} %get-tuple-element.168), channel_id=1, source_target_pairs={{0,1},{1,2},{2,3},{3,4},{4,5},{5,6},{6,7},{8,9},{9,10},{10,11},{11... | collective-permute-start | bytes 276488 | tf_op jit(solution)/shard_map/ppermute | solution.py:28
  111.6 6.7 %copy-start.14 = (f32[2,64,3,128]{3,2,1,0:T(4,128)S(1)}, f32[2,64,3,128]{3,2,1,0:T(4,128)}, u32[]{:S(2)}) copy-start(f32[2,64,3,128]{3,2,1,0:T(4,128)} %get-tuple-element.58) | copy-start | bytes 589828
  114.8 3.5 %copy-start.6 = (f32[5,18,1,256]{3,2,1,0:T(1,128)}, f32[5,18,1,256]{3,2,1,0:T(1,128)S(1)}, u32[]{:S(2)}) copy-start(f32[5,18,1,256]{3,2,1,0:T(1,128)S(1)} %collective-permute-done.3) | copy-start | bytes 276484
  150.0 16.6 %copy-start.2 = (f32[5,18,16,256]{3,2,1,0:T(8,128)S(1)}, f32[5,18,16,256]{3,2,1,0:T(8,128)}, u32[]{:S(2)}) copy-start(f32[5,18,16,256]{3,2,1,0:T(8,128)} %copy-done.1) | copy-start | bytes 4423684
  150.0 16.6 %copy-start.7 = (f32[5,18,1,256]{3,2,1,0:T(1,128)S(1)}, f32[5,18,1,256]{3,2,1,0:T(1,128)}, u32[]{:S(2)}) copy-start(f32[5,18,1,256]{3,2,1,0:T(1,128)} %copy-done.6) | copy-start | bytes 276484
  150.0 16.6 %copy-start.9 = (f32[5,1,16,256]{3,2,1,0:T(8,128)S(1)}, f32[5,1,16,256]{3,2,1,0:T(8,128)}, u32[]{:S(2)}) copy-start(f32[5,1,16,256]{3,2,1,0:T(8,128)} %copy-done.8) | copy-start | bytes 245764
  150.0 16.6 %copy-start.11 = (f32[5,1,16,256]{3,2,1,0:T(8,128)S(1)}, f32[5,1,16,256]{3,2,1,0:T(8,128)}, u32[]{:S(2)}) copy-start(f32[5,1,16,256]{3,2,1,0:T(8,128)} %copy-done.10) | copy-start | bytes 245764
where the time goes:
time: 174 us; the launch traced here: 172 us
  local copies, waits for them, and re-layouts  91.4 us (53%)
  starting transfers between devices  26.8 us (15%)
  other arithmetic  24.3 us (14%)
  matrix products  20.6 us (12%)
  waiting for transfers between devices  7.17 us (4%)
    div x4, local copies, waits for them, and re-layouts, shards(): gas_next = gas_state + DIFFUSION * diffused + source_field / CELL_MASS  35.6 us
    reshape x1, local copies, waits for them, and re-layouts, split_tiles(): block.reshape(fields, extent_x // TILE_X, TILE_X, extent_y // TILE_Y, TIL...  14.5 us
    transpose x1, local copies, waits for them, and re-layouts, split_tiles(): grid = grid.transpose(1, 3, 5, 0, 2, 4, 6)  14.1 us
    dot_general x2, matrix products, parcel_update(): jnp.einsum('scp,spq->scq', source, stencil, precision=lax.Precision.HIGHEST)  13.3 us
    scatter-add x1, other arithmetic, shards(): jax.ops.segment_sum(arrived.reshape(slot_total, fields, -1), wanted.resha...  9.47 us
    reshape x2, local copies, waits for them, and re-layouts, split_tiles(): return grid.reshape(-1, fields, TILE_X * TILE_Y * TILE_Z)  7.48 us
    dot_general x2, matrix products, parcel_update(): jnp.einsum('scq,spq->scp', tile_data, stencil, precision=lax.Precision.HI...  7.36 us
    all_to_all x1, starting transfers between devices, shards(): lax.all_to_all(tile_index, ('gx', 'yz'), split_axis=0, concat_axis=0, til...  7.33 us
  transfers between devices with their start and end apart: 7, of which 3 were waited for; matrix products, arithmetic and copies ran while one was open for 44% of the time, Pallas kernels for 0%

commit v1 on v0

v1 whole, which is shorter than its diff:
```python
import functools

import jax
import jax.numpy as jnp
from jax import lax
from jax.experimental import pallas as pl
from jax.experimental.pallas import tpu as pltpu
from jax.sharding import PartitionSpec as P

TILE_X = 4
TILE_Y = 4
TILE_Z = 8
DIFFUSION = 0.1
CELL_MASS = 4.0
DRAG_RATE = 0.5
EVAPORATION = 0.3
LATENT_HEAT = 2.0

LANES = 128
SUB = 8
GRANULES = LANES // TILE_Z
FLOWS = 4
BOTH = ("gx", "yz")


def roll(x, shift, axis):
    size = x.shape[axis]
    shift = shift % size
    return pltpu.roll(x, shift, axis) if shift else x


def exchange(upper, lower):
    row = lax.broadcasted_iota(jnp.int32, (SUB, LANES), 0)
    column = lax.broadcasted_iota(jnp.int32, (SUB, LANES), 1) // TILE_Z
    right = (column & 8) != 0
    half = LANES // 2
    pair = [jnp.where(right, roll(lower, half, 1), upper), jnp.where(right, lower, roll(upper, half, 1))]
    for step in (4, 2, 1):
        row_bit = (row & step) != 0
        column_bit = (column & step) != 0
        same = row_bit == column_bit
        for place in range(2):
            x = pair[place]
            from_below = roll(roll(x, -step, 0), TILE_Z * step, 1)
            from_above = roll(roll(x, step, 0), -TILE_Z * step, 1)
            pair[place] = jnp.where(same, x, jnp.where(column_bit, from_below, from_above))
    return pair


def pack_kernel(speed, mass, offsets, cells, tile_ids, counts, message, *, rows):
    devices, capacity = speed.shape[:2]
    group = SUB * rows
    lane = lax.broadcasted_iota(jnp.int32, (1, capacity), 1)

    def per_group(g, carry):
        part = message.at[pl.ds(pl.multiple_of(g * group, SUB), group)]
        for i in range(SUB):
            d = g * SUB + i
            base = i * rows
            for k in range(capacity):
                part[base + 3 * k : base + 3 * k + 3, :] = speed[d, k]
                part[base + 12 + 3 * k : base + 15 + 3 * k, :] = offsets[d, k]
                part[base + 24 + 3 * k : base + 27 + 3 * k, :] = cells[d, k].astype(jnp.float32)
            part[base + 36 : base + 40, :] = mass[d]
            ids = jnp.where(lane < counts[d], tile_ids[pl.ds(d, 1), :], -1)
            part[base + 40 : base + 41, 0:capacity] = ids.astype(jnp.float32)
        return carry

    lax.fori_loop(0, devices // SUB, per_group, 0)


def table_kernel(gas, table, face_x0, face_x1, face_y0, face_y1):
    fields, extent_x, extent_y, extent_z = gas.shape
    across_y = extent_y // TILE_Y
    across_z = extent_z // TILE_Z
    face_x0[...] = gas[:, 0]
    face_x1[...] = gas[:, extent_x - 1]
    face_y0[...] = gas[:, :, 0, :]
    face_y1[...] = gas[:, :, extent_y - 1, :]

    def per_a(a, carry):
        for f in range(FLOWS):
            for b in range(across_y):
                for h in range(extent_z // LANES):
                    lanes = slice(h * LANES, (h + 1) * LANES)
                    rows = slice(b * TILE_Y, (b + 1) * TILE_Y)
                    parts = []
                    for u in range(TILE_X):
                        piece = gas[f, a * TILE_X + u, rows, lanes]
                        if f == 3:
                            piece = piece - gas[4, a * TILE_X + u, rows, lanes]
                        parts.append(piece)
                    pair = exchange(jnp.concatenate(parts[:2], 0), jnp.concatenate(parts[2:], 0))
                    start = pl.multiple_of((a * across_y + b) * across_z + h * GRANULES, SUB)
                    table[f, pl.ds(start, SUB), :] = pair[0]
                    table[f, pl.ds(start + SUB, SUB), :] = pair[1]
        return carry

    lax.fori_loop(0, extent_x // TILE_X, per_a, 0)


def update_kernel(message, table, result, source, ids_out, ids_vmem, ids_smem, products, sem, *, rows, capacity):
    devices = message.shape[0] // rows
    group = SUB * rows
    for g in range(devices // SUB):
        ids_vmem[g * SUB : (g + 1) * SUB, :] = message[pl.ds(g * group + 40, SUB, stride=rows), :].astype(jnp.int32)
    ids_out[...] = ids_vmem[...]
    copy = pltpu.make_async_copy(ids_vmem, ids_smem, sem)
    copy.start()
    copy.wait()
    corner = lax.broadcasted_iota(jnp.int32, (SUB, LANES), 0)
    high = [(corner & bit) != 0 for bit in (4, 2, 1)]
    least = [jnp.where(h, 0.0, 1.0) for h in high]
    slope = [jnp.where(h, 1.0, -1.0) for h in high]
    shift = (
        jnp.where(high[0], TILE_Y * TILE_Z, 0) + jnp.where(high[1], TILE_Z, 0) + jnp.where(high[2], 1, 0)
    )
    row = corner

    def per_group(g, carry):
        part = message.at[pl.ds(pl.multiple_of(g * group, SUB), group)]
        for step in range(SUB // 2):
            alive = jnp.zeros((SUB, LANES), jnp.int32)
            for j in range(2 * capacity):
                i, k = 2 * step + j // capacity, j % capacity
                base = i * rows
                tile = ids_smem[g * SUB + i, k]
                alive = jnp.where(row == j, tile, alive)
                safe = jnp.maximum(tile, 0)
                weight = None
                for dim in range(3):
                    fraction = part[base + 12 + 3 * k + dim : base + 13 + 3 * k + dim, :]
                    along = least[dim] + slope[dim] * fraction
                    weight = along if weight is None else weight * along
                cell = part[base + 24 + 3 * k : base + 27 + 3 * k, :].astype(jnp.int32)
                first = (cell[0:1] * TILE_Y + cell[1:2]) * TILE_Z + cell[2:3]
                index = first + shift
                for f in range(FLOWS):
                    held = jnp.broadcast_to(table[f, pl.ds(safe, 1), :], (SUB, LANES))
                    found = jnp.take_along_axis(held, index, axis=1, mode="promise_in_bounds")
                    products[(f * SUB + j) * SUB : (f * SUB + j + 1) * SUB, :] = found * weight
            live = alive >= 0
            sampled = []
            for f in range(FLOWS):
                total = products[pl.ds(f * SUB * SUB, SUB, stride=SUB), :]
                for c in range(1, SUB):
                    total = total + products[pl.ds(f * SUB * SUB + c, SUB, stride=SUB), :]
                sampled.append(total)

            def both(offset, stride):
                return jnp.concatenate(
                    [
                        part[pl.ds((2 * step + n) * rows + offset, capacity, stride=stride), :]
                        for n in range(2)
                    ],
                    axis=0,
                )

            mass_old = both(36, 1)
            radius = jnp.exp(jnp.log(mass_old) * (1.0 / 3.0))
            factor = DRAG_RATE / (radius * radius)
            share = 1.0 / (1.0 + factor)
            gap = sampled[3]
            soft = jnp.maximum(gap, 0.0) + jnp.log(1.0 + jnp.exp(-jnp.abs(gap)))
            mass_new = jnp.where(live, mass_old / (1.0 + EVAPORATION * soft / radius), mass_old)
            vapour = mass_old - mass_new
            fields, sources = [], []
            for f in range(3):
                velocity = both(f, 3)
                moved = jnp.where(live, (velocity + factor * sampled[f]) * share, velocity)
                fields.append(moved)
                sources.append(mass_old * (velocity - moved) + vapour * moved)
            fields.append(mass_new)
            sources.append(vapour)
            for dim in range(3):
                sources.append(both(12 + dim, 3) + both(24 + dim, 3))
            first_block = (g * SUB + 2 * step) * capacity
            out = result.at[pl.ds(pl.multiple_of(first_block * FLOWS, SUB), SUB * FLOWS)]
            for f in range(FLOWS):
                out[pl.ds(f, SUB, stride=FLOWS), :] = fields[f]
            out = source.at[pl.ds(pl.multiple_of(first_block * SUB, SUB), SUB * SUB)]
            for f in range(7):
                out[pl.ds(f, SUB, stride=SUB), :] = sources[f]
        return carry

    lax.fori_loop(0, devices // SUB, per_group, 0)


def tent(position, cell):
    return jnp.maximum(0.0, 1.0 - jnp.abs(position - cell))


def deposit_kernel(ids, source, gas, from_x0, from_x1, from_y0, from_y1, gas_next, total, *, capacity):
    fields, extent_x, extent_y, extent_z = gas.shape
    across_y = extent_y // TILE_Y
    across_z = extent_z // TILE_Z
    blocks = source.shape[0] // SUB
    total[...] = jnp.zeros(total.shape, total.dtype)
    row = lax.broadcasted_iota(jnp.int32, (SUB, LANES), 0)
    along_z = row.astype(jnp.float32)
    along_y = (row % TILE_Y).astype(jnp.float32)
    along_x = (row // TILE_Y).astype(jnp.float32)

    def one(n):
        tile = jnp.maximum(ids[n // capacity, n % capacity], 0)
        held = source[pl.ds(pl.multiple_of(n * SUB, SUB), SUB), :]
        given = held[0:FLOWS]
        coarse = given.astype(jnp.bfloat16).astype(jnp.float32)
        left = jnp.concatenate([given, given - coarse], axis=0).astype(jnp.bfloat16)
        x, y, z = held[4:5], held[5:6], held[6:7]
        weight_z = tent(z, along_z)
        weight_y = tent(y, along_y)
        planes = []
        for part in range(2):
            weight_xy = tent(x, along_x + 2.0 * part) * weight_y
            for i in range(SUB):
                planes.append(weight_xy[i : i + 1] * weight_z)
        stencil = jnp.concatenate(planes, axis=0)
        high = stencil.astype(jnp.bfloat16)
        low = (stencil - high.astype(jnp.float32)).astype(jnp.bfloat16)
        right = jnp.concatenate([high, low], axis=0)
        sums = lax.dot_general(left, right, (((1,), (1,)), ((), ())), preferred_element_type=jnp.float32)
        return pl.multiple_of(tile * SUB, SUB), sums[:, :LANES] + sums[:, LANES:]

    unroll = 4

    def per_step(step, carry):
        made = [one(step * unroll + n) for n in range(unroll)]
        for start, sums in made:
            total[pl.ds(start, SUB), :] += sums
        return carry

    lax.fori_loop(0, blocks // unroll, per_step, 0)

    last_z = extent_z - 1
    lane = lax.broadcasted_iota(jnp.int32, (extent_y, extent_z), 1)
    line = lax.broadcasted_iota(jnp.int32, (extent_y, extent_z), 0)

    def per_field(f, carry):
        for x in range(extent_x):
            centre = gas[f, x]
            before = from_x0[f] if x == 0 else gas[f, x - 1]
            after = from_x1[f] if x == extent_x - 1 else gas[f, x + 1]
            beside = before + after
            beside += jnp.where(line == 0, from_y0[f, x : x + 1, :], roll(centre, 1, 0))
            beside += jnp.where(line == extent_y - 1, from_y1[f, x : x + 1, :], roll(centre, -1, 0))
            beside += jnp.where(lane == 0, 0.0, roll(centre, 1, 1))
            beside += jnp.where(lane == last_z, 0.0, roll(centre, -1, 1))
            gas_next[f, x] = centre + DIFFUSION * (beside - 6.0 * centre)
        return carry

    lax.fori_loop(0, fields, per_field, 0)

    def per_a(a, carry):
        for f in range(FLOWS):
            for b in range(across_y):
                for h in range(extent_z // LANES):
                    start = ((a * across_y + b) * across_z + h * GRANULES) * SUB
                    part = total.at[pl.ds(pl.multiple_of(start, SUB), GRANULES * SUB)]
                    pair = [
                        part[pl.ds(n * SUB * SUB + f, SUB, stride=SUB), :]
                        + part[pl.ds(n * SUB * SUB + f + FLOWS, SUB, stride=SUB), :]
                        for n in range(2)
                    ]
                    pair = exchange(*pair)
                    lanes = slice(h * LANES, (h + 1) * LANES)
                    lines = slice(b * TILE_Y, (b + 1) * TILE_Y)
                    for u in range(TILE_X):
                        piece = pair[u // 2][(u % 2) * TILE_Y : (u % 2 + 1) * TILE_Y]
                        piece = piece * (1.0 / CELL_MASS)
                        x = a * TILE_X + u
                        if f < 3:
                            gas_next[f, x, lines, lanes] += piece
                        else:
                            gas_next[3, x, lines, lanes] += -LATENT_HEAT * piece
                            gas_next[4, x, lines, lanes] += piece
        return carry

    lax.fori_loop(0, extent_x // TILE_X, per_a, 0)


def call(kernel, name, out_shape, in_specs=None, scratch=(), flops=0, moved=0):
    extra = {} if in_specs is None else {"in_specs": in_specs}
    return pl.pallas_call(
        kernel,
        out_shape=out_shape,
        scratch_shapes=scratch,
        name=name,
        cost_estimate=pl.CostEstimate(flops=flops, bytes_accessed=moved, transcendentals=0),
        compiler_params=pltpu.CompilerParams(vmem_limit_bytes=32 * 1024 * 1024),
        **extra,
    )


def vmem():
    return pl.BlockSpec(memory_space=pltpu.VMEM)


def smem():
    return pl.BlockSpec(memory_space=pltpu.SMEM)


def shards(gas_state, parcel_speed, parcel_mass, offsets, cell_base, block_tile, block_count):
    fields, extent_x, extent_y, extent_z = gas_state.shape
    devices, capacity = block_tile.shape[2:]
    rows = 10 * capacity + 1
    tiles = (extent_x // TILE_X) * (extent_y // TILE_Y) * (extent_z // TILE_Z)
    f32 = jnp.float32

    def shape(*dims, dtype=f32):
        return jax.ShapeDtypeStruct(dims, dtype)

    message = call(
        functools.partial(pack_kernel, rows=rows),
        "pack",
        shape(devices * rows, LANES),
        [vmem()] * 5 + [smem()],
    )(parcel_speed[0, 0], parcel_mass[0, 0], offsets[0, 0], cell_base[0, 0], block_tile[0, 0], block_count[0, 0])
    message = lax.all_to_all(message.reshape(devices, rows, 1, LANES), BOTH, split_axis=0, concat_axis=0, tiled=True)
    message = message.reshape(devices * rows, LANES)

    face = shape(fields, extent_x, extent_z)
    table, face_x0, face_x1, face_y0, face_y1 = call(
        table_kernel,
        "table",
        (shape(FLOWS, tiles, LANES), shape(fields, extent_y, extent_z), shape(fields, extent_y, extent_z), face, face),
        flops=10**7,
    )(gas_state)

    def shifted(value, axis, step):
        count = lax.axis_size(axis)
        pairs = [(i, i + step) for i in range(count) if 0 <= i + step < count]
        return lax.ppermute(value, axis, pairs)

    from_x0 = shifted(face_x1, "gx", 1)
    from_x1 = shifted(face_x0, "gx", -1)
    from_y0 = shifted(face_y1, "yz", 1)
    from_y1 = shifted(face_y0, "yz", -1)

    blocks = devices * capacity
    result, source, ids = call(
        functools.partial(update_kernel, rows=rows, capacity=capacity),
        "update",
        (shape(blocks * FLOWS, LANES), shape(blocks * SUB, LANES), shape(devices, LANES, dtype=jnp.int32)),
        scratch=[
            pltpu.VMEM((devices, LANES), jnp.int32),
            pltpu.SMEM((devices, LANES), jnp.int32),
            pltpu.VMEM((FLOWS * SUB * SUB, LANES), f32),
            pltpu.SemaphoreType.DMA(()),
        ],
        flops=10**7,
    )(message, table)
    result = lax.all_to_all(
        result.reshape(devices, capacity * FLOWS, LANES), BOTH, split_axis=0, concat_axis=0, tiled=True
    )
    gas_next = call(
        functools.partial(deposit_kernel, capacity=capacity),
        "deposit",
        shape(*gas_state.shape),
        [smem()] + [vmem()] * 6,
        scratch=[pltpu.VMEM((tiles * SUB, LANES), f32)],
        flops=3 * 10**7,
    )(ids, source, gas_state, from_x0, from_x1, from_y0, from_y1)
    result = result.reshape(devices, capacity, FLOWS, LANES)
    return gas_next, result[:, :, :3].reshape(parcel_speed.shape), result[:, :, 3].reshape(parcel_mass.shape)


def solution(mesh):
    in_specs = (
        P(None, "gx", "yz", None),
        P("gx", "yz", None, None, None, None),
        P("gx", "yz", None, None, None),
        P("gx", "yz", None, None, None, None),
        P("gx", "yz", None, None, None, None),
        P("gx", "yz", None, None),
        P("gx", "yz", None),
    )
    out_specs = (
        P(None, "gx", "yz", None),
        P("gx", "yz", None, None, None, None),
        P("gx", "yz", None, None, None),
    )
    return jax.shard_map(shards, mesh=mesh, in_specs=in_specs, out_specs=out_specs, check_vma=False)
```

time: 174 us -> 75.9 us (0.44)
  the two profiles are of different devices: /device:TPU:0 before, /device:TPU:6 now
where the time goes in v1:
time: 75.9 us; the launch traced here: 75.5 us
  Pallas kernels  34.1 us (45%)
  starting transfers between devices  21.8 us (29%)
  waiting for transfers between devices  11.5 us (15%)
  local copies, waits for them, and re-layouts  7.21 us (9%)
  between operations  0.81 us (1%)
    pallas_call x1, Pallas kernels, shards(): call(functools.partial(deposit_kernel, capacity=capacity), 'deposit', sha...  19.8 us
    ppermute x4, starting transfers between devices, shifted(): return lax.ppermute(value, axis, pairs)  11.4 us
    pallas_call x1, Pallas kernels, shards(): call(table_kernel, 'table', (shape(FLOWS, tiles, LANES), shape(fields, ex...  10.4 us
    all_to_all x1, waiting for transfers between devices, shards(): lax.all_to_all(message.reshape(devices, rows, 1, LANES), BOTH, split_axis...  6.54 us
    all_to_all x1, starting transfers between devices, shards(): lax.all_to_all(message.reshape(devices, rows, 1, LANES), BOTH, split_axis...  6.07 us
    unnamed x23, local copies, waits for them, and re-layouts  5.14 us
    ppermute x4, waiting for transfers between devices, shifted(): return lax.ppermute(value, axis, pairs)  5 us
    all_to_all x1, starting transfers between devices, shards(): lax.all_to_all(result.reshape(devices, capacity * FLOWS, LANES), BOTH, sp...  4.28 us
  transfers between devices with their start and end apart: 6, of which 3 were waited for; matrix products, arithmetic and copies ran while one was open for 0% of the time, Pallas kernels for 40%

profile of v1, /device:TPU:6, one launch (start us, length us, event | category | flops | bytes accessed | tf_op | source)
XLA Modules:
  0.0 75.5 jit_solution(14085753625803067993)
XLA Ops:
  0.6 0.0 copy-start.5
  0.6 0.0 copy-start.2
  0.7 0.8 %copy.24.tile_ids = s32[32,4]{1,0:T(8,128)S(1)} copy(s32[32,4]{0,1:T(4,128)} %bitcast.25) | data formatting | bytes 1024 | tf_op jit(solution)/shard_map/squeeze | solution.py:318
  1.4 1.0 %copy.32 = s32[1,1,32,4,3,128]{5,4,3,2,1,0:T(4,128)S(1)} copy(s32[1,1,32,4,3,128]{5,3,4,2,1,0:T(4,128)} %param.11) | data formatting | bytes 393216 | tf_op args[4]
  2.4 1.2 %copy_bitcast_fusion.1 = (f32[32,4,3,128]{3,2,1,0:T(4,128)S(1)}, f32[32,4,3,128]{3,2,1,0:T(4,128)S(1)}) fusion(f32[1,1,32,4,3,128]{5,3,4,2,1,0:T(4,128)} %param.10, f32[1,1,32,4,3,128]{5,3,4,2,1,0:T(4,128)} %param.8), kind=kLoop, calls=%fused_computation.1 | loop fusion | bytes 786432 | tf_op jit(solution)/shard_map/squeeze | solution.py:318
  3.6 0.0 copy-done.5
  3.6 0.0 copy-done.2
  3.6 0.0 copy-start
  3.6 1.6 %pack.1 = f32[1312,128]{1,0:T(8,128)} custom-call(f32[32,4,3,128]{3,2,1,0:T(4,128)S(1)} %get-tuple-element.26.speed, f32[32,4,128]{2,1,0:T(4,128)S(1)} %bitcast.21, f32[32,4,3,128]{3,2,1,0:T(4,128)S(1)} %get-tuple-element.25.offsets, s32[32,4,3,128]{3,2,1,0:T(4,128)S(1)} %bitcast.19, s32[32,4]{1,0:T(8,128)S(1)} %copy.24.tile_ids, s32[32]{0:T(128)S(1)} %bitcast.22), custom_call_target="tpu_custom_call" | custom-call | tf_op jit(solution)/shard_map/pack/pallas_call | solution.py:313
  5.2 6.1 %all-to-all-start = ((f32[32,41,1,128]{3,2,1,0:T(1,128)}), f32[32,41,1,128]{3,2,1,0:T(1,128)S(1)}, u32[]{:S(2)}, u32[]{:S(2)}) async-start(f32[32,41,1,128]{3,2,1,0:T(1,128)} %bitcast.6), calls=%async_computation | async-start | bytes 1343488 | tf_op jit(solution)/shard_map/all_to_all | solution.py:319
  11.3 0.0 copy-done
  11.3 10.4 %table.1 = (f32[4,512,128]{2,1,0:T(8,128)S(1)}, f32[5,16,256]{2,1,0:T(8,128)S(1)}, f32[5,16,256]{2,1,0:T(8,128)S(1)}, f32[5,16,256]{2,1,0:T(8,128)S(1)}, f32[5,16,256]{2,1,0:T(8,128)S(1)}) custom-call(f32[5,16,16,256]{3,2,1,0:T(8,128)S(1)} %copy-done), custom_call_target="tpu_custom_call" | custom-call | flops 10000000 | tf_op jit(solution)/shard_map/table/pallas_call | solution.py:323
  21.7 0.0 copy-start.9
  21.7 0.6 copy-done.9
  22.3 0.0 copy-start.6
  22.3 0.0 copy-start.7
  22.3 0.0 copy-start.8
  22.3 6.5 %all-to-all-done = f32[32,41,1,128]{3,2,1,0:T(1,128)S(1)} async-done(((f32[32,41,1,128]{3,2,1,0:T(1,128)}), f32[32,41,1,128]{3,2,1,0:T(1,128)S(1)}, u32[]{:S(2)}, u32[]{:S(2)}) %all-to-all-start) | async-done | bytes 671776 | tf_op jit(solution)/shard_map/all_to_all | solution.py:319
  28.9 0.0 copy-done.6
  28.9 0.0 copy-done.7
  28.9 0.0 copy-done.8
  28.9 2.3 %update.1 = (f32[512,128]{1,0:T(8,128)S(1)}, f32[1024,128]{1,0:T(8,128)S(1)}, s32[32,128]{1,0:T(8,128)S(1)}) custom-call(f32[1312,128]{1,0:T(8,128)S(1)} %bitcast.18, f32[4,512,128]{2,1,0:T(8,128)S(1)} %get-tuple-element.11.table), custom_call_target="tpu_custom_call" | custom-call | flops 10000000 | tf_op jit(solution)/shard_map/update/pallas_call | solution.py:341
  31.2 0.0 copy-start.1
  31.3 0.7 copy-done.1
  31.9 0.0 copy-start.3
  31.9 0.6 copy-done.3
  32.6 4.3 %all-to-all-start.1 = ((f32[32,16,128]{2,1,0:T(8,128)}), f32[32,16,128]{2,1,0:T(8,128)S(1)}, u32[]{:S(2)}, u32[]{:S(2)}) async-start(f32[32,16,128]{2,1,0:T(8,128)} %bitcast.20), calls=%async_computation.1 | async-start | bytes 524288 | tf_op jit(solution)/shard_map/all_to_all | solution.py:353
  36.8 2.0 %collective-permute-start = (f32[5,16,256]{2,1,0:T(8,128)}, f32[5,16,256]{2,1,0:T(8,128)S(1)}, u32[]{:S(2)}, u32[]{:S(2)}) collective-permute-start(f32[5,16,256]{2,1,0:T(8,128)} %copy-done.9), channel_id=1, source_target_pairs={{0,8},{8,16},{16,24},{1,9},{9,17},{17,25},{2,10},{10,18},{18,26},{... | collective-permute-start | bytes 245768 | tf_op jit(solution)/shard_map/ppermute | solution.py:333
  38.9 3.5 %collective-permute-start.1 = (f32[5,16,256]{2,1,0:T(8,128)}, f32[5,16,256]{2,1,0:T(8,128)S(1)}, u32[]{:S(2)}, u32[]{:S(2)}) collective-permute-start(f32[5,16,256]{2,1,0:T(8,128)} %copy-done.8), channel_id=1, source_target_pairs={{8,0},{16,8},{24,16},{9,1},{17,9},{25,17},{10,2},{18,10},{26,18},{... | collective-permute-start | bytes 245768 | tf_op jit(solution)/shard_map/ppermute | solution.py:333
  42.4 3.4 %collective-permute-start.2 = (f32[5,16,256]{2,1,0:T(8,128)}, f32[5,16,256]{2,1,0:T(8,128)S(1)}, u32[]{:S(2)}, u32[]{:S(2)}) collective-permute-start(f32[5,16,256]{2,1,0:T(8,128)} %copy-done.7), channel_id=1, source_target_pairs={{0,1},{1,2},{2,3},{3,4},{4,5},{5,6},{6,7},{8,9},{9,10},{10,11},{11... | collective-permute-start | bytes 245768 | tf_op jit(solution)/shard_map/ppermute | solution.py:333
  45.8 2.4 %collective-permute-start.3 = (f32[5,16,256]{2,1,0:T(8,128)}, f32[5,16,256]{2,1,0:T(8,128)S(1)}, u32[]{:S(2)}, u32[]{:S(2)}) collective-permute-start(f32[5,16,256]{2,1,0:T(8,128)} %copy-done.6), channel_id=1, source_target_pairs={{1,0},{2,1},{3,2},{4,3},{5,4},{6,5},{7,6},{9,8},{10,9},{11,10},{12... | collective-permute-start | bytes 245768 | tf_op jit(solution)/shard_map/ppermute | solution.py:333
  48.3 0.0 collective-permute-done.from_x0
  48.3 0.0 collective-permute-done.1.from_x1
  48.3 0.7 collective-permute-done.2.from_y0
  49.0 4.3 %collective-permute-done.3.from_y1 = f32[5,16,256]{2,1,0:T(8,128)S(1)} collective-permute-done((f32[5,16,256]{2,1,0:T(8,128)}, f32[5,16,256]{2,1,0:T(8,128)S(1)}, u32[]{:S(2)}, u32[]{:S(2)}) %collective-permute-start.3) | collective-permute-done | bytes 81952 | tf_op jit(solution)/shard_map/ppermute | solution.py:333
  53.3 0.0 copy-start.4
  53.3 0.7 copy-done.4
  54.0 19.8 %deposit.1 = f32[5,16,16,256]{3,2,1,0:T(8,128)} custom-call(s32[32,128]{1,0:T(8,128)S(1)} %copy-done.4, f32[1024,128]{1,0:T(8,128)S(1)} %get-tuple-element.13.source, f32[5,16,16,256]{3,2,1,0:T(8,128)S(1)} %copy-done, f32[5,16,256]{2,1,0:T(8,128)S(1)} %collective-permute-done.from_x0, f32[5,16,256]{2,1,0:T(8,128)S(1)} %collective-permute-done.1.from_x1, ...), custom_call_target="tpu_custom_call" | custom-call | flops 30000000 | tf_op jit(solution)/shard_map/deposit/pallas_call | solution.py:356
  73.8 0.0 all-to-all-done.1
  73.8 0.1 copy.26
  74.0 0.8 %copy.27 = f32[1,1,32,4,3,128]{5,3,4,2,1,0:T(4,128)} copy(f32[1,1,32,4,3,128]{5,2,4,3,1,0:T(8,128)S(1)} %slice_bitcast_fusion) | data formatting | bytes 393216
  74.8 0.7 copy.28
  (2 shorter events, 0.0 us)
Async XLA Ops:
  0.6 3.0 %copy-start.5 = (s32[1,1,32]{2,1,0:T(1,128)S(1)}, s32[1,1,32]{2,1,0:T(1,128)}, u32[]{:S(2)}) copy-start(s32[1,1,32]{2,1,0:T(1,128)} %param.13) | copy-start | bytes 388
  0.6 3.0 %copy-start.2 = (f32[1,1,32,4,128]{4,3,2,1,0:T(4,128)S(1)}, f32[1,1,32,4,128]{4,3,2,1,0:T(4,128)}, u32[]{:S(2)}) copy-start(f32[1,1,32,4,128]{4,3,2,1,0:T(4,128)} %param.9) | copy-start | bytes 196612
  3.6 7.7 %copy-start = (f32[5,16,16,256]{3,2,1,0:T(8,128)S(1)}, f32[5,16,16,256]{3,2,1,0:T(8,128)}, u32[]{:S(2)}) copy-start(f32[5,16,16,256]{3,2,1,0:T(8,128)} %gas.3) | copy-start | bytes 3932164
  5.2 23.7 %all-to-all-start = ((f32[32,41,1,128]{3,2,1,0:T(1,128)}), f32[32,41,1,128]{3,2,1,0:T(1,128)S(1)}, u32[]{:S(2)}, u32[]{:S(2)}) async-start(f32[32,41,1,128]{3,2,1,0:T(1,128)} %bitcast.6), calls=%async_computation | async-start | bytes 1343488 | tf_op jit(solution)/shard_map/all_to_all | solution.py:319
  21.7 0.6 copy-start.9
  22.3 6.5 %copy-start.6 = (f32[5,16,256]{2,1,0:T(8,128)}, f32[5,16,256]{2,1,0:T(8,128)S(1)}, u32[]{:S(2)}) copy-start(f32[5,16,256]{2,1,0:T(8,128)S(1)} %get-tuple-element.17) | copy-start | bytes 245764
  22.3 6.5 %copy-start.7 = (f32[5,16,256]{2,1,0:T(8,128)}, f32[5,16,256]{2,1,0:T(8,128)S(1)}, u32[]{:S(2)}) copy-start(f32[5,16,256]{2,1,0:T(8,128)S(1)} %get-tuple-element.16) | copy-start | bytes 245764
  22.3 6.5 %copy-start.8 = (f32[5,16,256]{2,1,0:T(8,128)}, f32[5,16,256]{2,1,0:T(8,128)S(1)}, u32[]{:S(2)}) copy-start(f32[5,16,256]{2,1,0:T(8,128)S(1)} %get-tuple-element.15) | copy-start | bytes 245764
  31.2 0.7 copy-start.1
  31.9 0.6 copy-start.3
  32.6 41.3 %all-to-all-start.1 = ((f32[32,16,128]{2,1,0:T(8,128)}), f32[32,16,128]{2,1,0:T(8,128)S(1)}, u32[]{:S(2)}, u32[]{:S(2)}) async-start(f32[32,16,128]{2,1,0:T(8,128)} %bitcast.20), calls=%async_computation.1 | async-start | bytes 524288 | tf_op jit(solution)/shard_map/all_to_all | solution.py:353
  36.8 11.4 %collective-permute-start = (f32[5,16,256]{2,1,0:T(8,128)}, f32[5,16,256]{2,1,0:T(8,128)S(1)}, u32[]{:S(2)}, u32[]{:S(2)}) collective-permute-start(f32[5,16,256]{2,1,0:T(8,128)} %copy-done.9), channel_id=1, source_target_pairs={{0,8},{8,16},{16,24},{1,9},{9,17},{17,25},{2,10},{10,18},{18,26},{... | collective-permute-start | bytes 245768 | tf_op jit(solution)/shard_map/ppermute | solution.py:333
  38.9 9.4 %collective-permute-start.1 = (f32[5,16,256]{2,1,0:T(8,128)}, f32[5,16,256]{2,1,0:T(8,128)S(1)}, u32[]{:S(2)}, u32[]{:S(2)}) collective-permute-start(f32[5,16,256]{2,1,0:T(8,128)} %copy-done.8), channel_id=1, source_target_pairs={{8,0},{16,8},{24,16},{9,1},{17,9},{25,17},{10,2},{18,10},{26,18},{... | collective-permute-start | bytes 245768 | tf_op jit(solution)/shard_map/ppermute | solution.py:333
  42.4 6.5 %collective-permute-start.2 = (f32[5,16,256]{2,1,0:T(8,128)}, f32[5,16,256]{2,1,0:T(8,128)S(1)}, u32[]{:S(2)}, u32[]{:S(2)}) collective-permute-start(f32[5,16,256]{2,1,0:T(8,128)} %copy-done.7), channel_id=1, source_target_pairs={{0,1},{1,2},{2,3},{3,4},{4,5},{5,6},{6,7},{8,9},{9,10},{10,11},{11... | collective-permute-start | bytes 245768 | tf_op jit(solution)/shard_map/ppermute | solution.py:333
  45.8 7.4 %collective-permute-start.3 = (f32[5,16,256]{2,1,0:T(8,128)}, f32[5,16,256]{2,1,0:T(8,128)S(1)}, u32[]{:S(2)}, u32[]{:S(2)}) collective-permute-start(f32[5,16,256]{2,1,0:T(8,128)} %copy-done.6), channel_id=1, source_target_pairs={{1,0},{2,1},{3,2},{4,3},{5,4},{6,5},{7,6},{9,8},{10,9},{11,10},{12... | collective-permute-start | bytes 245768 | tf_op jit(solution)/shard_map/ppermute | solution.py:333
  53.3 0.7 copy-start.4

commit v2 on v1

--- a/solution.py
+++ b/solution.py
@@ -24,49 +24,48 @@
 
 
 def roll(x, shift, axis):
-    size = x.shape[axis]
-    shift = shift % size
+    shift = shift % x.shape[axis]
     return pltpu.roll(x, shift, axis) if shift else x
+
+
+def pick(x, rows):
+    return jnp.take_along_axis(x, rows, axis=0, mode="promise_in_bounds")
 
 
 def exchange(upper, lower):
     row = lax.broadcasted_iota(jnp.int32, (SUB, LANES), 0)
-    column = lax.broadcasted_iota(jnp.int32, (SUB, LANES), 1) // TILE_Z
-    right = (column & 8) != 0
+    granule = lax.broadcasted_iota(jnp.int32, (SUB, LANES), 1) // TILE_Z
     half = LANES // 2
-    pair = [jnp.where(right, roll(lower, half, 1), upper), jnp.where(right, lower, roll(upper, half, 1))]
-    for step in (4, 2, 1):
-        row_bit = (row & step) != 0
-        column_bit = (column & step) != 0
-        same = row_bit == column_bit
-        for place in range(2):
-            x = pair[place]
-            from_below = roll(roll(x, -step, 0), TILE_Z * step, 1)
-            from_above = roll(roll(x, step, 0), -TILE_Z * step, 1)
-            pair[place] = jnp.where(same, x, jnp.where(column_bit, from_below, from_above))
+    turned = [
+        pltpu.roll(x, shift, 1, stride=TILE_Z, stride_axis=0) for x, shift in ((upper, 0), (lower, half))
+    ]
+    back = SUB - 1 - row
+    pair = []
+    for part in range(2):
+        wanted = (granule - back - SUB * part) % GRANULES
+        mixed = jnp.where(wanted < SUB, pick(turned[0], wanted % SUB), pick(turned[1], wanted % SUB))
+        shift = (-TILE_Z * (SUB - 1) - half * part) % LANES
+        pair.append(pick(pltpu.roll(mixed, shift, 1, stride=TILE_Z, stride_axis=0), back))
     return pair
 
 
-def pack_kernel(speed, mass, offsets, cells, tile_ids, counts, message, *, rows):
-    devices, capacity = speed.shape[:2]
+def pack_kernel(speed, mass, offsets, cells, tile_ids, counts, message, *, rows, capacity):
     group = SUB * rows
-    lane = lax.broadcasted_iota(jnp.int32, (1, capacity), 1)
-
-    def per_group(g, carry):
-        part = message.at[pl.ds(pl.multiple_of(g * group, SUB), group)]
+    vector = 3 * capacity
+    owners = tile_ids.shape[1]
+    slot = lax.broadcasted_iota(jnp.int32, tile_ids.shape, 0)
+    ids = jnp.where(slot < counts[...], tile_ids[...], -1).astype(jnp.float32)
+    ids = jnp.concatenate([ids, jnp.zeros((LANES - capacity, owners), jnp.float32)], axis=0).T
+
+    for g in range(owners // SUB):
         for i in range(SUB):
             d = g * SUB + i
-            base = i * rows
-            for k in range(capacity):
-                part[base + 3 * k : base + 3 * k + 3, :] = speed[d, k]
-                part[base + 12 + 3 * k : base + 15 + 3 * k, :] = offsets[d, k]
-                part[base + 24 + 3 * k : base + 27 + 3 * k, :] = cells[d, k].astype(jnp.float32)
-            part[base + 36 : base + 40, :] = mass[d]
-            ids = jnp.where(lane < counts[d], tile_ids[pl.ds(d, 1), :], -1)
-            part[base + 40 : base + 41, 0:capacity] = ids.astype(jnp.float32)
-        return carry
-
-    lax.fori_loop(0, devices // SUB, per_group, 0)
+            base = d * rows
+            message[base : base + vector, :] = speed[d * vector : (d + 1) * vector, :]
+            message[base + vector : base + 2 * vector, :] = offsets[d * vector : (d + 1) * vector, :]
+            message[base + 2 * vector : base + 3 * vector, :] = cells[d * vector : (d + 1) * vector, :].astype(jnp.float32)
+            message[base + 3 * vector : base + 3 * vector + capacity, :] = mass[d * capacity : (d + 1) * capacity, :]
+            message[base + rows - 1 : base + rows, :] = ids[d : d + 1, :]
 
 
 def table_kernel(gas, table, face_x0, face_x1, face_y0, face_y1):
@@ -103,7 +102,7 @@
     devices = message.shape[0] // rows
     group = SUB * rows
     for g in range(devices // SUB):
-        ids_vmem[g * SUB : (g + 1) * SUB, :] = message[pl.ds(g * group + 40, SUB, stride=rows), :].astype(jnp.int32)
+        ids_vmem[g * SUB : (g + 1) * SUB, :] = message[pl.ds(g * group + rows - 1, SUB, stride=rows), :].astype(jnp.int32)
     ids_out[...] = ids_vmem[...]
     copy = pltpu.make_async_copy(ids_vmem, ids_smem, sem)
     copy.start()
@@ -129,12 +128,13 @@
                 safe = jnp.maximum(tile, 0)
                 weight = None
                 for dim in range(3):
-                    fraction = part[base + 12 + 3 * k + dim : base + 13 + 3 * k + dim, :]
+                    start = base + (3 + dim) * capacity + k
+                    fraction = part[start : start + 1, :]
                     along = least[dim] + slope[dim] * fraction
                     weight = along if weight is None else weight * along
-                cell = part[base + 24 + 3 * k : base + 27 + 3 * k, :].astype(jnp.int32)
-                first = (cell[0:1] * TILE_Y + cell[1:2]) * TILE_Z + cell[2:3]
-                index = first + shift
+                cell = [part[base + (6 + dim) * capacity + k, :][None] for dim in range(3)]
+                first = (cell[0] * TILE_Y + cell[1]) * TILE_Z + cell[2]
+                index = first.astype(jnp.int32) + shift
                 for f in range(FLOWS):
                     held = jnp.broadcast_to(table[f, pl.ds(safe, 1), :], (SUB, LANES))
                     found = jnp.take_along_axis(held, index, axis=1, mode="promise_in_bounds")
@@ -147,16 +147,11 @@
                     total = total + products[pl.ds(f * SUB * SUB + c, SUB, stride=SUB), :]
                 sampled.append(total)
 
-            def both(offset, stride):
-                return jnp.concatenate(
-                    [
-                        part[pl.ds((2 * step + n) * rows + offset, capacity, stride=stride), :]
-                        for n in range(2)
-                    ],
-                    axis=0,
-                )
-
-            mass_old = both(36, 1)
+            def both(field):
+                starts = [(2 * step + n) * rows + field * capacity for n in range(2)]
+                return jnp.concatenate([part[start : start + capacity, :] for start in starts], axis=0)
+
+            mass_old = both(9)
             radius = jnp.exp(jnp.log(mass_old) * (1.0 / 3.0))
             factor = DRAG_RATE / (radius * radius)
             share = 1.0 / (1.0 + factor)
@@ -166,18 +161,20 @@
             vapour = mass_old - mass_new
             fields, sources = [], []
             for f in range(3):
-                velocity = both(f, 3)
+                velocity = both(f)
                 moved = jnp.where(live, (velocity + factor * sampled[f]) * share, velocity)
                 fields.append(moved)
                 sources.append(mass_old * (velocity - moved) + vapour * moved)
             fields.append(mass_new)
             sources.append(vapour)
             for dim in range(3):
-                sources.append(both(12 + dim, 3) + both(24 + dim, 3))
+                sources.append(both(3 + dim) + both(6 + dim))
             first_block = (g * SUB + 2 * step) * capacity
             out = result.at[pl.ds(pl.multiple_of(first_block * FLOWS, SUB), SUB * FLOWS)]
-            for f in range(FLOWS):
-                out[pl.ds(f, SUB, stride=FLOWS), :] = fields[f]
+            for n in range(2):
+                for f in range(FLOWS):
+                    start = (n * FLOWS + f) * capacity
+                    out[start : start + capacity, :] = fields[f][n * capacity : (n + 1) * capacity]
             out = source.at[pl.ds(pl.multiple_of(first_block * SUB, SUB), SUB * SUB)]
             for f in range(7):
                 out[pl.ds(f, SUB, stride=SUB), :] = sources[f]
@@ -190,16 +187,40 @@
     return jnp.maximum(0.0, 1.0 - jnp.abs(position - cell))
 
 
-def deposit_kernel(ids, source, gas, from_x0, from_x1, from_y0, from_y1, gas_next, total, *, capacity):
+def diffuse_kernel(gas, from_x0, from_x1, from_y0, from_y1, diffused):
     fields, extent_x, extent_y, extent_z = gas.shape
+    lane = lax.broadcasted_iota(jnp.int32, (extent_y, extent_z), 1)
+    line = lax.broadcasted_iota(jnp.int32, (extent_y, extent_z), 0)
+
+    def per_field(f, carry):
+        for x in range(extent_x):
+            centre = gas[f, x]
+            before = from_x0[f] if x == 0 else gas[f, x - 1]
+            after = from_x1[f] if x == extent_x - 1 else gas[f, x + 1]
+            beside = before + after
+            beside += jnp.where(line == 0, from_y0[f, x : x + 1, :], roll(centre, 1, 0))
+            beside += jnp.where(line == extent_y - 1, from_y1[f, x : x + 1, :], roll(centre, -1, 0))
+            beside += jnp.where(lane == 0, 0.0, roll(centre, 1, 1))
+            beside += jnp.where(lane == extent_z - 1, 0.0, roll(centre, -1, 1))
+            diffused[f, x] = centre + DIFFUSION * (beside - 6.0 * centre)
+        return carry
+
+    lax.fori_loop(0, fields, per_field, 0)
+
+
+def deposit_kernel(ids_vmem, source, diffused, gas_next, total, ids, sem, *, capacity):
+    fields, extent_x, extent_y, extent_z = diffused.shape
     across_y = extent_y // TILE_Y
     across_z = extent_z // TILE_Z
     blocks = source.shape[0] // SUB
+    copy = pltpu.make_async_copy(ids_vmem, ids, sem)
+    copy.start()
     total[...] = jnp.zeros(total.shape, total.dtype)
     row = lax.broadcasted_iota(jnp.int32, (SUB, LANES), 0)
     along_z = row.astype(jnp.float32)
     along_y = (row % TILE_Y).astype(jnp.float32)
     along_x = (row // TILE_Y).astype(jnp.float32)
+    copy.wait()
 
     def one(n):
         tile = jnp.maximum(ids[n // capacity, n % capacity], 0)
@@ -232,55 +253,34 @@
 
     lax.fori_loop(0, blocks // unroll, per_step, 0)
 
-    last_z = extent_z - 1
-    lane = lax.broadcasted_iota(jnp.int32, (extent_y, extent_z), 1)
-    line = lax.broadcasted_iota(jnp.int32, (extent_y, extent_z), 0)
-
-    def per_field(f, carry):
-        for x in range(extent_x):
-            centre = gas[f, x]
-            before = from_x0[f] if x == 0 else gas[f, x - 1]
-            after = from_x1[f] if x == extent_x - 1 else gas[f, x + 1]
-            beside = before + after
-            beside += jnp.where(line == 0, from_y0[f, x : x + 1, :], roll(centre, 1, 0))
-            beside += jnp.where(line == extent_y - 1, from_y1[f, x : x + 1, :], roll(centre, -1, 0))
-            beside += jnp.where(lane == 0, 0.0, roll(centre, 1, 1))
-            beside += jnp.where(lane == last_z, 0.0, roll(centre, -1, 1))
-            gas_next[f, x] = centre + DIFFUSION * (beside - 6.0 * centre)
-        return carry
-
-    lax.fori_loop(0, fields, per_field, 0)
-
     def per_a(a, carry):
-        for f in range(FLOWS):
-            for b in range(across_y):
-                for h in range(extent_z // LANES):
-                    start = ((a * across_y + b) * across_z + h * GRANULES) * SUB
-                    part = total.at[pl.ds(pl.multiple_of(start, SUB), GRANULES * SUB)]
+        for b in range(across_y):
+            for h in range(extent_z // LANES):
+                start = ((a * across_y + b) * across_z + h * GRANULES) * SUB
+                part = total.at[pl.ds(pl.multiple_of(start, SUB), GRANULES * SUB)]
+                lanes = slice(h * LANES, (h + 1) * LANES)
+                lines = slice(b * TILE_Y, (b + 1) * TILE_Y)
+                for f in range(FLOWS):
                     pair = [
                         part[pl.ds(n * SUB * SUB + f, SUB, stride=SUB), :]
                         + part[pl.ds(n * SUB * SUB + f + FLOWS, SUB, stride=SUB), :]
                         for n in range(2)
                     ]
-                    pair = exchange(*pair)
-                    lanes = slice(h * LANES, (h + 1) * LANES)
-                    lines = slice(b * TILE_Y, (b + 1) * TILE_Y)
+                    pair = [x * (1.0 / CELL_MASS) for x in exchange(*pair)]
                     for u in range(TILE_X):
                         piece = pair[u // 2][(u % 2) * TILE_Y : (u % 2 + 1) * TILE_Y]
-                        piece = piece * (1.0 / CELL_MASS)
                         x = a * TILE_X + u
                         if f < 3:
-                            gas_next[f, x, lines, lanes] += piece
+                            gas_next[f, x, lines, lanes] = diffused[f, x, lines, lanes] + piece
                         else:
-                            gas_next[3, x, lines, lanes] += -LATENT_HEAT * piece
-                            gas_next[4, x, lines, lanes] += piece
+                            gas_next[3, x, lines, lanes] = diffused[3, x, lines, lanes] - LATENT_HEAT * piece
+                            gas_next[4, x, lines, lanes] = diffused[4, x, lines, lanes] + piece
         return carry
 
     lax.fori_loop(0, extent_x // TILE_X, per_a, 0)
 
 
-def call(kernel, name, out_shape, in_specs=None, scratch=(), flops=0, moved=0):
-    extra = {} if in_specs is None else {"in_specs": in_specs}
+def call(kernel, name, out_shape, scratch=(), flops=0, moved=0):
     return pl.pallas_call(
         kernel,
         out_shape=out_shape,
@@ -288,16 +288,7 @@
         name=name,
         cost_estimate=pl.CostEstimate(flops=flops, bytes_accessed=moved, transcendentals=0),
         compiler_params=pltpu.CompilerParams(vmem_limit_bytes=32 * 1024 * 1024),
-        **extra,
-    )
-
-
-def vmem():
-    return pl.BlockSpec(memory_space=pltpu.VMEM)
-
-
-def smem():
-    return pl.BlockSpec(memory_space=pltpu.SMEM)
+    )
 
 
 def shards(gas_state, parcel_speed, parcel_mass, offsets, cell_base, block_tile, block_count):
@@ -310,12 +301,21 @@
     def shape(*dims, dtype=f32):
         return jax.ShapeDtypeStruct(dims, dtype)
 
+    def by_component(value):
+        return value[0, 0].transpose(0, 2, 1, 3).reshape(devices * 3 * capacity, LANES)
+
     message = call(
-        functools.partial(pack_kernel, rows=rows),
+        functools.partial(pack_kernel, rows=rows, capacity=capacity),
         "pack",
         shape(devices * rows, LANES),
-        [vmem()] * 5 + [smem()],
-    )(parcel_speed[0, 0], parcel_mass[0, 0], offsets[0, 0], cell_base[0, 0], block_tile[0, 0], block_count[0, 0])
+    )(
+        by_component(parcel_speed),
+        parcel_mass.reshape(devices * capacity, LANES),
+        by_component(offsets),
+        by_component(cell_base),
+        block_tile[0, 0].T,
+        block_count[0],
+    )
     message = lax.all_to_all(message.reshape(devices, rows, 1, LANES), BOTH, split_axis=0, concat_axis=0, tiled=True)
     message = message.reshape(devices * rows, LANES)
 
@@ -332,10 +332,14 @@
         pairs = [(i, i + step) for i in range(count) if 0 <= i + step < count]
         return lax.ppermute(value, axis, pairs)
 
-    from_x0 = shifted(face_x1, "gx", 1)
-    from_x1 = shifted(face_x0, "gx", -1)
-    from_y0 = shifted(face_y1, "yz", 1)
-    from_y1 = shifted(face_y0, "yz", -1)
+    diffused = call(diffuse_kernel, "diffuse", shape(*gas_state.shape), flops=10**7)(
+        gas_state,
+        shifted(face_x1, "gx", 1),
+        shifted(face_x0, "gx", -1),
+        shifted(face_y1, "yz", 1),
+        shifted(face_y0, "yz", -1),
+    )
+    message, table, diffused = lax.optimization_barrier((message, table, diffused))
 
     blocks = devices * capacity
     result, source, ids = call(
@@ -357,12 +361,16 @@
         functools.partial(deposit_kernel, capacity=capacity),
         "deposit",
         shape(*gas_state.shape),
-        [smem()] + [vmem()] * 6,
-        scratch=[pltpu.VMEM((tiles * SUB, LANES), f32)],
+        scratch=[
+            pltpu.VMEM((tiles * SUB, LANES), f32),
+            pltpu.SMEM((devices, LANES), jnp.int32),
+            pltpu.SemaphoreType.DMA(()),
+        ],
         flops=3 * 10**7,
-    )(ids, source, gas_state, from_x0, from_x1, from_y0, from_y1)
-    result = result.reshape(devices, capacity, FLOWS, LANES)
-    return gas_next, result[:, :, :3].reshape(parcel_speed.shape), result[:, :, 3].reshape(parcel_mass.shape)
+    )(ids, source, diffused)
+    speed_next = result[:, : 3 * capacity].reshape(devices, 3, capacity, LANES).transpose(0, 2, 1, 3)
+    mass_next = result[:, 3 * capacity :]
+    return gas_next, speed_next.reshape(parcel_speed.shape), mass_next.reshape(parcel_mass.shape)
 
 
 def solution(mesh):

time: 75.9 us -> 55 us (0.72)
  the two profiles are of different devices: /device:TPU:6 before, /device:TPU:0 now
where the time goes in v2:
time: 55 us; the launch traced here: 54.4 us
  starting transfers between devices  20.5 us (37%)
  Pallas kernels  15.6 us (28%)
  waiting for transfers between devices  8.92 us (16%)
  local copies, waits for them, and re-layouts  8.66 us (16%)
  between operations  0.76 us (1%)
    pallas_call x1, Pallas kernels, shards(): call(functools.partial(deposit_kernel, capacity=capacity), 'deposit', sha...  9.38 us
    ppermute x4, starting transfers between devices, shifted(): return lax.ppermute(value, axis, pairs)  8.27 us
    unnamed x20, local copies, waits for them, and re-layouts  8.01 us
    all_to_all x1, starting transfers between devices, shards(): lax.all_to_all(message.reshape(devices, rows, 1, LANES), BOTH, split_axis...  7.33 us
    ppermute x4, waiting for transfers between devices, shifted(): return lax.ppermute(value, axis, pairs)  5.05 us
    all_to_all x1, starting transfers between devices, shards(): lax.all_to_all(result.reshape(devices, capacity * FLOWS, LANES), BOTH, sp...  4.93 us
    pallas_call x1, Pallas kernels, shards(): call(functools.partial(update_kernel, rows=rows, capacity=capacity), 'upd...  3.05 us
    all_to_all x1, waiting for transfers between devices, shards(): lax.all_to_all(message.reshape(devices, rows, 1, LANES), BOTH, split_axis...  2.81 us
  transfers between devices with their start and end apart: 6, of which 4 were waited for; matrix products, arithmetic and copies ran while one was open for 0% of the time, Pallas kernels for 21%

profile of v2, /device:TPU:0, one launch (start us, length us, event | category | flops | bytes accessed | tf_op | source)
XLA Modules:
  0.0 54.4 jit_solution(2988599563482936676)
XLA Ops:
  0.6 0.0 copy-start.3
  0.6 0.9 %copy-done.3 = f32[1,1,32,4,3,128]{5,3,4,2,1,0:T(4,128)S(1)} copy-done((f32[1,1,32,4,3,128]{5,3,4,2,1,0:T(4,128)S(1)}, f32[1,1,32,4,3,128]{5,3,4,2,1,0:T(4,128)}, u32[]{:S(2)}) %copy-start.3) | copy-done | bytes 196632
  1.6 0.0 copy-start.4
  1.6 0.9 %copy-done.4 = f32[1,1,32,4,3,128]{5,3,4,2,1,0:T(4,128)S(1)} copy-done((f32[1,1,32,4,3,128]{5,3,4,2,1,0:T(4,128)S(1)}, f32[1,1,32,4,3,128]{5,3,4,2,1,0:T(4,128)}, u32[]{:S(2)}) %copy-start.4) | copy-done | bytes 196632
  2.5 0.0 copy-start.5
  2.5 0.9 %copy-done.5 = s32[1,1,32,4,3,128]{5,3,4,2,1,0:T(4,128)S(1)} copy-done((s32[1,1,32,4,3,128]{5,3,4,2,1,0:T(4,128)S(1)}, s32[1,1,32,4,3,128]{5,3,4,2,1,0:T(4,128)}, u32[]{:S(2)}) %copy-start.5) | copy-done | bytes 196632
  3.4 0.0 copy-start.6
  3.4 0.8 %copy-done.6 = f32[1,1,32,4,128]{4,3,2,1,0:T(4,128)S(1)} copy-done((f32[1,1,32,4,128]{4,3,2,1,0:T(4,128)S(1)}, f32[1,1,32,4,128]{4,3,2,1,0:T(4,128)}, u32[]{:S(2)}) %copy-start.6) | copy-done | bytes 65560
  4.3 0.0 copy-start.7
  4.3 0.7 %copy-done.7 = s32[1,1,32,4]{2,3,1,0:T(4,128)S(1)} copy-done((s32[1,1,32,4]{2,3,1,0:T(4,128)S(1)}, s32[1,1,32,4]{2,3,1,0:T(4,128)}, u32[]{:S(2)}) %copy-start.7) | copy-done | bytes 536
  4.9 0.0 copy-start.8
  4.9 0.7 %copy-done.8 = s32[1,1,32]{2,1,0:T(1,128)S(1)} copy-done((s32[1,1,32]{2,1,0:T(1,128)S(1)}, s32[1,1,32]{2,1,0:T(1,128)}, u32[]{:S(2)}) %copy-start.8) | copy-done | bytes 152
  5.6 0.0 copy-start
  5.6 0.9 %pack.1 = f32[1312,128]{1,0:T(8,128)} custom-call(f32[384,128]{1,0:T(8,128)S(1)} %bitcast.32, f32[128,128]{1,0:T(8,128)S(1)} %bitcast.35, f32[384,128]{1,0:T(8,128)S(1)} %bitcast.33, s32[384,128]{1,0:T(8,128)S(1)} %bitcast.34, s32[4,32]{1,0:T(4,128)S(1)} %bitcast.36, s32[1,32]{1,0:T(1,128)S(1)} %bitcast.37), custom_call_target="tpu_custom_call" | custom-call | tf_op jit(solution)/shard_map/pack/pallas_call | solution.py:307
  6.5 7.3 %all-to-all-start = ((f32[32,41,1,128]{3,2,1,0:T(1,128)}), f32[32,41,1,128]{3,2,1,0:T(1,128)S(1)}, u32[]{:S(2)}, u32[]{:S(2)}) async-start(f32[32,41,1,128]{3,2,1,0:T(1,128)} %bitcast.13), calls=%async_computation | async-start | bytes 1343488 | tf_op jit(solution)/shard_map/all_to_all | solution.py:319
  13.9 0.0 copy-done
  13.9 1.2 %table.1 = (f32[4,512,128]{2,1,0:T(8,128)S(1)}, f32[5,16,256]{2,1,0:T(8,128)S(1)}, f32[5,16,256]{2,1,0:T(8,128)S(1)}, f32[5,16,256]{2,1,0:T(8,128)S(1)}, f32[5,16,256]{2,1,0:T(8,128)S(1)}) custom-call(f32[5,16,16,256]{3,2,1,0:T(8,128)S(1)} %copy-done), custom_call_target="tpu_custom_call" | custom-call | flops 10000000 | tf_op jit(solution)/shard_map/table/pallas_call | solution.py:323
  15.0 0.0 copy-start.1
  15.0 1.0 %copy-done.1 = f32[4,512,128]{2,1,0:T(8,128)} copy-done((f32[4,512,128]{2,1,0:T(8,128)}, f32[4,512,128]{2,1,0:T(8,128)S(1)}, u32[]{:S(2)}) %copy-start.1) | copy-done | bytes 1048600
  16.0 2.1 %collective-permute-start = (f32[5,16,256]{2,1,0:T(8,128)S(1)}, f32[5,16,256]{2,1,0:T(8,128)S(1)}, u32[]{:S(2)}, u32[]{:S(2)}) collective-permute-start(f32[5,16,256]{2,1,0:T(8,128)S(1)} %get-tuple-element.15), channel_id=1, source_target_pairs={{0,8},{8,16},{16,24},{1,9},{9,17},{17,25},{2,10},{10,18},{18,26},{... | collective-permute-start | bytes 245768 | tf_op jit(solution)/shard_map/ppermute | solution.py:333
  18.2 1.3 %collective-permute-start.1 = (f32[5,16,256]{2,1,0:T(8,128)S(1)}, f32[5,16,256]{2,1,0:T(8,128)S(1)}, u32[]{:S(2)}, u32[]{:S(2)}) collective-permute-start(f32[5,16,256]{2,1,0:T(8,128)S(1)} %get-tuple-element.16), channel_id=1, source_target_pairs={{8,0},{16,8},{24,16},{9,1},{17,9},{25,17},{10,2},{18,10},{26,18},{... | collective-permute-start | bytes 245768 | tf_op jit(solution)/shard_map/ppermute | solution.py:333
  19.5 3.5 %collective-permute-start.2 = (f32[5,16,256]{2,1,0:T(8,128)S(1)}, f32[5,16,256]{2,1,0:T(8,128)S(1)}, u32[]{:S(2)}, u32[]{:S(2)}) collective-permute-start(f32[5,16,256]{2,1,0:T(8,128)S(1)} %get-tuple-element.17), channel_id=1, source_target_pairs={{0,1},{1,2},{2,3},{3,4},{4,5},{5,6},{6,7},{8,9},{9,10},{10,11},{11... | collective-permute-start | bytes 245768 | tf_op jit(solution)/shard_map/ppermute | solution.py:333
  23.0 1.3 %collective-permute-start.3 = (f32[5,16,256]{2,1,0:T(8,128)S(1)}, f32[5,16,256]{2,1,0:T(8,128)S(1)}, u32[]{:S(2)}, u32[]{:S(2)}) collective-permute-start(f32[5,16,256]{2,1,0:T(8,128)S(1)} %get-tuple-element.18), channel_id=1, source_target_pairs={{1,0},{2,1},{3,2},{4,3},{5,4},{6,5},{7,6},{9,8},{10,9},{11,10},{12... | collective-permute-start | bytes 245768 | tf_op jit(solution)/shard_map/ppermute | solution.py:333
  24.3 0.0 collective-permute-done.from_x0
  24.3 0.0 collective-permute-done.1.from_x1
  24.3 0.7 %collective-permute-done.2.from_y0 = f32[5,16,256]{2,1,0:T(8,128)S(1)} collective-permute-done((f32[5,16,256]{2,1,0:T(8,128)S(1)}, f32[5,16,256]{2,1,0:T(8,128)S(1)}, u32[]{:S(2)}, u32[]{:S(2)}) %collective-permute-start.2) | collective-permute-done | bytes 81952 | tf_op jit(solution)/shard_map/ppermute | solution.py:333
  25.1 4.3 %collective-permute-done.3.from_y1 = f32[5,16,256]{2,1,0:T(8,128)S(1)} collective-permute-done((f32[5,16,256]{2,1,0:T(8,128)S(1)}, f32[5,16,256]{2,1,0:T(8,128)S(1)}, u32[]{:S(2)}, u32[]{:S(2)}) %collective-permute-start.3) | collective-permute-done | bytes 81952 | tf_op jit(solution)/shard_map/ppermute | solution.py:333
  29.4 1.1 %diffuse.1.diffused = f32[5,16,16,256]{3,2,1,0:T(8,128)S(1)} custom-call(f32[5,16,16,256]{3,2,1,0:T(8,128)S(1)} %copy-done, f32[5,16,256]{2,1,0:T(8,128)S(1)} %collective-permute-done.from_x0, f32[5,16,256]{2,1,0:T(8,128)S(1)} %collective-permute-done.1.from_x1, f32[5,16,256]{2,1,0:T(8,128)S(1)} %collective-permute-done.2.from_y0, ...), custom_call_target="tpu_custom_call" | custom-call | flops 10000000 | tf_op jit(solution)/shard_map/diffuse/pallas_call | solution.py:335
  30.4 2.8 %all-to-all-done = f32[32,41,1,128]{3,2,1,0:T(1,128)S(1)} async-done(((f32[32,41,1,128]{3,2,1,0:T(1,128)}), f32[32,41,1,128]{3,2,1,0:T(1,128)S(1)}, u32[]{:S(2)}, u32[]{:S(2)}) %all-to-all-start) | async-done | bytes 671776 | tf_op jit(solution)/shard_map/all_to_all | solution.py:319
  33.3 0.0 copy-start.2
  33.3 1.2 %copy-done.2 = f32[4,512,128]{2,1,0:T(8,128)S(1)} copy-done((f32[4,512,128]{2,1,0:T(8,128)S(1)}, f32[4,512,128]{2,1,0:T(8,128)}, u32[]{:S(2)}) %copy-start.2) | copy-done | bytes 1048600
  34.5 3.1 %update.1 = (f32[512,128]{1,0:T(8,128)}, f32[1024,128]{1,0:T(8,128)S(1)}, s32[32,128]{1,0:T(8,128)S(1)}) custom-call(f32[1312,128]{1,0:T(8,128)S(1)} %bitcast.31, f32[4,512,128]{2,1,0:T(8,128)S(1)} %copy-done.2), custom_call_target="tpu_custom_call" | custom-call | flops 10000000 | tf_op jit(solution)/shard_map/update/pallas_call | solution.py:345
  37.5 4.9 %all-to-all-start.1 = ((f32[32,16,128]{2,1,0:T(8,128)}), f32[32,16,128]{2,1,0:T(8,128)S(1)}, u32[]{:S(2)}, u32[]{:S(2)}) async-start(f32[32,16,128]{2,1,0:T(8,128)} %bitcast.15), calls=%async_computation.1 | async-start | bytes 524288 | tf_op jit(solution)/shard_map/all_to_all | solution.py:357
  42.5 9.4 %deposit.1 = f32[5,16,16,256]{3,2,1,0:T(8,128)} custom-call(s32[32,128]{1,0:T(8,128)S(1)} %get-tuple-element.21.ids_vmem, f32[1024,128]{1,0:T(8,128)S(1)} %get-tuple-element.22.source, f32[5,16,16,256]{3,2,1,0:T(8,128)S(1)} %diffuse.1.diffused), custom_call_target="tpu_custom_call" | custom-call | flops 30000000 | tf_op jit(solution)/shard_map/deposit/pallas_call | solution.py:360
  51.9 1.1 %all-to-all-done.1 = f32[32,16,128]{2,1,0:T(8,128)S(1)} async-done(((f32[32,16,128]{2,1,0:T(8,128)}), f32[32,16,128]{2,1,0:T(8,128)S(1)}, u32[]{:S(2)}, u32[]{:S(2)}) %all-to-all-start.1) | async-done | bytes 262176 | tf_op jit(solution)/shard_map/all_to_all | solution.py:357
  52.9 0.1 copy.16
  53.0 0.8 %copy.15 = f32[1,1,32,4,3,128]{5,3,4,2,1,0:T(4,128)} copy(f32[1,1,32,4,3,128]{5,2,3,4,1,0:T(8,128)S(1)} %bitcast.39) | data formatting | bytes 393216
  53.8 0.6 %slice_bitcast_fusion = f32[1,1,32,4,128]{4,3,2,1,0:T(4,128)} fusion(f32[32,16,128]{2,1,0:T(8,128)S(1)} %all-to-all-done.1), kind=kLoop, calls=%fused_computation | loop fusion | bytes 131072 | tf_op jit(solution)/shard_map/reshape | solution.py:373
Async XLA Ops:
  0.6 0.9 %copy-start.3 = (f32[1,1,32,4,3,128]{5,3,4,2,1,0:T(4,128)S(1)}, f32[1,1,32,4,3,128]{5,3,4,2,1,0:T(4,128)}, u32[]{:S(2)}) copy-start(f32[1,1,32,4,3,128]{5,3,4,2,1,0:T(4,128)} %param.8) | copy-start | bytes 589828
  1.6 0.9 %copy-start.4 = (f32[1,1,32,4,3,128]{5,3,4,2,1,0:T(4,128)S(1)}, f32[1,1,32,4,3,128]{5,3,4,2,1,0:T(4,128)}, u32[]{:S(2)}) copy-start(f32[1,1,32,4,3,128]{5,3,4,2,1,0:T(4,128)} %param.10) | copy-start | bytes 589828
  2.5 0.9 %copy-start.5 = (s32[1,1,32,4,3,128]{5,3,4,2,1,0:T(4,128)S(1)}, s32[1,1,32,4,3,128]{5,3,4,2,1,0:T(4,128)}, u32[]{:S(2)}) copy-start(s32[1,1,32,4,3,128]{5,3,4,2,1,0:T(4,128)} %param.11) | copy-start | bytes 589828
  3.4 0.8 %copy-start.6 = (f32[1,1,32,4,128]{4,3,2,1,0:T(4,128)S(1)}, f32[1,1,32,4,128]{4,3,2,1,0:T(4,128)}, u32[]{:S(2)}) copy-start(f32[1,1,32,4,128]{4,3,2,1,0:T(4,128)} %param.9) | copy-start | bytes 196612
  4.3 0.7 %copy-start.7 = (s32[1,1,32,4]{2,3,1,0:T(4,128)S(1)}, s32[1,1,32,4]{2,3,1,0:T(4,128)}, u32[]{:S(2)}) copy-start(s32[1,1,32,4]{2,3,1,0:T(4,128)} %param.12) | copy-start | bytes 1540
  4.9 0.7 %copy-start.8 = (s32[1,1,32]{2,1,0:T(1,128)S(1)}, s32[1,1,32]{2,1,0:T(1,128)}, u32[]{:S(2)}) copy-start(s32[1,1,32]{2,1,0:T(1,128)} %param.13) | copy-start | bytes 388
  5.6 8.3 %copy-start = (f32[5,16,16,256]{3,2,1,0:T(8,128)S(1)}, f32[5,16,16,256]{3,2,1,0:T(8,128)}, u32[]{:S(2)}) copy-start(f32[5,16,16,256]{3,2,1,0:T(8,128)} %gas.3) | copy-start | bytes 3932164
  6.5 26.7 %all-to-all-start = ((f32[32,41,1,128]{3,2,1,0:T(1,128)}), f32[32,41,1,128]{3,2,1,0:T(1,128)S(1)}, u32[]{:S(2)}, u32[]{:S(2)}) async-start(f32[32,41,1,128]{3,2,1,0:T(1,128)} %bitcast.13), calls=%async_computation | async-start | bytes 1343488 | tf_op jit(solution)/shard_map/all_to_all | solution.py:319
  15.0 1.0 %copy-start.1 = (f32[4,512,128]{2,1,0:T(8,128)}, f32[4,512,128]{2,1,0:T(8,128)S(1)}, u32[]{:S(2)}) copy-start(f32[4,512,128]{2,1,0:T(8,128)S(1)} %get-tuple-element.20.table) | copy-start | bytes 3145732
  16.0 8.3 %collective-permute-start = (f32[5,16,256]{2,1,0:T(8,128)S(1)}, f32[5,16,256]{2,1,0:T(8,128)S(1)}, u32[]{:S(2)}, u32[]{:S(2)}) collective-permute-start(f32[5,16,256]{2,1,0:T(8,128)S(1)} %get-tuple-element.15), channel_id=1, source_target_pairs={{0,8},{8,16},{16,24},{1,9},{9,17},{17,25},{2,10},{10,18},{18,26},{... | collective-permute-start | bytes 245768 | tf_op jit(solution)/shard_map/ppermute | solution.py:333
  18.2 6.2 %collective-permute-start.1 = (f32[5,16,256]{2,1,0:T(8,128)S(1)}, f32[5,16,256]{2,1,0:T(8,128)S(1)}, u32[]{:S(2)}, u32[]{:S(2)}) collective-permute-start(f32[5,16,256]{2,1,0:T(8,128)S(1)} %get-tuple-element.16), channel_id=1, source_target_pairs={{8,0},{16,8},{24,16},{9,1},{17,9},{25,17},{10,2},{18,10},{26,18},{... | collective-permute-start | bytes 245768 | tf_op jit(solution)/shard_map/ppermute | solution.py:333
  19.5 5.6 %collective-permute-start.2 = (f32[5,16,256]{2,1,0:T(8,128)S(1)}, f32[5,16,256]{2,1,0:T(8,128)S(1)}, u32[]{:S(2)}, u32[]{:S(2)}) collective-permute-start(f32[5,16,256]{2,1,0:T(8,128)S(1)} %get-tuple-element.17), channel_id=1, source_target_pairs={{0,1},{1,2},{2,3},{3,4},{4,5},{5,6},{6,7},{8,9},{9,10},{10,11},{11... | collective-permute-start | bytes 245768 | tf_op jit(solution)/shard_map/ppermute | solution.py:333
  23.0 6.4 %collective-permute-start.3 = (f32[5,16,256]{2,1,0:T(8,128)S(1)}, f32[5,16,256]{2,1,0:T(8,128)S(1)}, u32[]{:S(2)}, u32[]{:S(2)}) collective-permute-start(f32[5,16,256]{2,1,0:T(8,128)S(1)} %get-tuple-element.18), channel_id=1, source_target_pairs={{1,0},{2,1},{3,2},{4,3},{5,4},{6,5},{7,6},{9,8},{10,9},{11,10},{12... | collective-permute-start | bytes 245768 | tf_op jit(solution)/shard_map/ppermute | solution.py:333
  33.3 1.2 %copy-start.2 = (f32[4,512,128]{2,1,0:T(8,128)S(1)}, f32[4,512,128]{2,1,0:T(8,128)}, u32[]{:S(2)}) copy-start(f32[4,512,128]{2,1,0:T(8,128)} %copy-done.1) | copy-start | bytes 3145732
  37.5 15.4 %all-to-all-start.1 = ((f32[32,16,128]{2,1,0:T(8,128)}), f32[32,16,128]{2,1,0:T(8,128)S(1)}, u32[]{:S(2)}, u32[]{:S(2)}) async-start(f32[32,16,128]{2,1,0:T(8,128)} %bitcast.15), calls=%async_computation.1 | async-start | bytes 524288 | tf_op jit(solution)/shard_map/all_to_all | solution.py:357

commit v3 on v2

--- a/solution.py
+++ b/solution.py
@@ -49,26 +49,66 @@
     return pair
 
 
-def pack_kernel(speed, mass, offsets, cells, tile_ids, counts, message, *, rows, capacity):
-    group = SUB * rows
+def pack_kernel(
+    speed, mass, offsets, cells, tile_ids, counts, message,
+    speed_v, mass_v, offsets_v, cells_v, tile_ids_v, counts_v, ids_v, message_v, sems, *, rows, capacity
+):
+    owners = tile_ids.shape[1]
     vector = 3 * capacity
-    owners = tile_ids.shape[1]
-    slot = lax.broadcasted_iota(jnp.int32, tile_ids.shape, 0)
-    ids = jnp.where(slot < counts[...], tile_ids[...], -1).astype(jnp.float32)
-    ids = jnp.concatenate([ids, jnp.zeros((LANES - capacity, owners), jnp.float32)], axis=0).T
-
-    for g in range(owners // SUB):
+    sources = ((speed, speed_v, vector), (offsets, offsets_v, vector), (cells, cells_v, vector), (mass, mass_v, capacity))
+    parts = 2
+    each = owners // parts
+    small = [
+        pltpu.make_async_copy(tile_ids, tile_ids_v, sems.at[0]),
+        pltpu.make_async_copy(counts, counts_v, sems.at[1]),
+    ]
+    taken = []
+    for copy in small:
+        copy.start()
+    for part in range(parts):
+        taken.append([])
+        for n, (source, held, count) in enumerate(sources):
+            place = pl.ds(part * each * count, each * count)
+            copy = pltpu.make_async_copy(source.at[place], held.at[place], sems.at[2 + part * 4 + n])
+            copy.start()
+            taken[-1].append(copy)
+    for copy in small:
+        copy.wait()
+    slot = lax.broadcasted_iota(jnp.int32, tile_ids_v.shape, 0)
+    ids = jnp.where(slot < counts_v[...], tile_ids_v[...], -1).astype(jnp.float32)
+    ids_v[...] = jnp.concatenate([ids, jnp.zeros((LANES - capacity, owners), jnp.float32)], axis=0).T
+
+    def per_group(g, carry):
+        def at(held, count):
+            return held.at[pl.ds(pl.multiple_of(g * SUB * count, SUB), SUB * count)]
+
+        out = at(message_v, rows)
+        speed_g, offsets_g, cells_g, mass_g = (at(held, count) for _, held, count in sources)
+        ids_g = at(ids_v, 1)
         for i in range(SUB):
-            d = g * SUB + i
-            base = d * rows
-            message[base : base + vector, :] = speed[d * vector : (d + 1) * vector, :]
-            message[base + vector : base + 2 * vector, :] = offsets[d * vector : (d + 1) * vector, :]
-            message[base + 2 * vector : base + 3 * vector, :] = cells[d * vector : (d + 1) * vector, :].astype(jnp.float32)
-            message[base + 3 * vector : base + 3 * vector + capacity, :] = mass[d * capacity : (d + 1) * capacity, :]
-            message[base + rows - 1 : base + rows, :] = ids[d : d + 1, :]
-
-
-def table_kernel(gas, table, face_x0, face_x1, face_y0, face_y1):
+            base = i * rows
+            place = slice(i * vector, (i + 1) * vector)
+            out[base : base + vector, :] = speed_g[place, :]
+            out[base + vector : base + 2 * vector, :] = offsets_g[place, :]
+            out[base + 2 * vector : base + 3 * vector, :] = cells_g[place, :].astype(jnp.float32)
+            out[base + 3 * vector : base + 3 * vector + capacity, :] = mass_g[i * capacity : (i + 1) * capacity, :]
+            out[base + rows - 1 : base + rows, :] = ids_g[i : i + 1, :]
+        return carry
+
+    sent = []
+    for part in range(parts):
+        for copy in taken[part]:
+            copy.wait()
+        lax.fori_loop(part * each // SUB, (part + 1) * each // SUB, per_group, 0)
+        place = pl.ds(part * each * rows, each * rows)
+        copy = pltpu.make_async_copy(message_v.at[place], message.at[place], sems.at[2 + parts * 4 + part])
+        copy.start()
+        sent.append(copy)
+    for copy in sent:
+        copy.wait()
+
+
+def table_kernel(gas, table_hbm, face_x0, face_x1, face_y0, face_y1, table, sem):
     fields, extent_x, extent_y, extent_z = gas.shape
     across_y = extent_y // TILE_Y
     across_z = extent_z // TILE_Z
@@ -96,17 +136,22 @@
         return carry
 
     lax.fori_loop(0, extent_x // TILE_X, per_a, 0)
-
-
-def update_kernel(message, table, result, source, ids_out, ids_vmem, ids_smem, products, sem, *, rows, capacity):
+    copy = pltpu.make_async_copy(table, table_hbm, sem)
+    copy.start()
+    copy.wait()
+
+
+def update_kernel(
+    message, table_hbm, result_hbm, source, ids_vmem, ids_smem, products, table, result, sems, *, rows, capacity
+):
     devices = message.shape[0] // rows
     group = SUB * rows
+    fetch = pltpu.make_async_copy(table_hbm, table, sems.at[0])
+    fetch.start()
     for g in range(devices // SUB):
         ids_vmem[g * SUB : (g + 1) * SUB, :] = message[pl.ds(g * group + rows - 1, SUB, stride=rows), :].astype(jnp.int32)
-    ids_out[...] = ids_vmem[...]
-    copy = pltpu.make_async_copy(ids_vmem, ids_smem, sem)
+    copy = pltpu.make_async_copy(ids_vmem, ids_smem, sems.at[1])
     copy.start()
-    copy.wait()
     corner = lax.broadcasted_iota(jnp.int32, (SUB, LANES), 0)
     high = [(corner & bit) != 0 for bit in (4, 2, 1)]
     least = [jnp.where(h, 0.0, 1.0) for h in high]
@@ -115,6 +160,12 @@
         jnp.where(high[0], TILE_Y * TILE_Z, 0) + jnp.where(high[1], TILE_Z, 0) + jnp.where(high[2], 1, 0)
     )
     row = corner
+    copy.wait()
+    fetch.wait()
+
+    def returned(g):
+        place = pl.ds(pl.multiple_of(g * SUB * capacity * FLOWS, SUB), SUB * capacity * FLOWS)
+        return pltpu.make_async_copy(result.at[place], result_hbm.at[place], sems.at[2 + g])
 
     def per_group(g, carry):
         part = message.at[pl.ds(pl.multiple_of(g * group, SUB), group)]
@@ -132,7 +183,8 @@
                     fraction = part[start : start + 1, :]
                     along = least[dim] + slope[dim] * fraction
                     weight = along if weight is None else weight * along
-                cell = [part[base + (6 + dim) * capacity + k, :][None] for dim in range(3)]
+                starts = [base + (6 + dim) * capacity + k for dim in range(3)]
+                cell = [part[start : start + 1, :] for start in starts]
                 first = (cell[0] * TILE_Y + cell[1]) * TILE_Z + cell[2]
                 index = first.astype(jnp.int32) + shift
                 for f in range(FLOWS):
@@ -178,9 +230,12 @@
             out = source.at[pl.ds(pl.multiple_of(first_block * SUB, SUB), SUB * SUB)]
             for f in range(7):
                 out[pl.ds(f, SUB, stride=SUB), :] = sources[f]
+        returned(g).start()
         return carry
 
     lax.fori_loop(0, devices // SUB, per_group, 0)
+    for g in range(devices // SUB):
+        returned(g).wait()
 
 
 def tent(position, cell):
@@ -280,15 +335,51 @@
     lax.fori_loop(0, extent_x // TILE_X, per_a, 0)
 
 
-def call(kernel, name, out_shape, scratch=(), flops=0, moved=0):
-    return pl.pallas_call(
+def unpack_kernel(result, speed, mass, sems):
+    vector = speed.shape[1]
+    copies = [
+        pltpu.make_async_copy(result.at[:, :vector], speed, sems.at[0]),
+        pltpu.make_async_copy(result.at[:, vector:], mass, sems.at[1]),
+    ]
+    for copy in copies:
+        copy.start()
+    for copy in copies:
+        copy.wait()
+
+
+def specs(spaces):
+    return [pl.BlockSpec(memory_space=space) for space in spaces]
+
+
+def call(kernel, name, out_shape, scratch=(), flops=0, moved=0, ins=None, outs=None):
+    extra = {}
+    if ins is not None:
+        extra["in_specs"] = specs(ins)
+    if outs is not None:
+        extra["out_specs"] = specs(outs) if len(outs) > 1 else specs(outs)[0]
+        if pltpu.HBM in outs:
+            shapes = out_shape if len(outs) > 1 else (out_shape,)
+            shapes = [pltpu.HBM(o.shape, o.dtype) if space == pltpu.HBM else o for o, space in zip(shapes, outs)]
+            out_shape = shapes if len(outs) > 1 else shapes[0]
+    called = pl.pallas_call(
         kernel,
         out_shape=out_shape,
         scratch_shapes=scratch,
         name=name,
         cost_estimate=pl.CostEstimate(flops=flops, bytes_accessed=moved, transcendentals=0),
         compiler_params=pltpu.CompilerParams(vmem_limit_bytes=32 * 1024 * 1024),
-    )
+        **extra,
+    )
+
+    def with_spaces(*values):
+        if ins is not None:
+            values = [
+                pltpu.with_memory_space_constraint(v, space) if space == pltpu.HBM else v
+                for v, space in zip(values, ins)
+            ]
+        return called(*values)
+
+    return with_spaces
 
 
 def shards(gas_state, parcel_speed, parcel_mass, offsets, cell_base, block_tile, block_count):
@@ -304,13 +395,31 @@
     def by_component(value):
         return value[0, 0].transpose(0, 2, 1, 3).reshape(devices * 3 * capacity, LANES)
 
+    vector = 3 * capacity
+    blocks = devices * capacity
+    i32 = jnp.int32
+    hbm, vmem = pltpu.HBM, pltpu.VMEM
+    dma = pltpu.SemaphoreType.DMA
     message = call(
         functools.partial(pack_kernel, rows=rows, capacity=capacity),
         "pack",
         shape(devices * rows, LANES),
+        scratch=[
+            vmem((devices * vector, LANES), f32),
+            vmem((blocks, LANES), f32),
+            vmem((devices * vector, LANES), f32),
+            vmem((devices * vector, LANES), i32),
+            vmem((capacity, devices), i32),
+            vmem((1, devices), i32),
+            vmem((devices, LANES), f32),
+            vmem((devices * rows, LANES), f32),
+            dma((12,)),
+        ],
+        ins=[hbm] * 6,
+        outs=[hbm],
     )(
         by_component(parcel_speed),
-        parcel_mass.reshape(devices * capacity, LANES),
+        parcel_mass.reshape(blocks, LANES),
         by_component(offsets),
         by_component(cell_base),
         block_tile[0, 0].T,
@@ -324,7 +433,10 @@
         table_kernel,
         "table",
         (shape(FLOWS, tiles, LANES), shape(fields, extent_y, extent_z), shape(fields, extent_y, extent_z), face, face),
+        scratch=[vmem((FLOWS, tiles, LANES), f32), dma(())],
         flops=10**7,
+        ins=[vmem],
+        outs=[hbm] + [vmem] * 4,
     )(gas_state)
 
     def shifted(value, axis, step):
@@ -341,35 +453,40 @@
     )
     message, table, diffused = lax.optimization_barrier((message, table, diffused))
 
-    blocks = devices * capacity
     result, source, ids = call(
         functools.partial(update_kernel, rows=rows, capacity=capacity),
         "update",
-        (shape(blocks * FLOWS, LANES), shape(blocks * SUB, LANES), shape(devices, LANES, dtype=jnp.int32)),
+        (shape(blocks * FLOWS, LANES), shape(blocks * SUB, LANES), shape(devices, LANES, dtype=i32)),
         scratch=[
-            pltpu.VMEM((devices, LANES), jnp.int32),
-            pltpu.SMEM((devices, LANES), jnp.int32),
-            pltpu.VMEM((FLOWS * SUB * SUB, LANES), f32),
-            pltpu.SemaphoreType.DMA(()),
+            pltpu.SMEM((devices, LANES), i32),
+            vmem((FLOWS * SUB * SUB, LANES), f32),
+            vmem((FLOWS, tiles, LANES), f32),
+            vmem((blocks * FLOWS, LANES), f32),
+            dma((2 + devices // SUB,)),
         ],
         flops=10**7,
+        ins=[vmem, hbm],
+        outs=[hbm, vmem, vmem],
     )(message, table)
     result = lax.all_to_all(
-        result.reshape(devices, capacity * FLOWS, LANES), BOTH, split_axis=0, concat_axis=0, tiled=True
+        result.reshape(devices, capacity * FLOWS, 1, LANES), BOTH, split_axis=0, concat_axis=0, tiled=True
     )
     gas_next = call(
         functools.partial(deposit_kernel, capacity=capacity),
         "deposit",
         shape(*gas_state.shape),
-        scratch=[
-            pltpu.VMEM((tiles * SUB, LANES), f32),
-            pltpu.SMEM((devices, LANES), jnp.int32),
-            pltpu.SemaphoreType.DMA(()),
-        ],
+        scratch=[vmem((tiles * SUB, LANES), f32), pltpu.SMEM((devices, LANES), i32), dma(())],
         flops=3 * 10**7,
     )(ids, source, diffused)
-    speed_next = result[:, : 3 * capacity].reshape(devices, 3, capacity, LANES).transpose(0, 2, 1, 3)
-    mass_next = result[:, 3 * capacity :]
+    speed_next, mass_next = call(
+        unpack_kernel,
+        "unpack",
+        (shape(devices, vector, 1, LANES), shape(devices, capacity, 1, LANES)),
+        scratch=[dma((2,))],
+        ins=[vmem],
+        outs=[hbm, hbm],
+    )(result)
+    speed_next = speed_next.reshape(devices, 3, capacity, LANES).transpose(0, 2, 1, 3)
     return gas_next, speed_next.reshape(parcel_speed.shape), mass_next.reshape(parcel_mass.shape)
 
 

time: 55 us -> 49.5 us (0.900)
  local copies, waits for them, and re-layouts: 8.66 us -> 0.01 us
  Pallas kernels: 15.6 us -> 18.9 us
    unnamed x20 -> x2, local copies, waits for them, and re-layouts: 8.01 us -> 0.01 us
    pallas_call x5 -> x6, Pallas kernels: 15.6 us -> 18.9 us  [with_spaces(): return called(*values)]
    reshape x1 -> x0, local copies, waits for them, and re-layouts: 0.64 us -> none  [shards(): mass_next.reshape(parcel_mass.shape)]
  transfers between devices with their start and end apart: 6 -> 6, of which waited for: 4 -> 4; matrix products, arithmetic and copies ran while one was open for 0% -> 0% of each run, Pallas kernels for 21% -> 26%
where the time goes in v3:
time: 49.5 us; the launch traced here: 49.1 us
  starting transfers between devices  20.6 us (42%)
  Pallas kernels  18.9 us (38%)
  waiting for transfers between devices  8.88 us (18%)
  between operations  0.75 us (2%)
    pallas_call x6, Pallas kernels, with_spaces(): return called(*values)  18.9 us
    ppermute x4, starting transfers between devices, shifted(): return lax.ppermute(value, axis, pairs)  8.28 us
    all_to_all x1, starting transfers between devices, shards(): lax.all_to_all(message.reshape(devices, rows, 1, LANES), BOTH, split_axis...  7.33 us
    ppermute x4, waiting for transfers between devices, shifted(): return lax.ppermute(value, axis, pairs)  5.05 us
    all_to_all x1, starting transfers between devices, shards(): lax.all_to_all(result.reshape(devices, capacity * FLOWS, 1, LANES), BOTH,...  4.96 us
    all_to_all x1, waiting for transfers between devices, shards(): lax.all_to_all(message.reshape(devices, rows, 1, LANES), BOTH, split_axis...  2.79 us
    all_to_all x1, waiting for transfers between devices, shards(): lax.all_to_all(result.reshape(devices, capacity * FLOWS, 1, LANES), BOTH,...  1.04 us
  transfers between devices with their start and end apart: 6, of which 4 were waited for; matrix products, arithmetic and copies ran while one was open for 0% of the time, Pallas kernels for 26%

profile of v3, /device:TPU:0, one launch (start us, length us, event | category | flops | bytes accessed | tf_op | source)
XLA Modules:
  0.0 49.1 jit_solution(9962563925746954908)
XLA Ops:
  0.6 0.0 copy-start
  0.6 2.1 %pack.1 = f32[1312,128]{1,0:T(8,128)} custom-call(f32[384,128]{1,0:T(8,128)} %bitcast.32, f32[128,128]{1,0:T(8,128)} %bitcast.35, f32[384,128]{1,0:T(8,128)} %bitcast.33, s32[384,128]{1,0:T(8,128)} %bitcast.34, s32[4,32]{1,0:T(4,128)} %bitcast.36, s32[1,32]{1,0:T(1,128)} %bitcast.37), custom_call_target="tpu_custom_call" | custom-call | tf_op jit(solution)/shard_map/pack/pallas_call | solution.py:380
  2.8 7.3 %all-to-all-start = ((f32[32,41,1,128]{3,2,1,0:T(1,128)}), f32[32,41,1,128]{3,2,1,0:T(1,128)S(1)}, u32[]{:S(2)}, u32[]{:S(2)}) async-start(f32[32,41,1,128]{3,2,1,0:T(1,128)} %bitcast.30), calls=%async_computation | async-start | bytes 1343488 | tf_op jit(solution)/shard_map/all_to_all | solution.py:428
  10.1 0.0 copy-done
  10.1 2.1 %table.1 = (f32[4,512,128]{2,1,0:T(8,128)}, f32[5,16,256]{2,1,0:T(8,128)S(1)}, f32[5,16,256]{2,1,0:T(8,128)S(1)}, f32[5,16,256]{2,1,0:T(8,128)S(1)}, f32[5,16,256]{2,1,0:T(8,128)S(1)}) custom-call(f32[5,16,16,256]{3,2,1,0:T(8,128)S(1)} %copy-done), custom_call_target="tpu_custom_call" | custom-call | flops 10000000 | tf_op jit(solution)/shard_map/table/pallas_call | solution.py:380
  12.3 2.2 %collective-permute-start = (f32[5,16,256]{2,1,0:T(8,128)S(1)}, f32[5,16,256]{2,1,0:T(8,128)S(1)}, u32[]{:S(2)}, u32[]{:S(2)}) collective-permute-start(f32[5,16,256]{2,1,0:T(8,128)S(1)} %get-tuple-element.17), channel_id=1, source_target_pairs={{0,8},{8,16},{16,24},{1,9},{9,17},{17,25},{2,10},{10,18},{18,26},{... | collective-permute-start | bytes 245768 | tf_op jit(solution)/shard_map/ppermute | solution.py:445
  14.5 1.3 %collective-permute-start.1 = (f32[5,16,256]{2,1,0:T(8,128)S(1)}, f32[5,16,256]{2,1,0:T(8,128)S(1)}, u32[]{:S(2)}, u32[]{:S(2)}) collective-permute-start(f32[5,16,256]{2,1,0:T(8,128)S(1)} %get-tuple-element.18), channel_id=1, source_target_pairs={{8,0},{16,8},{24,16},{9,1},{17,9},{25,17},{10,2},{18,10},{26,18},{... | collective-permute-start | bytes 245768 | tf_op jit(solution)/shard_map/ppermute | solution.py:445
  15.8 3.5 %collective-permute-start.2 = (f32[5,16,256]{2,1,0:T(8,128)S(1)}, f32[5,16,256]{2,1,0:T(8,128)S(1)}, u32[]{:S(2)}, u32[]{:S(2)}) collective-permute-start(f32[5,16,256]{2,1,0:T(8,128)S(1)} %get-tuple-element.19), channel_id=1, source_target_pairs={{0,1},{1,2},{2,3},{3,4},{4,5},{5,6},{6,7},{8,9},{9,10},{10,11},{11... | collective-permute-start | bytes 245768 | tf_op jit(solution)/shard_map/ppermute | solution.py:445
  19.3 1.3 %collective-permute-start.3 = (f32[5,16,256]{2,1,0:T(8,128)S(1)}, f32[5,16,256]{2,1,0:T(8,128)S(1)}, u32[]{:S(2)}, u32[]{:S(2)}) collective-permute-start(f32[5,16,256]{2,1,0:T(8,128)S(1)} %get-tuple-element.20), channel_id=1, source_target_pairs={{1,0},{2,1},{3,2},{4,3},{5,4},{6,5},{7,6},{9,8},{10,9},{11,10},{12... | collective-permute-start | bytes 245768 | tf_op jit(solution)/shard_map/ppermute | solution.py:445
  20.6 0.0 collective-permute-done.from_x0
  20.6 0.0 collective-permute-done.1.from_x1
  20.6 0.7 %collective-permute-done.2.from_y0 = f32[5,16,256]{2,1,0:T(8,128)S(1)} collective-permute-done((f32[5,16,256]{2,1,0:T(8,128)S(1)}, f32[5,16,256]{2,1,0:T(8,128)S(1)}, u32[]{:S(2)}, u32[]{:S(2)}) %collective-permute-start.2) | collective-permute-done | bytes 81952 | tf_op jit(solution)/shard_map/ppermute | solution.py:445
  21.4 4.3 %collective-permute-done.3.from_y1 = f32[5,16,256]{2,1,0:T(8,128)S(1)} collective-permute-done((f32[5,16,256]{2,1,0:T(8,128)S(1)}, f32[5,16,256]{2,1,0:T(8,128)S(1)}, u32[]{:S(2)}, u32[]{:S(2)}) %collective-permute-start.3) | collective-permute-done | bytes 81952 | tf_op jit(solution)/shard_map/ppermute | solution.py:445
  25.7 1.1 %diffuse.1.diffused = f32[5,16,16,256]{3,2,1,0:T(8,128)S(1)} custom-call(f32[5,16,16,256]{3,2,1,0:T(8,128)S(1)} %copy-done, f32[5,16,256]{2,1,0:T(8,128)S(1)} %collective-permute-done.from_x0, f32[5,16,256]{2,1,0:T(8,128)S(1)} %collective-permute-done.1.from_x1, f32[5,16,256]{2,1,0:T(8,128)S(1)} %collective-permute-done.2.from_y0, ...), custom_call_target="tpu_custom_call" | custom-call | flops 10000000 | tf_op jit(solution)/shard_map/diffuse/pallas_call | solution.py:380
  26.7 2.8 %all-to-all-done = f32[32,41,1,128]{3,2,1,0:T(1,128)S(1)} async-done(((f32[32,41,1,128]{3,2,1,0:T(1,128)}), f32[32,41,1,128]{3,2,1,0:T(1,128)S(1)}, u32[]{:S(2)}, u32[]{:S(2)}) %all-to-all-start) | async-done | bytes 671776 | tf_op jit(solution)/shard_map/all_to_all | solution.py:428
  29.5 3.4 %update.1 = (f32[512,128]{1,0:T(8,128)}, f32[1024,128]{1,0:T(8,128)S(1)}, s32[32,128]{1,0:T(8,128)S(1)}) custom-call(f32[1312,128]{1,0:T(8,128)S(1)} %bitcast.29, f32[4,512,128]{2,1,0:T(8,128)} %get-tuple-element.22.table_hbm), custom_call_target="tpu_custom_call" | custom-call | flops 10000000 | tf_op jit(solution)/shard_map/update/pallas_call | solution.py:380
  32.9 5.0 %all-to-all-start.1 = ((f32[32,16,1,128]{3,2,1,0:T(1,128)}), f32[32,16,1,128]{3,2,1,0:T(1,128)S(1)}, u32[]{:S(2)}, u32[]{:S(2)}) async-start(f32[32,16,1,128]{3,2,1,0:T(1,128)} %bitcast.31), calls=%async_computation.1 | async-start | bytes 524288 | tf_op jit(solution)/shard_map/all_to_all | solution.py:471
  37.9 9.4 %deposit.1 = f32[5,16,16,256]{3,2,1,0:T(8,128)} custom-call(s32[32,128]{1,0:T(8,128)S(1)} %get-tuple-element.23.ids_vmem, f32[1024,128]{1,0:T(8,128)S(1)} %get-tuple-element.24.source, f32[5,16,16,256]{3,2,1,0:T(8,128)S(1)} %diffuse.1.diffused), custom_call_target="tpu_custom_call" | custom-call | flops 30000000 | tf_op jit(solution)/shard_map/deposit/pallas_call | solution.py:380
  47.3 1.0 %all-to-all-done.1.result = f32[32,16,1,128]{3,2,1,0:T(1,128)S(1)} async-done(((f32[32,16,1,128]{3,2,1,0:T(1,128)}), f32[32,16,1,128]{3,2,1,0:T(1,128)S(1)}, u32[]{:S(2)}, u32[]{:S(2)}) %all-to-all-start.1) | async-done | bytes 262176 | tf_op jit(solution)/shard_map/all_to_all | solution.py:471
  48.4 0.7 %unpack.1 = (f32[32,12,1,128]{3,2,1,0:T(1,128)}, f32[32,4,1,128]{3,2,1,0:T(1,128)}) custom-call(f32[32,16,1,128]{3,2,1,0:T(1,128)S(1)} %all-to-all-done.1.result), custom_call_target="tpu_custom_call" | custom-call | tf_op jit(solution)/shard_map/unpack/pallas_call | solution.py:380
Async XLA Ops:
  0.6 9.5 %copy-start = (f32[5,16,16,256]{3,2,1,0:T(8,128)S(1)}, f32[5,16,16,256]{3,2,1,0:T(8,128)}, u32[]{:S(2)}) copy-start(f32[5,16,16,256]{3,2,1,0:T(8,128)} %gas.3) | copy-start | bytes 3932164
  2.8 26.7 %all-to-all-start = ((f32[32,41,1,128]{3,2,1,0:T(1,128)}), f32[32,41,1,128]{3,2,1,0:T(1,128)S(1)}, u32[]{:S(2)}, u32[]{:S(2)}) async-start(f32[32,41,1,128]{3,2,1,0:T(1,128)} %bitcast.30), calls=%async_computation | async-start | bytes 1343488 | tf_op jit(solution)/shard_map/all_to_all | solution.py:428
  12.3 8.3 %collective-permute-start = (f32[5,16,256]{2,1,0:T(8,128)S(1)}, f32[5,16,256]{2,1,0:T(8,128)S(1)}, u32[]{:S(2)}, u32[]{:S(2)}) collective-permute-start(f32[5,16,256]{2,1,0:T(8,128)S(1)} %get-tuple-element.17), channel_id=1, source_target_pairs={{0,8},{8,16},{16,24},{1,9},{9,17},{17,25},{2,10},{10,18},{18,26},{... | collective-permute-start | bytes 245768 | tf_op jit(solution)/shard_map/ppermute | solution.py:445
  14.5 6.2 %collective-permute-start.1 = (f32[5,16,256]{2,1,0:T(8,128)S(1)}, f32[5,16,256]{2,1,0:T(8,128)S(1)}, u32[]{:S(2)}, u32[]{:S(2)}) collective-permute-start(f32[5,16,256]{2,1,0:T(8,128)S(1)} %get-tuple-element.18), channel_id=1, source_target_pairs={{8,0},{16,8},{24,16},{9,1},{17,9},{25,17},{10,2},{18,10},{26,18},{... | collective-permute-start | bytes 245768 | tf_op jit(solution)/shard_map/ppermute | solution.py:445
  15.8 5.6 %collective-permute-start.2 = (f32[5,16,256]{2,1,0:T(8,128)S(1)}, f32[5,16,256]{2,1,0:T(8,128)S(1)}, u32[]{:S(2)}, u32[]{:S(2)}) collective-permute-start(f32[5,16,256]{2,1,0:T(8,128)S(1)} %get-tuple-element.19), channel_id=1, source_target_pairs={{0,1},{1,2},{2,3},{3,4},{4,5},{5,6},{6,7},{8,9},{9,10},{10,11},{11... | collective-permute-start | bytes 245768 | tf_op jit(solution)/shard_map/ppermute | solution.py:445
  19.3 6.4 %collective-permute-start.3 = (f32[5,16,256]{2,1,0:T(8,128)S(1)}, f32[5,16,256]{2,1,0:T(8,128)S(1)}, u32[]{:S(2)}, u32[]{:S(2)}) collective-permute-start(f32[5,16,256]{2,1,0:T(8,128)S(1)} %get-tuple-element.20), channel_id=1, source_target_pairs={{1,0},{2,1},{3,2},{4,3},{5,4},{6,5},{7,6},{9,8},{10,9},{11,10},{12... | collective-permute-start | bytes 245768 | tf_op jit(solution)/shard_map/ppermute | solution.py:445
  32.9 15.4 %all-to-all-start.1 = ((f32[32,16,1,128]{3,2,1,0:T(1,128)}), f32[32,16,1,128]{3,2,1,0:T(1,128)S(1)}, u32[]{:S(2)}, u32[]{:S(2)}) async-start(f32[32,16,1,128]{3,2,1,0:T(1,128)} %bitcast.31), calls=%async_computation.1 | async-start | bytes 524288 | tf_op jit(solution)/shard_map/all_to_all | solution.py:471

commit v4 on v3

--- a/solution.py
+++ b/solution.py
@@ -6,6 +6,7 @@
 from jax.experimental import pallas as pl
 from jax.experimental.pallas import tpu as pltpu
 from jax.sharding import PartitionSpec as P
+
 
 TILE_X = 4
 TILE_Y = 4
@@ -108,14 +109,46 @@
         copy.wait()
 
 
-def table_kernel(gas, table_hbm, face_x0, face_x1, face_y0, face_y1, table, sem):
-    fields, extent_x, extent_y, extent_z = gas.shape
-    across_y = extent_y // TILE_Y
-    across_z = extent_z // TILE_Z
+def faces_kernel(gas_hbm, face_x0, face_x1, face_y0, face_y1, gas, sem):
+    extent_x, extent_y = gas_hbm.shape[1:3]
+    copy = pltpu.make_async_copy(gas_hbm, gas, sem)
+    copy.start()
+    copy.wait()
     face_x0[...] = gas[:, 0]
     face_x1[...] = gas[:, extent_x - 1]
     face_y0[...] = gas[:, :, 0, :]
     face_y1[...] = gas[:, :, extent_y - 1, :]
+
+
+def local_kernel(gas_hbm, table, diffused_hbm, gas, diffused, sems):
+    fields, extent_x, extent_y, extent_z = gas.shape
+    across_y = extent_y // TILE_Y
+    across_z = extent_z // TILE_Z
+    lane = lax.broadcasted_iota(jnp.int32, (extent_y, extent_z), 1)
+    line = lax.broadcasted_iota(jnp.int32, (extent_y, extent_z), 0)
+    copy = pltpu.make_async_copy(gas_hbm, gas, sems.at[fields])
+    copy.start()
+    copy.wait()
+
+    def sent(f):
+        return pltpu.make_async_copy(diffused.at[f], diffused_hbm.at[f], sems.at[f])
+
+    def per_field(f, carry):
+        for x in range(extent_x):
+            centre = gas[f, x]
+            beside = jnp.where(line == 0, 0.0, roll(centre, 1, 0))
+            beside += jnp.where(line == extent_y - 1, 0.0, roll(centre, -1, 0))
+            beside += jnp.where(lane == 0, 0.0, roll(centre, 1, 1))
+            beside += jnp.where(lane == extent_z - 1, 0.0, roll(centre, -1, 1))
+            if x > 0:
+                beside += gas[f, x - 1]
+            if x < extent_x - 1:
+                beside += gas[f, x + 1]
+            diffused[f, x * extent_y : (x + 1) * extent_y, :] = centre + DIFFUSION * (beside - 6.0 * centre)
+        sent(f).start()
+        return carry
+
+    lax.fori_loop(0, fields, per_field, 0)
 
     def per_a(a, carry):
         for f in range(FLOWS):
@@ -136,21 +169,18 @@
         return carry
 
     lax.fori_loop(0, extent_x // TILE_X, per_a, 0)
-    copy = pltpu.make_async_copy(table, table_hbm, sem)
-    copy.start()
-    copy.wait()
+    for f in range(fields):
+        sent(f).wait()
 
 
 def update_kernel(
-    message, table_hbm, result_hbm, source, ids_vmem, ids_smem, products, table, result, sems, *, rows, capacity
+    message, table, result_hbm, source, ids_vmem, ids_smem, products, result, sems, *, rows, capacity
 ):
     devices = message.shape[0] // rows
     group = SUB * rows
-    fetch = pltpu.make_async_copy(table_hbm, table, sems.at[0])
-    fetch.start()
     for g in range(devices // SUB):
         ids_vmem[g * SUB : (g + 1) * SUB, :] = message[pl.ds(g * group + rows - 1, SUB, stride=rows), :].astype(jnp.int32)
-    copy = pltpu.make_async_copy(ids_vmem, ids_smem, sems.at[1])
+    copy = pltpu.make_async_copy(ids_vmem, ids_smem, sems.at[0])
     copy.start()
     corner = lax.broadcasted_iota(jnp.int32, (SUB, LANES), 0)
     high = [(corner & bit) != 0 for bit in (4, 2, 1)]
@@ -161,11 +191,10 @@
     )
     row = corner
     copy.wait()
-    fetch.wait()
 
     def returned(g):
         place = pl.ds(pl.multiple_of(g * SUB * capacity * FLOWS, SUB), SUB * capacity * FLOWS)
-        return pltpu.make_async_copy(result.at[place], result_hbm.at[place], sems.at[2 + g])
+        return pltpu.make_async_copy(result.at[place], result_hbm.at[place], sems.at[1 + g])
 
     def per_group(g, carry):
         part = message.at[pl.ds(pl.multiple_of(g * group, SUB), group)]
@@ -242,34 +271,18 @@
     return jnp.maximum(0.0, 1.0 - jnp.abs(position - cell))
 
 
-def diffuse_kernel(gas, from_x0, from_x1, from_y0, from_y1, diffused):
-    fields, extent_x, extent_y, extent_z = gas.shape
-    lane = lax.broadcasted_iota(jnp.int32, (extent_y, extent_z), 1)
-    line = lax.broadcasted_iota(jnp.int32, (extent_y, extent_z), 0)
-
-    def per_field(f, carry):
-        for x in range(extent_x):
-            centre = gas[f, x]
-            before = from_x0[f] if x == 0 else gas[f, x - 1]
-            after = from_x1[f] if x == extent_x - 1 else gas[f, x + 1]
-            beside = before + after
-            beside += jnp.where(line == 0, from_y0[f, x : x + 1, :], roll(centre, 1, 0))
-            beside += jnp.where(line == extent_y - 1, from_y1[f, x : x + 1, :], roll(centre, -1, 0))
-            beside += jnp.where(lane == 0, 0.0, roll(centre, 1, 1))
-            beside += jnp.where(lane == extent_z - 1, 0.0, roll(centre, -1, 1))
-            diffused[f, x] = centre + DIFFUSION * (beside - 6.0 * centre)
-        return carry
-
-    lax.fori_loop(0, fields, per_field, 0)
-
-
-def deposit_kernel(ids_vmem, source, diffused, gas_next, total, ids, sem, *, capacity):
-    fields, extent_x, extent_y, extent_z = diffused.shape
+def deposit_kernel(
+    ids_vmem, source, diffused, from_x0, from_x1, from_y0, from_y1, gas_next, total, ids, work, sems, *, capacity
+):
+    fields, extent_x, extent_z = from_y0.shape
+    extent_y = from_x0.shape[1]
     across_y = extent_y // TILE_Y
     across_z = extent_z // TILE_Z
     blocks = source.shape[0] // SUB
-    copy = pltpu.make_async_copy(ids_vmem, ids, sem)
+    copy = pltpu.make_async_copy(ids_vmem, ids, sems.at[0])
     copy.start()
+    fetch = pltpu.make_async_copy(diffused, work, sems.at[1])
+    fetch.start()
     total[...] = jnp.zeros(total.shape, total.dtype)
     row = lax.broadcasted_iota(jnp.int32, (SUB, LANES), 0)
     along_z = row.astype(jnp.float32)
@@ -298,7 +311,7 @@
         sums = lax.dot_general(left, right, (((1,), (1,)), ((), ())), preferred_element_type=jnp.float32)
         return pl.multiple_of(tile * SUB, SUB), sums[:, :LANES] + sums[:, LANES:]
 
-    unroll = 4
+    unroll = 16
 
     def per_step(step, carry):
         made = [one(step * unroll + n) for n in range(unroll)]
@@ -308,13 +321,29 @@
 
     lax.fori_loop(0, blocks // unroll, per_step, 0)
 
+    fetch.wait()
+    last_x = (extent_x - 1) * extent_y
+    for f in range(fields):
+        work[f, 0:extent_y, :] += DIFFUSION * from_x0[f]
+        work[f, last_x : last_x + extent_y, :] += DIFFUSION * from_x1[f]
+        for h in range(extent_z // LANES):
+            lanes = slice(h * LANES, (h + 1) * LANES)
+            for line, face in ((0, from_y0), (extent_y - 1, from_y1)):
+                for x in range(extent_x):
+                    spot = x * extent_y + line
+                    work[f, spot : spot + 1, lanes] += DIFFUSION * face[f, x : x + 1, lanes]
+
+    def sent(a):
+        place = pl.ds(pl.multiple_of(a * TILE_X * extent_y, SUB), TILE_X * extent_y)
+        return pltpu.make_async_copy(work.at[:, place], gas_next.at[:, place], sems.at[2 + a])
+
     def per_a(a, carry):
+        held = work.at[:, pl.ds(pl.multiple_of(a * TILE_X * extent_y, SUB), TILE_X * extent_y)]
         for b in range(across_y):
             for h in range(extent_z // LANES):
                 start = ((a * across_y + b) * across_z + h * GRANULES) * SUB
                 part = total.at[pl.ds(pl.multiple_of(start, SUB), GRANULES * SUB)]
                 lanes = slice(h * LANES, (h + 1) * LANES)
-                lines = slice(b * TILE_Y, (b + 1) * TILE_Y)
                 for f in range(FLOWS):
                     pair = [
                         part[pl.ds(n * SUB * SUB + f, SUB, stride=SUB), :]
@@ -324,15 +353,19 @@
                     pair = [x * (1.0 / CELL_MASS) for x in exchange(*pair)]
                     for u in range(TILE_X):
                         piece = pair[u // 2][(u % 2) * TILE_Y : (u % 2 + 1) * TILE_Y]
-                        x = a * TILE_X + u
+                        spot = u * extent_y + b * TILE_Y
+                        lines = slice(spot, spot + TILE_Y)
                         if f < 3:
-                            gas_next[f, x, lines, lanes] = diffused[f, x, lines, lanes] + piece
+                            held[f, lines, lanes] += piece
                         else:
-                            gas_next[3, x, lines, lanes] = diffused[3, x, lines, lanes] - LATENT_HEAT * piece
-                            gas_next[4, x, lines, lanes] = diffused[4, x, lines, lanes] + piece
+                            held[3, lines, lanes] -= LATENT_HEAT * piece
+                            held[4, lines, lanes] += piece
+        sent(a).start()
         return carry
 
     lax.fori_loop(0, extent_x // TILE_X, per_a, 0)
+    for a in range(extent_x // TILE_X):
+        sent(a).wait()
 
 
 def unpack_kernel(result, speed, mass, sems):
@@ -351,7 +384,7 @@
     return [pl.BlockSpec(memory_space=space) for space in spaces]
 
 
-def call(kernel, name, out_shape, scratch=(), flops=0, moved=0, ins=None, outs=None):
+def call(kernel, out_shape, scratch=(), flops=0, moved=0, ins=None, outs=None):
     extra = {}
     if ins is not None:
         extra["in_specs"] = specs(ins)
@@ -365,7 +398,6 @@
         kernel,
         out_shape=out_shape,
         scratch_shapes=scratch,
-        name=name,
         cost_estimate=pl.CostEstimate(flops=flops, bytes_accessed=moved, transcendentals=0),
         compiler_params=pltpu.CompilerParams(vmem_limit_bytes=32 * 1024 * 1024),
         **extra,
@@ -382,7 +414,7 @@
     return with_spaces
 
 
-def shards(gas_state, parcel_speed, parcel_mass, offsets, cell_base, block_tile, block_count):
+def step(gas_state, parcel_speed, parcel_mass, offsets, cell_base, block_tile, block_count):
     fields, extent_x, extent_y, extent_z = gas_state.shape
     devices, capacity = block_tile.shape[2:]
     rows = 10 * capacity + 1
@@ -402,7 +434,6 @@
     dma = pltpu.SemaphoreType.DMA
     message = call(
         functools.partial(pack_kernel, rows=rows, capacity=capacity),
-        "pack",
         shape(devices * rows, LANES),
         scratch=[
             vmem((devices * vector, LANES), f32),
@@ -429,14 +460,11 @@
     message = message.reshape(devices * rows, LANES)
 
     face = shape(fields, extent_x, extent_z)
-    table, face_x0, face_x1, face_y0, face_y1 = call(
-        table_kernel,
-        "table",
-        (shape(FLOWS, tiles, LANES), shape(fields, extent_y, extent_z), shape(fields, extent_y, extent_z), face, face),
-        scratch=[vmem((FLOWS, tiles, LANES), f32), dma(())],
-        flops=10**7,
-        ins=[vmem],
-        outs=[hbm] + [vmem] * 4,
+    side = shape(fields, extent_y, extent_z)
+    whole = vmem(gas_state.shape, f32)
+    flat = (fields, extent_x * extent_y, extent_z)
+    face_x0, face_x1, face_y0, face_y1 = call(
+        faces_kernel, (side, side, face, face), scratch=[whole, dma(())], ins=[hbm], outs=[vmem] * 4
     )(gas_state)
 
     def shifted(value, axis, step):
@@ -444,28 +472,30 @@
         pairs = [(i, i + step) for i in range(count) if 0 <= i + step < count]
         return lax.ppermute(value, axis, pairs)
 
-    diffused = call(diffuse_kernel, "diffuse", shape(*gas_state.shape), flops=10**7)(
-        gas_state,
-        shifted(face_x1, "gx", 1),
-        shifted(face_x0, "gx", -1),
-        shifted(face_y1, "yz", 1),
-        shifted(face_y0, "yz", -1),
-    )
+    halo = (
+        shifted(face_x1, "gx", 1), shifted(face_x0, "gx", -1), shifted(face_y1, "yz", 1), shifted(face_y0, "yz", -1)
+    )
+    table, diffused = call(
+        local_kernel,
+        (shape(FLOWS, tiles, LANES), shape(*flat)),
+        scratch=[whole, vmem(flat, f32), dma((fields + 1,))],
+        flops=10**7,
+        ins=[hbm],
+        outs=[vmem, hbm],
+    )(gas_state)
     message, table, diffused = lax.optimization_barrier((message, table, diffused))
 
     result, source, ids = call(
         functools.partial(update_kernel, rows=rows, capacity=capacity),
-        "update",
         (shape(blocks * FLOWS, LANES), shape(blocks * SUB, LANES), shape(devices, LANES, dtype=i32)),
         scratch=[
             pltpu.SMEM((devices, LANES), i32),
             vmem((FLOWS * SUB * SUB, LANES), f32),
-            vmem((FLOWS, tiles, LANES), f32),
             vmem((blocks * FLOWS, LANES), f32),
-            dma((2 + devices // SUB,)),
+            dma((1 + devices // SUB,)),
         ],
         flops=10**7,
-        ins=[vmem, hbm],
+        ins=[vmem, vmem],
         outs=[hbm, vmem, vmem],
     )(message, table)
     result = lax.all_to_all(
@@ -473,21 +503,26 @@
     )
     gas_next = call(
         functools.partial(deposit_kernel, capacity=capacity),
-        "deposit",
-        shape(*gas_state.shape),
-        scratch=[vmem((tiles * SUB, LANES), f32), pltpu.SMEM((devices, LANES), i32), dma(())],
+        shape(*flat),
+        scratch=[
+            vmem((tiles * SUB, LANES), f32),
+            pltpu.SMEM((devices, LANES), i32),
+            vmem(flat, f32),
+            dma((2 + extent_x // TILE_X,)),
+        ],
         flops=3 * 10**7,
-    )(ids, source, diffused)
+        ins=[vmem, vmem, hbm] + [vmem] * 4,
+        outs=[hbm],
+    )(ids, source, diffused, *halo)
     speed_next, mass_next = call(
         unpack_kernel,
-        "unpack",
         (shape(devices, vector, 1, LANES), shape(devices, capacity, 1, LANES)),
         scratch=[dma((2,))],
         ins=[vmem],
         outs=[hbm, hbm],
     )(result)
     speed_next = speed_next.reshape(devices, 3, capacity, LANES).transpose(0, 2, 1, 3)
-    return gas_next, speed_next.reshape(parcel_speed.shape), mass_next.reshape(parcel_mass.shape)
+    return gas_next.reshape(gas_state.shape), speed_next.reshape(parcel_speed.shape), mass_next.reshape(parcel_mass.shape)
 
 
 def solution(mesh):
@@ -505,4 +540,4 @@
         P("gx", "yz", None, None, None, None),
         P("gx", "yz", None, None, None),
     )
-    return jax.shard_map(shards, mesh=mesh, in_specs=in_specs, out_specs=out_specs, check_vma=False)
+    return jax.shard_map(step, mesh=mesh, in_specs=in_specs, out_specs=out_specs, check_vma=False)

time: 49.5 us -> 58.7 us (1.19)
  the two profiles are of different devices: /device:TPU:0 before, /device:TPU:6 now
where the time goes in v4:
time: 58.7 us; the launch traced here: 58.3 us
  starting transfers between devices  21.8 us (37%)
  waiting for transfers between devices  18.9 us (32%)
  Pallas kernels  16.9 us (29%)
  between operations  0.74 us (1%)
    pallas_call x6, Pallas kernels, with_spaces(): return called(*values)  16.9 us
    all_to_all x1, waiting for transfers between devices, step(): lax.all_to_all(message.reshape(devices, rows, 1, LANES), BOTH, split_axis...  14.1 us
    ppermute x4, starting transfers between devices, shifted(): return lax.ppermute(value, axis, pairs)  11.4 us
    all_to_all x1, starting transfers between devices, step(): lax.all_to_all(message.reshape(devices, rows, 1, LANES), BOTH, split_axis...  6.08 us
    ppermute x4, waiting for transfers between devices, shifted(): return lax.ppermute(value, axis, pairs)  4.79 us
    all_to_all x1, starting transfers between devices, step(): lax.all_to_all(result.reshape(devices, capacity * FLOWS, 1, LANES), BOTH,...  4.3 us
  transfers between devices with their start and end apart: 6, of which 3 were waited for; matrix products, arithmetic and copies ran while one was open for 0% of the time, Pallas kernels for 19%

profile of v4, /device:TPU:6, one launch (start us, length us, event | category | flops | bytes accessed | tf_op | source)
XLA Modules:
  0.0 58.3 jit_solution(624909080427751624)
XLA Ops:
  0.6 2.0 %shard_map.94 = f32[1312,128]{1,0:T(8,128)} custom-call(f32[384,128]{1,0:T(8,128)} %bitcast.34, f32[128,128]{1,0:T(8,128)} %bitcast.37, f32[384,128]{1,0:T(8,128)} %bitcast.35, s32[384,128]{1,0:T(8,128)} %bitcast.36, s32[4,32]{1,0:T(4,128)} %bitcast.38, s32[1,32]{1,0:T(1,128)} %bitcast.39), custom_call_target="tpu_custom_call" | custom-call | tf_op jit(solution)/shard_map/pallas_call | solution.py:412
  2.7 6.1 %all-to-all-start = ((f32[32,41,1,128]{3,2,1,0:T(1,128)}), f32[32,41,1,128]{3,2,1,0:T(1,128)S(1)}, u32[]{:S(2)}, u32[]{:S(2)}) async-start(f32[32,41,1,128]{3,2,1,0:T(1,128)} %bitcast.31), calls=%async_computation | async-start | bytes 1343488 | tf_op jit(solution)/shard_map/all_to_all | solution.py:459
  8.8 3.5 %shard_map.95 = (f32[4,512,128]{2,1,0:T(8,128)S(1)}, f32[5,256,256]{2,1,0:T(8,128)}) custom-call(f32[5,16,16,256]{3,2,1,0:T(8,128)} %gas_hbm.3), custom_call_target="tpu_custom_call" | custom-call | flops 10000000 | tf_op jit(solution)/shard_map/pallas_call | solution.py:412
  12.3 14.1 %all-to-all-done = f32[32,41,1,128]{3,2,1,0:T(1,128)S(1)} async-done(((f32[32,41,1,128]{3,2,1,0:T(1,128)}), f32[32,41,1,128]{3,2,1,0:T(1,128)S(1)}, u32[]{:S(2)}, u32[]{:S(2)}) %all-to-all-start) | async-done | bytes 671776 | tf_op jit(solution)/shard_map/all_to_all | solution.py:459
  26.4 3.0 %shard_map.96 = (f32[512,128]{1,0:T(8,128)}, f32[1024,128]{1,0:T(8,128)S(1)}, s32[32,128]{1,0:T(8,128)S(1)}) custom-call(f32[1312,128]{1,0:T(8,128)S(1)} %bitcast.30, f32[4,512,128]{2,1,0:T(8,128)S(1)} %get-tuple-element.20.table), custom_call_target="tpu_custom_call" | custom-call | flops 10000000 | tf_op jit(solution)/shard_map/pallas_call | solution.py:412
  29.4 4.3 %all-to-all-start.1 = ((f32[32,16,1,128]{3,2,1,0:T(1,128)}), f32[32,16,1,128]{3,2,1,0:T(1,128)S(1)}, u32[]{:S(2)}, u32[]{:S(2)}) async-start(f32[32,16,1,128]{3,2,1,0:T(1,128)} %bitcast.33), calls=%async_computation.1 | async-start | bytes 524288 | tf_op jit(solution)/shard_map/all_to_all | solution.py:501
  33.7 1.4 %shard_map.97 = (f32[5,16,256]{2,1,0:T(8,128)S(1)}, f32[5,16,256]{2,1,0:T(8,128)S(1)}, f32[5,16,256]{2,1,0:T(8,128)S(1)}, f32[5,16,256]{2,1,0:T(8,128)S(1)}) custom-call(f32[5,16,16,256]{3,2,1,0:T(8,128)} %gas_hbm.3), custom_call_target="tpu_custom_call" | custom-call | tf_op jit(solution)/shard_map/pallas_call | solution.py:412
  35.1 2.0 %collective-permute-start = (f32[5,16,256]{2,1,0:T(8,128)S(1)}, f32[5,16,256]{2,1,0:T(8,128)S(1)}, u32[]{:S(2)}, u32[]{:S(2)}) collective-permute-start(f32[5,16,256]{2,1,0:T(8,128)S(1)} %get-tuple-element.24), channel_id=1, source_target_pairs={{0,8},{8,16},{16,24},{1,9},{9,17},{17,25},{2,10},{10,18},{18,26},{... | collective-permute-start | bytes 245768 | tf_op jit(solution)/shard_map/ppermute | solution.py:473
  37.1 3.5 %collective-permute-start.1 = (f32[5,16,256]{2,1,0:T(8,128)S(1)}, f32[5,16,256]{2,1,0:T(8,128)S(1)}, u32[]{:S(2)}, u32[]{:S(2)}) collective-permute-start(f32[5,16,256]{2,1,0:T(8,128)S(1)} %get-tuple-element.25), channel_id=1, source_target_pairs={{8,0},{16,8},{24,16},{9,1},{17,9},{25,17},{10,2},{18,10},{26,18},{... | collective-permute-start | bytes 245768 | tf_op jit(solution)/shard_map/ppermute | solution.py:473
  40.7 3.4 %collective-permute-start.2 = (f32[5,16,256]{2,1,0:T(8,128)S(1)}, f32[5,16,256]{2,1,0:T(8,128)S(1)}, u32[]{:S(2)}, u32[]{:S(2)}) collective-permute-start(f32[5,16,256]{2,1,0:T(8,128)S(1)} %get-tuple-element.26), channel_id=1, source_target_pairs={{0,1},{1,2},{2,3},{3,4},{4,5},{5,6},{6,7},{8,9},{9,10},{10,11},{11... | collective-permute-start | bytes 245768 | tf_op jit(solution)/shard_map/ppermute | solution.py:473
  44.1 2.4 %collective-permute-start.3 = (f32[5,16,256]{2,1,0:T(8,128)S(1)}, f32[5,16,256]{2,1,0:T(8,128)S(1)}, u32[]{:S(2)}, u32[]{:S(2)}) collective-permute-start(f32[5,16,256]{2,1,0:T(8,128)S(1)} %get-tuple-element.27), channel_id=1, source_target_pairs={{1,0},{2,1},{3,2},{4,3},{5,4},{6,5},{7,6},{9,8},{10,9},{11,10},{12... | collective-permute-start | bytes 245768 | tf_op jit(solution)/shard_map/ppermute | solution.py:473
  46.5 0.0 collective-permute-done.from_x0
  46.5 0.0 collective-permute-done.1.from_x1
  46.5 0.5 collective-permute-done.2.from_y0
  47.0 4.3 %collective-permute-done.3.from_y1 = f32[5,16,256]{2,1,0:T(8,128)S(1)} collective-permute-done((f32[5,16,256]{2,1,0:T(8,128)S(1)}, f32[5,16,256]{2,1,0:T(8,128)S(1)}, u32[]{:S(2)}, u32[]{:S(2)}) %collective-permute-start.3) | collective-permute-done | bytes 81952 | tf_op jit(solution)/shard_map/ppermute | solution.py:473
  51.3 6.2 %shard_map.98 = f32[5,256,256]{2,1,0:T(8,128)} custom-call(s32[32,128]{1,0:T(8,128)S(1)} %get-tuple-element.21.ids_vmem, f32[1024,128]{1,0:T(8,128)S(1)} %get-tuple-element.22.source, f32[5,256,256]{2,1,0:T(8,128)} %get-tuple-element.23.diffused, f32[5,16,256]{2,1,0:T(8,128)S(1)} %collective-permute-done.from_x0, ...), custom_call_target="tpu_custom_call" | custom-call | flops 30000000 | tf_op jit(solution)/shard_map/pallas_call | solution.py:412
  57.5 0.0 all-to-all-done.1.result
  57.5 0.7 %shard_map.99 = (f32[32,12,1,128]{3,2,1,0:T(1,128)}, f32[32,4,1,128]{3,2,1,0:T(1,128)}) custom-call(f32[32,16,1,128]{3,2,1,0:T(1,128)S(1)} %all-to-all-done.1.result), custom_call_target="tpu_custom_call" | custom-call | tf_op jit(solution)/shard_map/pallas_call | solution.py:412
Async XLA Ops:
  2.7 23.7 %all-to-all-start = ((f32[32,41,1,128]{3,2,1,0:T(1,128)}), f32[32,41,1,128]{3,2,1,0:T(1,128)S(1)}, u32[]{:S(2)}, u32[]{:S(2)}) async-start(f32[32,41,1,128]{3,2,1,0:T(1,128)} %bitcast.31), calls=%async_computation | async-start | bytes 1343488 | tf_op jit(solution)/shard_map/all_to_all | solution.py:459
  29.4 28.2 %all-to-all-start.1 = ((f32[32,16,1,128]{3,2,1,0:T(1,128)}), f32[32,16,1,128]{3,2,1,0:T(1,128)S(1)}, u32[]{:S(2)}, u32[]{:S(2)}) async-start(f32[32,16,1,128]{3,2,1,0:T(1,128)} %bitcast.33), calls=%async_computation.1 | async-start | bytes 524288 | tf_op jit(solution)/shard_map/all_to_all | solution.py:501
  35.1 11.4 %collective-permute-start = (f32[5,16,256]{2,1,0:T(8,128)S(1)}, f32[5,16,256]{2,1,0:T(8,128)S(1)}, u32[]{:S(2)}, u32[]{:S(2)}) collective-permute-start(f32[5,16,256]{2,1,0:T(8,128)S(1)} %get-tuple-element.24), channel_id=1, source_target_pairs={{0,8},{8,16},{16,24},{1,9},{9,17},{17,25},{2,10},{10,18},{18,26},{... | collective-permute-start | bytes 245768 | tf_op jit(solution)/shard_map/ppermute | solution.py:473
  37.1 9.4 %collective-permute-start.1 = (f32[5,16,256]{2,1,0:T(8,128)S(1)}, f32[5,16,256]{2,1,0:T(8,128)S(1)}, u32[]{:S(2)}, u32[]{:S(2)}) collective-permute-start(f32[5,16,256]{2,1,0:T(8,128)S(1)} %get-tuple-element.25), channel_id=1, source_target_pairs={{8,0},{16,8},{24,16},{9,1},{17,9},{25,17},{10,2},{18,10},{26,18},{... | collective-permute-start | bytes 245768 | tf_op jit(solution)/shard_map/ppermute | solution.py:473
  40.7 6.3 %collective-permute-start.2 = (f32[5,16,256]{2,1,0:T(8,128)S(1)}, f32[5,16,256]{2,1,0:T(8,128)S(1)}, u32[]{:S(2)}, u32[]{:S(2)}) collective-permute-start(f32[5,16,256]{2,1,0:T(8,128)S(1)} %get-tuple-element.26), channel_id=1, source_target_pairs={{0,1},{1,2},{2,3},{3,4},{4,5},{5,6},{6,7},{8,9},{9,10},{10,11},{11... | collective-permute-start | bytes 245768 | tf_op jit(solution)/shard_map/ppermute | solution.py:473
  44.1 7.2 %collective-permute-start.3 = (f32[5,16,256]{2,1,0:T(8,128)S(1)}, f32[5,16,256]{2,1,0:T(8,128)S(1)}, u32[]{:S(2)}, u32[]{:S(2)}) collective-permute-start(f32[5,16,256]{2,1,0:T(8,128)S(1)} %get-tuple-element.27), channel_id=1, source_target_pairs={{1,0},{2,1},{3,2},{4,3},{5,4},{6,5},{7,6},{9,8},{10,9},{11,10},{12... | collective-permute-start | bytes 245768 | tf_op jit(solution)/shard_map/ppermute | solution.py:473

commit v5 on v4

--- a/solution.py
+++ b/solution.py
@@ -21,7 +21,7 @@
 SUB = 8
 GRANULES = LANES // TILE_Z
 FLOWS = 4
-BOTH = ("gx", "yz")
+BOTH = ("yz", "gx")
 
 
 def roll(x, shift, axis):
@@ -52,13 +52,13 @@
 
 def pack_kernel(
     speed, mass, offsets, cells, tile_ids, counts, message,
-    speed_v, mass_v, offsets_v, cells_v, tile_ids_v, counts_v, ids_v, message_v, sems, *, rows, capacity
+    speed_v, mass_v, offsets_v, cells_v, tile_ids_v, counts_v, ids_v, message_v, sems, *, rows, capacity, parts
 ):
-    owners = tile_ids.shape[1]
+    across_i = speed.shape[0]
     vector = 3 * capacity
+    across_j = speed.shape[1] // vector
+    each = across_j // parts
     sources = ((speed, speed_v, vector), (offsets, offsets_v, vector), (cells, cells_v, vector), (mass, mass_v, capacity))
-    parts = 2
-    each = owners // parts
     small = [
         pltpu.make_async_copy(tile_ids, tile_ids_v, sems.at[0]),
         pltpu.make_async_copy(counts, counts_v, sems.at[1]),
@@ -70,39 +70,32 @@
         taken.append([])
         for n, (source, held, count) in enumerate(sources):
             place = pl.ds(part * each * count, each * count)
-            copy = pltpu.make_async_copy(source.at[place], held.at[place], sems.at[2 + part * 4 + n])
+            copy = pltpu.make_async_copy(source.at[:, place], held.at[:, place], sems.at[2 + part * 5 + n])
             copy.start()
             taken[-1].append(copy)
     for copy in small:
         copy.wait()
     slot = lax.broadcasted_iota(jnp.int32, tile_ids_v.shape, 0)
     ids = jnp.where(slot < counts_v[...], tile_ids_v[...], -1).astype(jnp.float32)
-    ids_v[...] = jnp.concatenate([ids, jnp.zeros((LANES - capacity, owners), jnp.float32)], axis=0).T
-
-    def per_group(g, carry):
-        def at(held, count):
-            return held.at[pl.ds(pl.multiple_of(g * SUB * count, SUB), SUB * count)]
-
-        out = at(message_v, rows)
-        speed_g, offsets_g, cells_g, mass_g = (at(held, count) for _, held, count in sources)
-        ids_g = at(ids_v, 1)
-        for i in range(SUB):
-            base = i * rows
-            place = slice(i * vector, (i + 1) * vector)
-            out[base : base + vector, :] = speed_g[place, :]
-            out[base + vector : base + 2 * vector, :] = offsets_g[place, :]
-            out[base + 2 * vector : base + 3 * vector, :] = cells_g[place, :].astype(jnp.float32)
-            out[base + 3 * vector : base + 3 * vector + capacity, :] = mass_g[i * capacity : (i + 1) * capacity, :]
-            out[base + rows - 1 : base + rows, :] = ids_g[i : i + 1, :]
-        return carry
+    ids_v[...] = jnp.concatenate([ids, jnp.zeros((LANES - capacity, ids.shape[1]), jnp.float32)], axis=0).T
 
     sent = []
     for part in range(parts):
         for copy in taken[part]:
             copy.wait()
-        lax.fori_loop(part * each // SUB, (part + 1) * each // SUB, per_group, 0)
-        place = pl.ds(part * each * rows, each * rows)
-        copy = pltpu.make_async_copy(message_v.at[place], message.at[place], sems.at[2 + parts * 4 + part])
+        for j in range(part * each, (part + 1) * each):
+            for i in range(across_i):
+                base = (j * across_i + i) * rows
+                place = slice(j * vector, (j + 1) * vector)
+                message_v[base : base + vector, :] = speed_v[i, place, :]
+                message_v[base + vector : base + 2 * vector, :] = offsets_v[i, place, :]
+                message_v[base + 2 * vector : base + 3 * vector, :] = cells_v[i, place, :].astype(jnp.float32)
+                base += 3 * vector
+                message_v[base : base + capacity, :] = mass_v[i, j * capacity : (j + 1) * capacity, :]
+                owner = i * across_j + j
+                message_v[base + capacity : base + capacity + 1, :] = ids_v[owner : owner + 1, :]
+        place = pl.ds(part * each * across_i * rows, each * across_i * rows)
+        copy = pltpu.make_async_copy(message_v.at[place], message.at[place], sems.at[2 + part * 5 + 4])
         copy.start()
         sent.append(copy)
     for copy in sent:
@@ -174,14 +167,12 @@
 
 
 def update_kernel(
-    message, table, result_hbm, source, ids_vmem, ids_smem, products, result, sems, *, rows, capacity
+    message, table, result_hbm, source, ids_vmem, products, result, sems, *, rows, capacity
 ):
     devices = message.shape[0] // rows
     group = SUB * rows
     for g in range(devices // SUB):
         ids_vmem[g * SUB : (g + 1) * SUB, :] = message[pl.ds(g * group + rows - 1, SUB, stride=rows), :].astype(jnp.int32)
-    copy = pltpu.make_async_copy(ids_vmem, ids_smem, sems.at[0])
-    copy.start()
     corner = lax.broadcasted_iota(jnp.int32, (SUB, LANES), 0)
     high = [(corner & bit) != 0 for bit in (4, 2, 1)]
     least = [jnp.where(h, 0.0, 1.0) for h in high]
@@ -190,20 +181,26 @@
         jnp.where(high[0], TILE_Y * TILE_Z, 0) + jnp.where(high[1], TILE_Z, 0) + jnp.where(high[2], 1, 0)
     )
     row = corner
-    copy.wait()
 
     def returned(g):
         place = pl.ds(pl.multiple_of(g * SUB * capacity * FLOWS, SUB), SUB * capacity * FLOWS)
-        return pltpu.make_async_copy(result.at[place], result_hbm.at[place], sems.at[1 + g])
+        return pltpu.make_async_copy(result.at[place], result_hbm.at[place], sems.at[g])
 
     def per_group(g, carry):
+        numbers = ids_vmem[pl.ds(pl.multiple_of(g * SUB, SUB), SUB), :]
         part = message.at[pl.ds(pl.multiple_of(g * group, SUB), group)]
         for step in range(SUB // 2):
+
+            def both(field):
+                starts = [(2 * step + n) * rows + field * capacity for n in range(2)]
+                return jnp.concatenate([part[start : start + capacity, :] for start in starts], axis=0)
+
+            first = ((both(6) * TILE_Y + both(7)) * TILE_Z + both(8)).astype(jnp.int32)
             alive = jnp.zeros((SUB, LANES), jnp.int32)
             for j in range(2 * capacity):
                 i, k = 2 * step + j // capacity, j % capacity
                 base = i * rows
-                tile = ids_smem[g * SUB + i, k]
+                tile = numbers[i, k]
                 alive = jnp.where(row == j, tile, alive)
                 safe = jnp.maximum(tile, 0)
                 weight = None
@@ -212,10 +209,7 @@
                     fraction = part[start : start + 1, :]
                     along = least[dim] + slope[dim] * fraction
                     weight = along if weight is None else weight * along
-                starts = [base + (6 + dim) * capacity + k for dim in range(3)]
-                cell = [part[start : start + 1, :] for start in starts]
-                first = (cell[0] * TILE_Y + cell[1]) * TILE_Z + cell[2]
-                index = first.astype(jnp.int32) + shift
+                index = jnp.broadcast_to(first[j : j + 1], (SUB, LANES)) + shift
                 for f in range(FLOWS):
                     held = jnp.broadcast_to(table[f, pl.ds(safe, 1), :], (SUB, LANES))
                     found = jnp.take_along_axis(held, index, axis=1, mode="promise_in_bounds")
@@ -227,10 +221,6 @@
                 for c in range(1, SUB):
                     total = total + products[pl.ds(f * SUB * SUB + c, SUB, stride=SUB), :]
                 sampled.append(total)
-
-            def both(field):
-                starts = [(2 * step + n) * rows + field * capacity for n in range(2)]
-                return jnp.concatenate([part[start : start + capacity, :] for start in starts], axis=0)
 
             mass_old = both(9)
             radius = jnp.exp(jnp.log(mass_old) * (1.0 / 3.0))
@@ -369,11 +359,11 @@
 
 
 def unpack_kernel(result, speed, mass, sems):
-    vector = speed.shape[1]
-    copies = [
-        pltpu.make_async_copy(result.at[:, :vector], speed, sems.at[0]),
-        pltpu.make_async_copy(result.at[:, vector:], mass, sems.at[1]),
-    ]
+    vector = speed.shape[2]
+    copies = []
+    for i in range(speed.shape[0]):
+        copies.append(pltpu.make_async_copy(result.at[:, i, :vector], speed.at[i], sems.at[2 * i]))
+        copies.append(pltpu.make_async_copy(result.at[:, i, vector:], mass.at[i], sems.at[2 * i + 1]))
     for copy in copies:
         copy.start()
     for copy in copies:
@@ -424,33 +414,36 @@
     def shape(*dims, dtype=f32):
         return jax.ShapeDtypeStruct(dims, dtype)
 
-    def by_component(value):
-        return value[0, 0].transpose(0, 2, 1, 3).reshape(devices * 3 * capacity, LANES)
-
     vector = 3 * capacity
     blocks = devices * capacity
+    across_i, across_j = lax.axis_size("gx"), lax.axis_size("yz")
+    parts = max(1, across_j // 2)
     i32 = jnp.int32
     hbm, vmem = pltpu.HBM, pltpu.VMEM
     dma = pltpu.SemaphoreType.DMA
+
+    def by_component(value):
+        return value[0, 0].transpose(0, 2, 1, 3).reshape(across_i, across_j * vector, LANES)
+
     message = call(
-        functools.partial(pack_kernel, rows=rows, capacity=capacity),
+        functools.partial(pack_kernel, rows=rows, capacity=capacity, parts=parts),
         shape(devices * rows, LANES),
         scratch=[
-            vmem((devices * vector, LANES), f32),
-            vmem((blocks, LANES), f32),
-            vmem((devices * vector, LANES), f32),
-            vmem((devices * vector, LANES), i32),
+            vmem((across_i, across_j * vector, LANES), f32),
+            vmem((across_i, across_j * capacity, LANES), f32),
+            vmem((across_i, across_j * vector, LANES), f32),
+            vmem((across_i, across_j * vector, LANES), i32),
             vmem((capacity, devices), i32),
             vmem((1, devices), i32),
             vmem((devices, LANES), f32),
             vmem((devices * rows, LANES), f32),
-            dma((12,)),
+            dma((2 + 5 * parts,)),
         ],
         ins=[hbm] * 6,
         outs=[hbm],
     )(
         by_component(parcel_speed),
-        parcel_mass.reshape(blocks, LANES),
+        parcel_mass.reshape(across_i, across_j * capacity, LANES),
         by_component(offsets),
         by_component(cell_base),
         block_tile[0, 0].T,
@@ -489,10 +482,9 @@
         functools.partial(update_kernel, rows=rows, capacity=capacity),
         (shape(blocks * FLOWS, LANES), shape(blocks * SUB, LANES), shape(devices, LANES, dtype=i32)),
         scratch=[
-            pltpu.SMEM((devices, LANES), i32),
             vmem((FLOWS * SUB * SUB, LANES), f32),
             vmem((blocks * FLOWS, LANES), f32),
-            dma((1 + devices // SUB,)),
+            dma((devices // SUB,)),
         ],
         flops=10**7,
         ins=[vmem, vmem],
@@ -516,11 +508,11 @@
     )(ids, source, diffused, *halo)
     speed_next, mass_next = call(
         unpack_kernel,
-        (shape(devices, vector, 1, LANES), shape(devices, capacity, 1, LANES)),
-        scratch=[dma((2,))],
+        (shape(across_i, across_j, vector, 1, LANES), shape(across_i, across_j, capacity, 1, LANES)),
+        scratch=[dma((2 * across_i,))],
         ins=[vmem],
         outs=[hbm, hbm],
-    )(result)
+    )(result.reshape(across_j, across_i, capacity * FLOWS, 1, LANES))
     speed_next = speed_next.reshape(devices, 3, capacity, LANES).transpose(0, 2, 1, 3)
     return gas_next.reshape(gas_state.shape), speed_next.reshape(parcel_speed.shape), mass_next.reshape(parcel_mass.shape)
 

time: 58.7 us -> 58.2 us (level)
  no operation moved by 1% of the time
where the time goes in v5:
time: 58.2 us; the launch traced here: 57.7 us
  starting transfers between devices  21.4 us (37%)
  waiting for transfers between devices  19.1 us (33%)
  Pallas kernels  16.6 us (29%)
  between operations  0.74 us (1%)
    pallas_call x6, Pallas kernels, with_spaces(): return called(*values)  16.6 us
    all_to_all x1, waiting for transfers between devices, step(): lax.all_to_all(message.reshape(devices, rows, 1, LANES), BOTH, split_axis...  14.3 us
    ppermute x4, starting transfers between devices, shifted(): return lax.ppermute(value, axis, pairs)  11.4 us
    all_to_all x1, starting transfers between devices, step(): lax.all_to_all(message.reshape(devices, rows, 1, LANES), BOTH, split_axis...  6.08 us
    ppermute x4, waiting for transfers between devices, shifted(): return lax.ppermute(value, axis, pairs)  4.74 us
    all_to_all x1, starting transfers between devices, step(): lax.all_to_all(result.reshape(devices, capacity * FLOWS, 1, LANES), BOTH,...  3.89 us
  transfers between devices with their start and end apart: 6, of which 3 were waited for; matrix products, arithmetic and copies ran while one was open for 0% of the time, Pallas kernels for 19%

profile of v5, /device:TPU:6, one launch (start us, length us, event | category | flops | bytes accessed | tf_op | source)
XLA Modules:
  0.0 57.7 jit_solution(14515358851465669934)
XLA Ops:
  0.6 2.0 %shard_map.94 = f32[1312,128]{1,0:T(8,128)} custom-call(f32[4,96,128]{2,1,0:T(8,128)} %bitcast.38, f32[4,32,128]{2,1,0:T(8,128)} %bitcast.41, f32[4,96,128]{2,1,0:T(8,128)} %bitcast.39, s32[4,96,128]{2,1,0:T(8,128)} %bitcast.40, s32[4,32]{1,0:T(4,128)} %bitcast.42, s32[1,32]{1,0:T(1,128)} %bitcast.43), custom_call_target="tpu_custom_call" | custom-call | tf_op jit(solution)/shard_map/pallas_call | solution.py:402
  2.6 6.1 %all-to-all-start = ((f32[32,41,1,128]{3,2,1,0:T(1,128)}), f32[32,41,1,128]{3,2,1,0:T(1,128)S(1)}, u32[]{:S(2)}, u32[]{:S(2)}) async-start(f32[32,41,1,128]{3,2,1,0:T(1,128)} %bitcast.35), calls=%async_computation | async-start | bytes 1343488 | tf_op jit(solution)/shard_map/all_to_all | solution.py:452
  8.7 3.5 %shard_map.95 = (f32[4,512,128]{2,1,0:T(8,128)S(1)}, f32[5,256,256]{2,1,0:T(8,128)}) custom-call(f32[5,16,16,256]{3,2,1,0:T(8,128)} %gas_hbm.3), custom_call_target="tpu_custom_call" | custom-call | flops 10000000 | tf_op jit(solution)/shard_map/pallas_call | solution.py:402
  12.2 14.3 %all-to-all-done = f32[32,41,1,128]{3,2,1,0:T(1,128)S(1)} async-done(((f32[32,41,1,128]{3,2,1,0:T(1,128)}), f32[32,41,1,128]{3,2,1,0:T(1,128)S(1)}, u32[]{:S(2)}, u32[]{:S(2)}) %all-to-all-start) | async-done | bytes 671776 | tf_op jit(solution)/shard_map/all_to_all | solution.py:452
  26.6 2.7 %shard_map.96 = (f32[512,128]{1,0:T(8,128)}, f32[1024,128]{1,0:T(8,128)S(1)}, s32[32,128]{1,0:T(8,128)S(1)}) custom-call(f32[1312,128]{1,0:T(8,128)S(1)} %bitcast.33, f32[4,512,128]{2,1,0:T(8,128)S(1)} %get-tuple-element.20.table), custom_call_target="tpu_custom_call" | custom-call | flops 10000000 | tf_op jit(solution)/shard_map/pallas_call | solution.py:402
  29.2 3.9 %all-to-all-start.1 = ((f32[32,16,1,128]{3,1,2,0:T(8,128)}), f32[32,16,1,128]{3,1,2,0:T(8,128)S(1)}, u32[]{:S(2)}, u32[]{:S(2)}) async-start(f32[32,16,1,128]{3,1,2,0:T(8,128)} %bitcast.37), calls=%async_computation.1 | async-start | bytes 524288 | tf_op jit(solution)/shard_map/all_to_all | solution.py:493
  33.2 1.4 %shard_map.97 = (f32[5,16,256]{2,1,0:T(8,128)S(1)}, f32[5,16,256]{2,1,0:T(8,128)S(1)}, f32[5,16,256]{2,1,0:T(8,128)S(1)}, f32[5,16,256]{2,1,0:T(8,128)S(1)}) custom-call(f32[5,16,16,256]{3,2,1,0:T(8,128)} %gas_hbm.3), custom_call_target="tpu_custom_call" | custom-call | tf_op jit(solution)/shard_map/pallas_call | solution.py:402
  34.6 2.0 %collective-permute-start = (f32[5,16,256]{2,1,0:T(8,128)S(1)}, f32[5,16,256]{2,1,0:T(8,128)S(1)}, u32[]{:S(2)}, u32[]{:S(2)}) collective-permute-start(f32[5,16,256]{2,1,0:T(8,128)S(1)} %get-tuple-element.24), channel_id=1, source_target_pairs={{0,8},{8,16},{16,24},{1,9},{9,17},{17,25},{2,10},{10,18},{18,26},{... | collective-permute-start | bytes 245768 | tf_op jit(solution)/shard_map/ppermute | solution.py:466
  36.6 3.5 %collective-permute-start.1 = (f32[5,16,256]{2,1,0:T(8,128)S(1)}, f32[5,16,256]{2,1,0:T(8,128)S(1)}, u32[]{:S(2)}, u32[]{:S(2)}) collective-permute-start(f32[5,16,256]{2,1,0:T(8,128)S(1)} %get-tuple-element.25), channel_id=1, source_target_pairs={{8,0},{16,8},{24,16},{9,1},{17,9},{25,17},{10,2},{18,10},{26,18},{... | collective-permute-start | bytes 245768 | tf_op jit(solution)/shard_map/ppermute | solution.py:466
  40.2 3.4 %collective-permute-start.2 = (f32[5,16,256]{2,1,0:T(8,128)S(1)}, f32[5,16,256]{2,1,0:T(8,128)S(1)}, u32[]{:S(2)}, u32[]{:S(2)}) collective-permute-start(f32[5,16,256]{2,1,0:T(8,128)S(1)} %get-tuple-element.26), channel_id=1, source_target_pairs={{0,1},{1,2},{2,3},{3,4},{4,5},{5,6},{6,7},{8,9},{9,10},{10,11},{11... | collective-permute-start | bytes 245768 | tf_op jit(solution)/shard_map/ppermute | solution.py:466
  43.5 2.5 %collective-permute-start.3 = (f32[5,16,256]{2,1,0:T(8,128)S(1)}, f32[5,16,256]{2,1,0:T(8,128)S(1)}, u32[]{:S(2)}, u32[]{:S(2)}) collective-permute-start(f32[5,16,256]{2,1,0:T(8,128)S(1)} %get-tuple-element.27), channel_id=1, source_target_pairs={{1,0},{2,1},{3,2},{4,3},{5,4},{6,5},{7,6},{9,8},{10,9},{11,10},{12... | collective-permute-start | bytes 245768 | tf_op jit(solution)/shard_map/ppermute | solution.py:466
  46.0 0.0 collective-permute-done.from_x0
  46.0 0.0 collective-permute-done.1.from_x1
  46.0 0.5 collective-permute-done.2.from_y0
  46.5 4.3 %collective-permute-done.3.from_y1 = f32[5,16,256]{2,1,0:T(8,128)S(1)} collective-permute-done((f32[5,16,256]{2,1,0:T(8,128)S(1)}, f32[5,16,256]{2,1,0:T(8,128)S(1)}, u32[]{:S(2)}, u32[]{:S(2)}) %collective-permute-start.3) | collective-permute-done | bytes 81952 | tf_op jit(solution)/shard_map/ppermute | solution.py:466
  50.8 6.2 %shard_map.98 = f32[5,256,256]{2,1,0:T(8,128)} custom-call(s32[32,128]{1,0:T(8,128)S(1)} %get-tuple-element.21.ids_vmem, f32[1024,128]{1,0:T(8,128)S(1)} %get-tuple-element.22.source, f32[5,256,256]{2,1,0:T(8,128)} %get-tuple-element.23.diffused, f32[5,16,256]{2,1,0:T(8,128)S(1)} %collective-permute-done.from_x0, ...), custom_call_target="tpu_custom_call" | custom-call | flops 30000000 | tf_op jit(solution)/shard_map/pallas_call | solution.py:402
  57.0 0.0 all-to-all-done.1
  57.0 0.8 %shard_map.99 = (f32[4,8,12,1,128]{4,3,2,1,0:T(1,128)}, f32[4,8,4,1,128]{4,3,2,1,0:T(1,128)}) custom-call(f32[8,4,16,1,128]{4,3,2,1,0:T(1,128)S(1)} %bitcast.34), custom_call_target="tpu_custom_call" | custom-call | tf_op jit(solution)/shard_map/pallas_call | solution.py:402
Async XLA Ops:
  2.6 23.9 %all-to-all-start = ((f32[32,41,1,128]{3,2,1,0:T(1,128)}), f32[32,41,1,128]{3,2,1,0:T(1,128)S(1)}, u32[]{:S(2)}, u32[]{:S(2)}) async-start(f32[32,41,1,128]{3,2,1,0:T(1,128)} %bitcast.35), calls=%async_computation | async-start | bytes 1343488 | tf_op jit(solution)/shard_map/all_to_all | solution.py:452
  29.2 27.7 %all-to-all-start.1 = ((f32[32,16,1,128]{3,1,2,0:T(8,128)}), f32[32,16,1,128]{3,1,2,0:T(8,128)S(1)}, u32[]{:S(2)}, u32[]{:S(2)}) async-start(f32[32,16,1,128]{3,1,2,0:T(8,128)} %bitcast.37), calls=%async_computation.1 | async-start | bytes 524288 | tf_op jit(solution)/shard_map/all_to_all | solution.py:493
  34.6 11.4 %collective-permute-start = (f32[5,16,256]{2,1,0:T(8,128)S(1)}, f32[5,16,256]{2,1,0:T(8,128)S(1)}, u32[]{:S(2)}, u32[]{:S(2)}) collective-permute-start(f32[5,16,256]{2,1,0:T(8,128)S(1)} %get-tuple-element.24), channel_id=1, source_target_pairs={{0,8},{8,16},{16,24},{1,9},{9,17},{17,25},{2,10},{10,18},{18,26},{... | collective-permute-start | bytes 245768 | tf_op jit(solution)/shard_map/ppermute | solution.py:466
  36.6 9.4 %collective-permute-start.1 = (f32[5,16,256]{2,1,0:T(8,128)S(1)}, f32[5,16,256]{2,1,0:T(8,128)S(1)}, u32[]{:S(2)}, u32[]{:S(2)}) collective-permute-start(f32[5,16,256]{2,1,0:T(8,128)S(1)} %get-tuple-element.25), channel_id=1, source_target_pairs={{8,0},{16,8},{24,16},{9,1},{17,9},{25,17},{10,2},{18,10},{26,18},{... | collective-permute-start | bytes 245768 | tf_op jit(solution)/shard_map/ppermute | solution.py:466
  40.2 6.3 %collective-permute-start.2 = (f32[5,16,256]{2,1,0:T(8,128)S(1)}, f32[5,16,256]{2,1,0:T(8,128)S(1)}, u32[]{:S(2)}, u32[]{:S(2)}) collective-permute-start(f32[5,16,256]{2,1,0:T(8,128)S(1)} %get-tuple-element.26), channel_id=1, source_target_pairs={{0,1},{1,2},{2,3},{3,4},{4,5},{5,6},{6,7},{8,9},{9,10},{10,11},{11... | collective-permute-start | bytes 245768 | tf_op jit(solution)/shard_map/ppermute | solution.py:466
  43.5 7.2 %collective-permute-start.3 = (f32[5,16,256]{2,1,0:T(8,128)S(1)}, f32[5,16,256]{2,1,0:T(8,128)S(1)}, u32[]{:S(2)}, u32[]{:S(2)}) collective-permute-start(f32[5,16,256]{2,1,0:T(8,128)S(1)} %get-tuple-element.27), channel_id=1, source_target_pairs={{1,0},{2,1},{3,2},{4,3},{5,4},{6,5},{7,6},{9,8},{10,9},{11,10},{12... | collective-permute-start | bytes 245768 | tf_op jit(solution)/shard_map/ppermute | solution.py:466

commit v6 on v5

--- a/solution.py
+++ b/solution.py
@@ -166,13 +166,20 @@
         sent(f).wait()
 
 
+def paired(ref, member, stride, offset, capacity):
+    starts = [(member + n) * stride + offset for n in range(2)]
+    return jnp.concatenate([ref[start : start + capacity, :] for start in starts], axis=0)
+
+
 def update_kernel(
-    message, table, result_hbm, source, ids_vmem, products, result, sems, *, rows, capacity
+    message, table, result_hbm, result, ids_vmem, products, turned, sems, *, rows, capacity
 ):
     devices = message.shape[0] // rows
     group = SUB * rows
     for g in range(devices // SUB):
         ids_vmem[g * SUB : (g + 1) * SUB, :] = message[pl.ds(g * group + rows - 1, SUB, stride=rows), :].astype(jnp.int32)
+    for k in range(capacity):
+        turned[k] = roll(ids_vmem[...], -k, 1)
     corner = lax.broadcasted_iota(jnp.int32, (SUB, LANES), 0)
     high = [(corner & bit) != 0 for bit in (4, 2, 1)]
     least = [jnp.where(h, 0.0, 1.0) for h in high]
@@ -187,20 +194,20 @@
         return pltpu.make_async_copy(result.at[place], result_hbm.at[place], sems.at[g])
 
     def per_group(g, carry):
-        numbers = ids_vmem[pl.ds(pl.multiple_of(g * SUB, SUB), SUB), :]
+        here = pl.ds(pl.multiple_of(g * SUB, SUB), SUB)
+        numbers = [turned[k, here, :] for k in range(capacity)]
         part = message.at[pl.ds(pl.multiple_of(g * group, SUB), group)]
         for step in range(SUB // 2):
 
             def both(field):
-                starts = [(2 * step + n) * rows + field * capacity for n in range(2)]
-                return jnp.concatenate([part[start : start + capacity, :] for start in starts], axis=0)
+                return paired(part, 2 * step, rows, field * capacity, capacity)
 
             first = ((both(6) * TILE_Y + both(7)) * TILE_Z + both(8)).astype(jnp.int32)
             alive = jnp.zeros((SUB, LANES), jnp.int32)
             for j in range(2 * capacity):
                 i, k = 2 * step + j // capacity, j % capacity
                 base = i * rows
-                tile = numbers[i, k]
+                tile = numbers[k][i, 0]
                 alive = jnp.where(row == j, tile, alive)
                 safe = jnp.maximum(tile, 0)
                 weight = None
@@ -229,26 +236,15 @@
             gap = sampled[3]
             soft = jnp.maximum(gap, 0.0) + jnp.log(1.0 + jnp.exp(-jnp.abs(gap)))
             mass_new = jnp.where(live, mass_old / (1.0 + EVAPORATION * soft / radius), mass_old)
-            vapour = mass_old - mass_new
-            fields, sources = [], []
-            for f in range(3):
-                velocity = both(f)
-                moved = jnp.where(live, (velocity + factor * sampled[f]) * share, velocity)
-                fields.append(moved)
-                sources.append(mass_old * (velocity - moved) + vapour * moved)
-            fields.append(mass_new)
-            sources.append(vapour)
-            for dim in range(3):
-                sources.append(both(3 + dim) + both(6 + dim))
+            fields = [
+                jnp.where(live, (both(f) + factor * sampled[f]) * share, both(f)) for f in range(3)
+            ] + [mass_new]
             first_block = (g * SUB + 2 * step) * capacity
             out = result.at[pl.ds(pl.multiple_of(first_block * FLOWS, SUB), SUB * FLOWS)]
             for n in range(2):
                 for f in range(FLOWS):
                     start = (n * FLOWS + f) * capacity
                     out[start : start + capacity, :] = fields[f][n * capacity : (n + 1) * capacity]
-            out = source.at[pl.ds(pl.multiple_of(first_block * SUB, SUB), SUB * SUB)]
-            for f in range(7):
-                out[pl.ds(f, SUB, stride=SUB), :] = sources[f]
         returned(g).start()
         return carry
 
@@ -262,18 +258,43 @@
 
 
 def deposit_kernel(
-    ids_vmem, source, diffused, from_x0, from_x1, from_y0, from_y1, gas_next, total, ids, work, sems, *, capacity
+    ids_vmem, message, result, diffused, from_x0, from_x1, from_y0, from_y1, gas_next,
+    total, source, ids, work, sems, *, rows, capacity
 ):
     fields, extent_x, extent_z = from_y0.shape
     extent_y = from_x0.shape[1]
     across_y = extent_y // TILE_Y
     across_z = extent_z // TILE_Z
     blocks = source.shape[0] // SUB
+    group = SUB * rows
+    spread = capacity * FLOWS
     copy = pltpu.make_async_copy(ids_vmem, ids, sems.at[0])
     copy.start()
     fetch = pltpu.make_async_copy(diffused, work, sems.at[1])
     fetch.start()
     total[...] = jnp.zeros(total.shape, total.dtype)
+
+    def per_group(g, carry):
+        part = message.at[pl.ds(pl.multiple_of(g * group, SUB), group)]
+        updated = result.at[pl.ds(pl.multiple_of(g * SUB * spread, SUB), SUB * spread)]
+        out = source.at[pl.ds(pl.multiple_of(g * SUB * SUB * capacity, SUB), SUB * SUB * capacity)]
+        for step in range(SUB // 2):
+
+            def before(field):
+                return paired(part, 2 * step, rows, field * capacity, capacity)
+
+            def after(field):
+                return paired(updated, 2 * step, spread, field * capacity, capacity)
+
+            mass_old = before(9)
+            vapour = mass_old - after(3)
+            found = [mass_old * (before(f) - after(f)) + vapour * after(f) for f in range(3)] + [vapour]
+            found += [before(3 + dim) + before(6 + dim) for dim in range(3)]
+            for f, value in enumerate(found):
+                out[pl.ds(2 * step * capacity * SUB + f, 2 * capacity, stride=SUB), :] = value
+        return carry
+
+    lax.fori_loop(0, blocks // (SUB * capacity), per_group, 0)
     row = lax.broadcasted_iota(jnp.int32, (SUB, LANES), 0)
     along_z = row.astype(jnp.float32)
     along_y = (row % TILE_Y).astype(jnp.float32)
@@ -478,41 +499,42 @@
     )(gas_state)
     message, table, diffused = lax.optimization_barrier((message, table, diffused))
 
-    result, source, ids = call(
+    returned, result, ids = call(
         functools.partial(update_kernel, rows=rows, capacity=capacity),
-        (shape(blocks * FLOWS, LANES), shape(blocks * SUB, LANES), shape(devices, LANES, dtype=i32)),
+        (shape(blocks * FLOWS, LANES), shape(blocks * FLOWS, LANES), shape(devices, LANES, dtype=i32)),
         scratch=[
             vmem((FLOWS * SUB * SUB, LANES), f32),
-            vmem((blocks * FLOWS, LANES), f32),
+            vmem((capacity, devices, LANES), i32),
             dma((devices // SUB,)),
         ],
         flops=10**7,
         ins=[vmem, vmem],
         outs=[hbm, vmem, vmem],
     )(message, table)
-    result = lax.all_to_all(
-        result.reshape(devices, capacity * FLOWS, 1, LANES), BOTH, split_axis=0, concat_axis=0, tiled=True
+    returned = lax.all_to_all(
+        returned.reshape(devices, capacity * FLOWS, 1, LANES), BOTH, split_axis=0, concat_axis=0, tiled=True
     )
     gas_next = call(
-        functools.partial(deposit_kernel, capacity=capacity),
+        functools.partial(deposit_kernel, rows=rows, capacity=capacity),
         shape(*flat),
         scratch=[
             vmem((tiles * SUB, LANES), f32),
+            vmem((blocks * SUB, LANES), f32),
             pltpu.SMEM((devices, LANES), i32),
             vmem(flat, f32),
             dma((2 + extent_x // TILE_X,)),
         ],
         flops=3 * 10**7,
-        ins=[vmem, vmem, hbm] + [vmem] * 4,
+        ins=[vmem, vmem, vmem, hbm] + [vmem] * 4,
         outs=[hbm],
-    )(ids, source, diffused, *halo)
+    )(ids, message, result, diffused, *halo)
     speed_next, mass_next = call(
         unpack_kernel,
         (shape(across_i, across_j, vector, 1, LANES), shape(across_i, across_j, capacity, 1, LANES)),
         scratch=[dma((2 * across_i,))],
         ins=[vmem],
         outs=[hbm, hbm],
-    )(result.reshape(across_j, across_i, capacity * FLOWS, 1, LANES))
+    )(returned.reshape(across_j, across_i, capacity * FLOWS, 1, LANES))
     speed_next = speed_next.reshape(devices, 3, capacity, LANES).transpose(0, 2, 1, 3)
     return gas_next.reshape(gas_state.shape), speed_next.reshape(parcel_speed.shape), mass_next.reshape(parcel_mass.shape)
 

time: 58.2 us -> 57.9 us (level)
  no operation moved by 1% of the time
where the time goes in v6:
time: 57.9 us; the launch traced here: 57.5 us
  starting transfers between devices  21.4 us (37%)
  waiting for transfers between devices  19.1 us (33%)
  Pallas kernels  16.3 us (28%)
  between operations  0.74 us (1%)
    pallas_call x6, Pallas kernels, with_spaces(): return called(*values)  16.3 us
    all_to_all x1, waiting for transfers between devices, step(): lax.all_to_all(message.reshape(devices, rows, 1, LANES), BOTH, split_axis...  14.3 us
    ppermute x4, starting transfers between devices, shifted(): return lax.ppermute(value, axis, pairs)  11.4 us
    all_to_all x1, starting transfers between devices, step(): lax.all_to_all(message.reshape(devices, rows, 1, LANES), BOTH, split_axis...  6.08 us
    ppermute x4, waiting for transfers between devices, shifted(): return lax.ppermute(value, axis, pairs)  4.74 us
    all_to_all x1, starting transfers between devices, step(): lax.all_to_all(returned.reshape(devices, capacity * FLOWS, 1, LANES), BOT...  3.89 us
  transfers between devices with their start and end apart: 6, of which 3 were waited for; matrix products, arithmetic and copies ran while one was open for 0% of the time, Pallas kernels for 19%

profile of v6, /device:TPU:6, one launch (start us, length us, event | category | flops | bytes accessed | tf_op | source)
XLA Modules:
  0.0 57.5 jit_solution(157931734723408510)
XLA Ops:
  0.6 2.0 %shard_map.94 = f32[1312,128]{1,0:T(8,128)} custom-call(f32[4,96,128]{2,1,0:T(8,128)} %bitcast.39, f32[4,32,128]{2,1,0:T(8,128)} %bitcast.42, f32[4,96,128]{2,1,0:T(8,128)} %bitcast.40, s32[4,96,128]{2,1,0:T(8,128)} %bitcast.41, s32[4,32]{1,0:T(4,128)} %bitcast.43, s32[1,32]{1,0:T(1,128)} %bitcast.44), custom_call_target="tpu_custom_call" | custom-call | tf_op jit(solution)/shard_map/pallas_call | solution.py:423
  2.6 6.1 %all-to-all-start = ((f32[32,41,1,128]{3,2,1,0:T(1,128)}), f32[32,41,1,128]{3,2,1,0:T(1,128)S(1)}, u32[]{:S(2)}, u32[]{:S(2)}) async-start(f32[32,41,1,128]{3,2,1,0:T(1,128)} %bitcast.36), calls=%async_computation | async-start | bytes 1343488 | tf_op jit(solution)/shard_map/all_to_all | solution.py:473
  8.7 3.5 %shard_map.95 = (f32[4,512,128]{2,1,0:T(8,128)S(1)}, f32[5,256,256]{2,1,0:T(8,128)}) custom-call(f32[5,16,16,256]{3,2,1,0:T(8,128)} %gas_hbm.3), custom_call_target="tpu_custom_call" | custom-call | flops 10000000 | tf_op jit(solution)/shard_map/pallas_call | solution.py:423
  12.2 14.3 %all-to-all-done = f32[32,41,1,128]{3,2,1,0:T(1,128)S(1)} async-done(((f32[32,41,1,128]{3,2,1,0:T(1,128)}), f32[32,41,1,128]{3,2,1,0:T(1,128)S(1)}, u32[]{:S(2)}, u32[]{:S(2)}) %all-to-all-start) | async-done | bytes 671776 | tf_op jit(solution)/shard_map/all_to_all | solution.py:473
  26.6 2.4 %shard_map.96 = (f32[512,128]{1,0:T(8,128)}, f32[512,128]{1,0:T(8,128)S(1)}, s32[32,128]{1,0:T(8,128)S(1)}) custom-call(f32[1312,128]{1,0:T(8,128)S(1)} %bitcast.33, f32[4,512,128]{2,1,0:T(8,128)S(1)} %get-tuple-element.20.table), custom_call_target="tpu_custom_call" | custom-call | flops 10000000 | tf_op jit(solution)/shard_map/pallas_call | solution.py:423
  29.0 3.9 %all-to-all-start.1 = ((f32[32,16,1,128]{3,1,2,0:T(8,128)}), f32[32,16,1,128]{3,1,2,0:T(8,128)S(1)}, u32[]{:S(2)}, u32[]{:S(2)}) async-start(f32[32,16,1,128]{3,1,2,0:T(8,128)} %bitcast.38), calls=%async_computation.1 | async-start | bytes 524288 | tf_op jit(solution)/shard_map/all_to_all | solution.py:514
  32.9 1.4 %shard_map.97 = (f32[5,16,256]{2,1,0:T(8,128)S(1)}, f32[5,16,256]{2,1,0:T(8,128)S(1)}, f32[5,16,256]{2,1,0:T(8,128)S(1)}, f32[5,16,256]{2,1,0:T(8,128)S(1)}) custom-call(f32[5,16,16,256]{3,2,1,0:T(8,128)} %gas_hbm.3), custom_call_target="tpu_custom_call" | custom-call | tf_op jit(solution)/shard_map/pallas_call | solution.py:423
  34.3 2.0 %collective-permute-start = (f32[5,16,256]{2,1,0:T(8,128)S(1)}, f32[5,16,256]{2,1,0:T(8,128)S(1)}, u32[]{:S(2)}, u32[]{:S(2)}) collective-permute-start(f32[5,16,256]{2,1,0:T(8,128)S(1)} %get-tuple-element.24), channel_id=1, source_target_pairs={{0,8},{8,16},{16,24},{1,9},{9,17},{17,25},{2,10},{10,18},{18,26},{... | collective-permute-start | bytes 245768 | tf_op jit(solution)/shard_map/ppermute | solution.py:487
  36.3 3.5 %collective-permute-start.1 = (f32[5,16,256]{2,1,0:T(8,128)S(1)}, f32[5,16,256]{2,1,0:T(8,128)S(1)}, u32[]{:S(2)}, u32[]{:S(2)}) collective-permute-start(f32[5,16,256]{2,1,0:T(8,128)S(1)} %get-tuple-element.25), channel_id=1, source_target_pairs={{8,0},{16,8},{24,16},{9,1},{17,9},{25,17},{10,2},{18,10},{26,18},{... | collective-permute-start | bytes 245768 | tf_op jit(solution)/shard_map/ppermute | solution.py:487
  39.9 3.4 %collective-permute-start.2 = (f32[5,16,256]{2,1,0:T(8,128)S(1)}, f32[5,16,256]{2,1,0:T(8,128)S(1)}, u32[]{:S(2)}, u32[]{:S(2)}) collective-permute-start(f32[5,16,256]{2,1,0:T(8,128)S(1)} %get-tuple-element.26), channel_id=1, source_target_pairs={{0,1},{1,2},{2,3},{3,4},{4,5},{5,6},{6,7},{8,9},{9,10},{10,11},{11... | collective-permute-start | bytes 245768 | tf_op jit(solution)/shard_map/ppermute | solution.py:487
  43.3 2.5 %collective-permute-start.3 = (f32[5,16,256]{2,1,0:T(8,128)S(1)}, f32[5,16,256]{2,1,0:T(8,128)S(1)}, u32[]{:S(2)}, u32[]{:S(2)}) collective-permute-start(f32[5,16,256]{2,1,0:T(8,128)S(1)} %get-tuple-element.27), channel_id=1, source_target_pairs={{1,0},{2,1},{3,2},{4,3},{5,4},{6,5},{7,6},{9,8},{10,9},{11,10},{12... | collective-permute-start | bytes 245768 | tf_op jit(solution)/shard_map/ppermute | solution.py:487
  45.7 0.0 collective-permute-done.from_x0
  45.7 0.0 collective-permute-done.1.from_x1
  45.8 0.5 collective-permute-done.2.from_y0
  46.2 4.3 %collective-permute-done.3.from_y1 = f32[5,16,256]{2,1,0:T(8,128)S(1)} collective-permute-done((f32[5,16,256]{2,1,0:T(8,128)S(1)}, f32[5,16,256]{2,1,0:T(8,128)S(1)}, u32[]{:S(2)}, u32[]{:S(2)}) %collective-permute-start.3) | collective-permute-done | bytes 81952 | tf_op jit(solution)/shard_map/ppermute | solution.py:487
  50.5 6.2 %shard_map.98 = f32[5,256,256]{2,1,0:T(8,128)} custom-call(s32[32,128]{1,0:T(8,128)S(1)} %get-tuple-element.21.ids_vmem, f32[1312,128]{1,0:T(8,128)S(1)} %bitcast.34, f32[512,128]{1,0:T(8,128)S(1)} %get-tuple-element.22.result, f32[5,256,256]{2,1,0:T(8,128)} %get-tuple-element.23.diffused, f32[5,16,256]{2,1,0:T(8,128)S(1)} %collective-permute-done.from_x0, ...), custom_call_target="tpu_custom_call" | custom-call | flops 30000000 | tf_op jit(solution)/shard_map/pallas_call | solution.py:423
  56.7 0.0 all-to-all-done.1
  56.7 0.8 %shard_map.99 = (f32[4,8,12,1,128]{4,3,2,1,0:T(1,128)}, f32[4,8,4,1,128]{4,3,2,1,0:T(1,128)}) custom-call(f32[8,4,16,1,128]{4,3,2,1,0:T(1,128)S(1)} %bitcast.35), custom_call_target="tpu_custom_call" | custom-call | tf_op jit(solution)/shard_map/pallas_call | solution.py:423
Async XLA Ops:
  2.6 23.9 %all-to-all-start = ((f32[32,41,1,128]{3,2,1,0:T(1,128)}), f32[32,41,1,128]{3,2,1,0:T(1,128)S(1)}, u32[]{:S(2)}, u32[]{:S(2)}) async-start(f32[32,41,1,128]{3,2,1,0:T(1,128)} %bitcast.36), calls=%async_computation | async-start | bytes 1343488 | tf_op jit(solution)/shard_map/all_to_all | solution.py:473
  29.0 27.7 %all-to-all-start.1 = ((f32[32,16,1,128]{3,1,2,0:T(8,128)}), f32[32,16,1,128]{3,1,2,0:T(8,128)S(1)}, u32[]{:S(2)}, u32[]{:S(2)}) async-start(f32[32,16,1,128]{3,1,2,0:T(8,128)} %bitcast.38), calls=%async_computation.1 | async-start | bytes 524288 | tf_op jit(solution)/shard_map/all_to_all | solution.py:514
  34.3 11.4 %collective-permute-start = (f32[5,16,256]{2,1,0:T(8,128)S(1)}, f32[5,16,256]{2,1,0:T(8,128)S(1)}, u32[]{:S(2)}, u32[]{:S(2)}) collective-permute-start(f32[5,16,256]{2,1,0:T(8,128)S(1)} %get-tuple-element.24), channel_id=1, source_target_pairs={{0,8},{8,16},{16,24},{1,9},{9,17},{17,25},{2,10},{10,18},{18,26},{... | collective-permute-start | bytes 245768 | tf_op jit(solution)/shard_map/ppermute | solution.py:487
  36.3 9.4 %collective-permute-start.1 = (f32[5,16,256]{2,1,0:T(8,128)S(1)}, f32[5,16,256]{2,1,0:T(8,128)S(1)}, u32[]{:S(2)}, u32[]{:S(2)}) collective-permute-start(f32[5,16,256]{2,1,0:T(8,128)S(1)} %get-tuple-element.25), channel_id=1, source_target_pairs={{8,0},{16,8},{24,16},{9,1},{17,9},{25,17},{10,2},{18,10},{26,18},{... | collective-permute-start | bytes 245768 | tf_op jit(solution)/shard_map/ppermute | solution.py:487
  39.9 6.3 %collective-permute-start.2 = (f32[5,16,256]{2,1,0:T(8,128)S(1)}, f32[5,16,256]{2,1,0:T(8,128)S(1)}, u32[]{:S(2)}, u32[]{:S(2)}) collective-permute-start(f32[5,16,256]{2,1,0:T(8,128)S(1)} %get-tuple-element.26), channel_id=1, source_target_pairs={{0,1},{1,2},{2,3},{3,4},{4,5},{5,6},{6,7},{8,9},{9,10},{10,11},{11... | collective-permute-start | bytes 245768 | tf_op jit(solution)/shard_map/ppermute | solution.py:487
  43.3 7.2 %collective-permute-start.3 = (f32[5,16,256]{2,1,0:T(8,128)S(1)}, f32[5,16,256]{2,1,0:T(8,128)S(1)}, u32[]{:S(2)}, u32[]{:S(2)}) collective-permute-start(f32[5,16,256]{2,1,0:T(8,128)S(1)} %get-tuple-element.27), channel_id=1, source_target_pairs={{1,0},{2,1},{3,2},{4,3},{5,4},{6,5},{7,6},{9,8},{10,9},{11,10},{12... | collective-permute-start | bytes 245768 | tf_op jit(solution)/shard_map/ppermute | solution.py:487

commit v7 on v6

--- a/solution.py
+++ b/solution.py
@@ -21,7 +21,8 @@
 SUB = 8
 GRANULES = LANES // TILE_Z
 FLOWS = 4
-BOTH = ("yz", "gx")
+SENT = ("yz", "gx")
+RETURNED = ("gx", "yz")
 
 
 def roll(x, shift, axis):
@@ -171,6 +172,11 @@
     return jnp.concatenate([ref[start : start + capacity, :] for start in starts], axis=0)
 
 
+def columns(g, across_i, spread):
+    size = SUB // across_i * spread
+    return pl.ds(pl.multiple_of(g * size, SUB), size)
+
+
 def update_kernel(
     message, table, result_hbm, result, ids_vmem, products, turned, sems, *, rows, capacity
 ):
@@ -189,11 +195,15 @@
     )
     row = corner
 
+    across_i = result.shape[0]
+    spread = capacity * FLOWS
+
     def returned(g):
-        place = pl.ds(pl.multiple_of(g * SUB * capacity * FLOWS, SUB), SUB * capacity * FLOWS)
-        return pltpu.make_async_copy(result.at[place], result_hbm.at[place], sems.at[g])
+        place = columns(g, across_i, spread)
+        return pltpu.make_async_copy(result.at[:, place], result_hbm.at[:, place], sems.at[g])
 
     def per_group(g, carry):
+        out = result.at[:, columns(g, across_i, spread)]
         here = pl.ds(pl.multiple_of(g * SUB, SUB), SUB)
         numbers = [turned[k, here, :] for k in range(capacity)]
         part = message.at[pl.ds(pl.multiple_of(g * group, SUB), group)]
@@ -239,12 +249,11 @@
             fields = [
                 jnp.where(live, (both(f) + factor * sampled[f]) * share, both(f)) for f in range(3)
             ] + [mass_new]
-            first_block = (g * SUB + 2 * step) * capacity
-            out = result.at[pl.ds(pl.multiple_of(first_block * FLOWS, SUB), SUB * FLOWS)]
             for n in range(2):
+                i, start = (2 * step + n) % across_i, (2 * step + n) // across_i * spread
                 for f in range(FLOWS):
-                    start = (n * FLOWS + f) * capacity
-                    out[start : start + capacity, :] = fields[f][n * capacity : (n + 1) * capacity]
+                    rows_f = slice(start + f * capacity, start + (f + 1) * capacity)
+                    out[i, rows_f, :] = fields[f][n * capacity : (n + 1) * capacity]
         returned(g).start()
         return carry
 
@@ -268,6 +277,7 @@
     blocks = source.shape[0] // SUB
     group = SUB * rows
     spread = capacity * FLOWS
+    across_i = result.shape[0]
     copy = pltpu.make_async_copy(ids_vmem, ids, sems.at[0])
     copy.start()
     fetch = pltpu.make_async_copy(diffused, work, sems.at[1])
@@ -276,7 +286,7 @@
 
     def per_group(g, carry):
         part = message.at[pl.ds(pl.multiple_of(g * group, SUB), group)]
-        updated = result.at[pl.ds(pl.multiple_of(g * SUB * spread, SUB), SUB * spread)]
+        updated = result.at[:, columns(g, across_i, spread)]
         out = source.at[pl.ds(pl.multiple_of(g * SUB * SUB * capacity, SUB), SUB * SUB * capacity)]
         for step in range(SUB // 2):
 
@@ -284,7 +294,11 @@
                 return paired(part, 2 * step, rows, field * capacity, capacity)
 
             def after(field):
-                return paired(updated, 2 * step, spread, field * capacity, capacity)
+                found = []
+                for member in (2 * step, 2 * step + 1):
+                    i, start = member % across_i, member // across_i * spread + field * capacity
+                    found.append(updated[i, start : start + capacity, :])
+                return jnp.concatenate(found, axis=0)
 
             mass_old = before(9)
             vapour = mass_old - after(3)
@@ -380,11 +394,11 @@
 
 
 def unpack_kernel(result, speed, mass, sems):
-    vector = speed.shape[2]
-    copies = []
-    for i in range(speed.shape[0]):
-        copies.append(pltpu.make_async_copy(result.at[:, i, :vector], speed.at[i], sems.at[2 * i]))
-        copies.append(pltpu.make_async_copy(result.at[:, i, vector:], mass.at[i], sems.at[2 * i + 1]))
+    vector = speed.shape[1]
+    copies = [
+        pltpu.make_async_copy(result.at[:, :vector], speed, sems.at[0]),
+        pltpu.make_async_copy(result.at[:, vector:], mass, sems.at[1]),
+    ]
     for copy in copies:
         copy.start()
     for copy in copies:
@@ -470,7 +484,7 @@
         block_tile[0, 0].T,
         block_count[0],
     )
-    message = lax.all_to_all(message.reshape(devices, rows, 1, LANES), BOTH, split_axis=0, concat_axis=0, tiled=True)
+    message = lax.all_to_all(message.reshape(devices, rows, 1, LANES), SENT, split_axis=0, concat_axis=0, tiled=True)
     message = message.reshape(devices * rows, LANES)
 
     face = shape(fields, extent_x, extent_z)
@@ -501,7 +515,11 @@
 
     returned, result, ids = call(
         functools.partial(update_kernel, rows=rows, capacity=capacity),
-        (shape(blocks * FLOWS, LANES), shape(blocks * FLOWS, LANES), shape(devices, LANES, dtype=i32)),
+        (
+            shape(across_i, across_j * capacity * FLOWS, LANES),
+            shape(across_i, across_j * capacity * FLOWS, LANES),
+            shape(devices, LANES, dtype=i32),
+        ),
         scratch=[
             vmem((FLOWS * SUB * SUB, LANES), f32),
             vmem((capacity, devices, LANES), i32),
@@ -512,7 +530,7 @@
         outs=[hbm, vmem, vmem],
     )(message, table)
     returned = lax.all_to_all(
-        returned.reshape(devices, capacity * FLOWS, 1, LANES), BOTH, split_axis=0, concat_axis=0, tiled=True
+        returned.reshape(devices, capacity * FLOWS, 1, LANES), RETURNED, split_axis=0, concat_axis=0, tiled=True
     )
     gas_next = call(
         functools.partial(deposit_kernel, rows=rows, capacity=capacity),
@@ -530,11 +548,11 @@
     )(ids, message, result, diffused, *halo)
     speed_next, mass_next = call(
         unpack_kernel,
-        (shape(across_i, across_j, vector, 1, LANES), shape(across_i, across_j, capacity, 1, LANES)),
-        scratch=[dma((2 * across_i,))],
+        (shape(devices, vector, 1, LANES), shape(devices, capacity, 1, LANES)),
+        scratch=[dma((2,))],
         ins=[vmem],
         outs=[hbm, hbm],
-    )(returned.reshape(across_j, across_i, capacity * FLOWS, 1, LANES))
+    )(returned)
     speed_next = speed_next.reshape(devices, 3, capacity, LANES).transpose(0, 2, 1, 3)
     return gas_next.reshape(gas_state.shape), speed_next.reshape(parcel_speed.shape), mass_next.reshape(parcel_mass.shape)
 

time: 57.9 us -> 57.9 us (level)
  no operation moved by 1% of the time
where the time goes in v7:
time: 57.9 us; the launch traced here: 57.4 us
  starting transfers between devices  21.4 us (37%)
  waiting for transfers between devices  19.1 us (33%)
  Pallas kernels  16.2 us (28%)
  between operations  0.74 us (1%)
    pallas_call x6, Pallas kernels, with_spaces(): return called(*values)  16.2 us
    all_to_all x1, waiting for transfers between devices, step(): lax.all_to_all(message.reshape(devices, rows, 1, LANES), SENT, split_axis...  14.3 us
    ppermute x4, starting transfers between devices, shifted(): return lax.ppermute(value, axis, pairs)  11.4 us
    all_to_all x1, starting transfers between devices, step(): lax.all_to_all(message.reshape(devices, rows, 1, LANES), SENT, split_axis...  6.08 us
    ppermute x4, waiting for transfers between devices, shifted(): return lax.ppermute(value, axis, pairs)  4.74 us
    all_to_all x1, starting transfers between devices, step(): lax.all_to_all(returned.reshape(devices, capacity * FLOWS, 1, LANES), RET...  3.89 us
  transfers between devices with their start and end apart: 6, of which 3 were waited for; matrix products, arithmetic and copies ran while one was open for 0% of the time, Pallas kernels for 19%

profile of v7, /device:TPU:6, one launch (start us, length us, event | category | flops | bytes accessed | tf_op | source)
XLA Modules:
  0.0 57.4 jit_solution(10058485288994647236)
XLA Ops:
  0.6 2.0 %shard_map.94 = f32[1312,128]{1,0:T(8,128)} custom-call(f32[4,96,128]{2,1,0:T(8,128)} %bitcast.35, f32[4,32,128]{2,1,0:T(8,128)} %bitcast.38, f32[4,96,128]{2,1,0:T(8,128)} %bitcast.36, s32[4,96,128]{2,1,0:T(8,128)} %bitcast.37, s32[4,32]{1,0:T(4,128)} %bitcast.39, s32[1,32]{1,0:T(1,128)} %bitcast.40), custom_call_target="tpu_custom_call" | custom-call | tf_op jit(solution)/shard_map/pallas_call | solution.py:437
  2.6 6.1 %all-to-all-start = ((f32[32,41,1,128]{3,2,1,0:T(1,128)}), f32[32,41,1,128]{3,2,1,0:T(1,128)S(1)}, u32[]{:S(2)}, u32[]{:S(2)}) async-start(f32[32,41,1,128]{3,2,1,0:T(1,128)} %bitcast.32), calls=%async_computation | async-start | bytes 1343488 | tf_op jit(solution)/shard_map/all_to_all | solution.py:487
  8.7 3.5 %shard_map.95 = (f32[4,512,128]{2,1,0:T(8,128)S(1)}, f32[5,256,256]{2,1,0:T(8,128)}) custom-call(f32[5,16,16,256]{3,2,1,0:T(8,128)} %gas_hbm.3), custom_call_target="tpu_custom_call" | custom-call | flops 10000000 | tf_op jit(solution)/shard_map/pallas_call | solution.py:437
  12.2 14.3 %all-to-all-done = f32[32,41,1,128]{3,2,1,0:T(1,128)S(1)} async-done(((f32[32,41,1,128]{3,2,1,0:T(1,128)}), f32[32,41,1,128]{3,2,1,0:T(1,128)S(1)}, u32[]{:S(2)}, u32[]{:S(2)}) %all-to-all-start) | async-done | bytes 671776 | tf_op jit(solution)/shard_map/all_to_all | solution.py:487
  26.6 2.4 %shard_map.96 = (f32[4,128,128]{2,1,0:T(8,128)}, f32[4,128,128]{2,1,0:T(8,128)S(1)}, s32[32,128]{1,0:T(8,128)S(1)}) custom-call(f32[1312,128]{1,0:T(8,128)S(1)} %bitcast.30, f32[4,512,128]{2,1,0:T(8,128)S(1)} %get-tuple-element.20.table), custom_call_target="tpu_custom_call" | custom-call | flops 10000000 | tf_op jit(solution)/shard_map/pallas_call | solution.py:437
  29.0 3.9 %all-to-all-start.1 = ((f32[32,16,1,128]{3,2,1,0:T(1,128)}), f32[32,16,1,128]{3,2,1,0:T(1,128)S(1)}, u32[]{:S(2)}, u32[]{:S(2)}) async-start(f32[32,16,1,128]{3,2,1,0:T(1,128)} %bitcast.34), calls=%async_computation.1 | async-start | bytes 524288 | tf_op jit(solution)/shard_map/all_to_all | solution.py:532
  32.9 1.4 %shard_map.97 = (f32[5,16,256]{2,1,0:T(8,128)S(1)}, f32[5,16,256]{2,1,0:T(8,128)S(1)}, f32[5,16,256]{2,1,0:T(8,128)S(1)}, f32[5,16,256]{2,1,0:T(8,128)S(1)}) custom-call(f32[5,16,16,256]{3,2,1,0:T(8,128)} %gas_hbm.3), custom_call_target="tpu_custom_call" | custom-call | tf_op jit(solution)/shard_map/pallas_call | solution.py:437
  34.3 2.0 %collective-permute-start = (f32[5,16,256]{2,1,0:T(8,128)S(1)}, f32[5,16,256]{2,1,0:T(8,128)S(1)}, u32[]{:S(2)}, u32[]{:S(2)}) collective-permute-start(f32[5,16,256]{2,1,0:T(8,128)S(1)} %get-tuple-element.24), channel_id=1, source_target_pairs={{0,8},{8,16},{16,24},{1,9},{9,17},{17,25},{2,10},{10,18},{18,26},{... | collective-permute-start | bytes 245768 | tf_op jit(solution)/shard_map/ppermute | solution.py:501
  36.3 3.5 %collective-permute-start.1 = (f32[5,16,256]{2,1,0:T(8,128)S(1)}, f32[5,16,256]{2,1,0:T(8,128)S(1)}, u32[]{:S(2)}, u32[]{:S(2)}) collective-permute-start(f32[5,16,256]{2,1,0:T(8,128)S(1)} %get-tuple-element.25), channel_id=1, source_target_pairs={{8,0},{16,8},{24,16},{9,1},{17,9},{25,17},{10,2},{18,10},{26,18},{... | collective-permute-start | bytes 245768 | tf_op jit(solution)/shard_map/ppermute | solution.py:501
  39.9 3.4 %collective-permute-start.2 = (f32[5,16,256]{2,1,0:T(8,128)S(1)}, f32[5,16,256]{2,1,0:T(8,128)S(1)}, u32[]{:S(2)}, u32[]{:S(2)}) collective-permute-start(f32[5,16,256]{2,1,0:T(8,128)S(1)} %get-tuple-element.26), channel_id=1, source_target_pairs={{0,1},{1,2},{2,3},{3,4},{4,5},{5,6},{6,7},{8,9},{9,10},{10,11},{11... | collective-permute-start | bytes 245768 | tf_op jit(solution)/shard_map/ppermute | solution.py:501
  43.3 2.5 %collective-permute-start.3 = (f32[5,16,256]{2,1,0:T(8,128)S(1)}, f32[5,16,256]{2,1,0:T(8,128)S(1)}, u32[]{:S(2)}, u32[]{:S(2)}) collective-permute-start(f32[5,16,256]{2,1,0:T(8,128)S(1)} %get-tuple-element.27), channel_id=1, source_target_pairs={{1,0},{2,1},{3,2},{4,3},{5,4},{6,5},{7,6},{9,8},{10,9},{11,10},{12... | collective-permute-start | bytes 245768 | tf_op jit(solution)/shard_map/ppermute | solution.py:501
  45.7 0.0 collective-permute-done.from_x0
  45.7 0.0 collective-permute-done.1.from_x1
  45.8 0.5 collective-permute-done.2.from_y0
  46.2 4.3 %collective-permute-done.3.from_y1 = f32[5,16,256]{2,1,0:T(8,128)S(1)} collective-permute-done((f32[5,16,256]{2,1,0:T(8,128)S(1)}, f32[5,16,256]{2,1,0:T(8,128)S(1)}, u32[]{:S(2)}, u32[]{:S(2)}) %collective-permute-start.3) | collective-permute-done | bytes 81952 | tf_op jit(solution)/shard_map/ppermute | solution.py:501
  50.5 6.2 %shard_map.98 = f32[5,256,256]{2,1,0:T(8,128)} custom-call(s32[32,128]{1,0:T(8,128)S(1)} %get-tuple-element.21.ids_vmem, f32[1312,128]{1,0:T(8,128)S(1)} %bitcast.31, f32[4,128,128]{2,1,0:T(8,128)S(1)} %get-tuple-element.22.result, f32[5,256,256]{2,1,0:T(8,128)} %get-tuple-element.23.diffused, f32[5,16,256]{2,1,0:T(8,128)S(1)} %collective-permute-done.from_x0, ...), custom_call_target="tpu_custom_call" | custom-call | flops 30000000 | tf_op jit(solution)/shard_map/pallas_call | solution.py:437
  56.7 0.0 all-to-all-done.1.result
  56.7 0.7 %shard_map.99 = (f32[32,12,1,128]{3,2,1,0:T(1,128)}, f32[32,4,1,128]{3,2,1,0:T(1,128)}) custom-call(f32[32,16,1,128]{3,2,1,0:T(1,128)S(1)} %all-to-all-done.1.result), custom_call_target="tpu_custom_call" | custom-call | tf_op jit(solution)/shard_map/pallas_call | solution.py:437
Async XLA Ops:
  2.6 23.9 %all-to-all-start = ((f32[32,41,1,128]{3,2,1,0:T(1,128)}), f32[32,41,1,128]{3,2,1,0:T(1,128)S(1)}, u32[]{:S(2)}, u32[]{:S(2)}) async-start(f32[32,41,1,128]{3,2,1,0:T(1,128)} %bitcast.32), calls=%async_computation | async-start | bytes 1343488 | tf_op jit(solution)/shard_map/all_to_all | solution.py:487
  29.0 27.7 %all-to-all-start.1 = ((f32[32,16,1,128]{3,2,1,0:T(1,128)}), f32[32,16,1,128]{3,2,1,0:T(1,128)S(1)}, u32[]{:S(2)}, u32[]{:S(2)}) async-start(f32[32,16,1,128]{3,2,1,0:T(1,128)} %bitcast.34), calls=%async_computation.1 | async-start | bytes 524288 | tf_op jit(solution)/shard_map/all_to_all | solution.py:532
  34.3 11.4 %collective-permute-start = (f32[5,16,256]{2,1,0:T(8,128)S(1)}, f32[5,16,256]{2,1,0:T(8,128)S(1)}, u32[]{:S(2)}, u32[]{:S(2)}) collective-permute-start(f32[5,16,256]{2,1,0:T(8,128)S(1)} %get-tuple-element.24), channel_id=1, source_target_pairs={{0,8},{8,16},{16,24},{1,9},{9,17},{17,25},{2,10},{10,18},{18,26},{... | collective-permute-start | bytes 245768 | tf_op jit(solution)/shard_map/ppermute | solution.py:501
  36.3 9.4 %collective-permute-start.1 = (f32[5,16,256]{2,1,0:T(8,128)S(1)}, f32[5,16,256]{2,1,0:T(8,128)S(1)}, u32[]{:S(2)}, u32[]{:S(2)}) collective-permute-start(f32[5,16,256]{2,1,0:T(8,128)S(1)} %get-tuple-element.25), channel_id=1, source_target_pairs={{8,0},{16,8},{24,16},{9,1},{17,9},{25,17},{10,2},{18,10},{26,18},{... | collective-permute-start | bytes 245768 | tf_op jit(solution)/shard_map/ppermute | solution.py:501
  39.9 6.3 %collective-permute-start.2 = (f32[5,16,256]{2,1,0:T(8,128)S(1)}, f32[5,16,256]{2,1,0:T(8,128)S(1)}, u32[]{:S(2)}, u32[]{:S(2)}) collective-permute-start(f32[5,16,256]{2,1,0:T(8,128)S(1)} %get-tuple-element.26), channel_id=1, source_target_pairs={{0,1},{1,2},{2,3},{3,4},{4,5},{5,6},{6,7},{8,9},{9,10},{10,11},{11... | collective-permute-start | bytes 245768 | tf_op jit(solution)/shard_map/ppermute | solution.py:501
  43.3 7.2 %collective-permute-start.3 = (f32[5,16,256]{2,1,0:T(8,128)S(1)}, f32[5,16,256]{2,1,0:T(8,128)S(1)}, u32[]{:S(2)}, u32[]{:S(2)}) collective-permute-start(f32[5,16,256]{2,1,0:T(8,128)S(1)} %get-tuple-element.27), channel_id=1, source_target_pairs={{1,0},{2,1},{3,2},{4,3},{5,4},{6,5},{7,6},{9,8},{10,9},{11,10},{12... | collective-permute-start | bytes 245768 | tf_op jit(solution)/shard_map/ppermute | solution.py:501

commit v8 on v7

--- a/solution.py
+++ b/solution.py
@@ -103,46 +103,14 @@
         copy.wait()
 
 
-def faces_kernel(gas_hbm, face_x0, face_x1, face_y0, face_y1, gas, sem):
-    extent_x, extent_y = gas_hbm.shape[1:3]
-    copy = pltpu.make_async_copy(gas_hbm, gas, sem)
-    copy.start()
-    copy.wait()
+def table_kernel(gas, table, face_x0, face_x1, face_y0, face_y1):
+    extent_x, extent_y, extent_z = gas.shape[1:]
+    across_y = extent_y // TILE_Y
+    across_z = extent_z // TILE_Z
     face_x0[...] = gas[:, 0]
     face_x1[...] = gas[:, extent_x - 1]
     face_y0[...] = gas[:, :, 0, :]
     face_y1[...] = gas[:, :, extent_y - 1, :]
-
-
-def local_kernel(gas_hbm, table, diffused_hbm, gas, diffused, sems):
-    fields, extent_x, extent_y, extent_z = gas.shape
-    across_y = extent_y // TILE_Y
-    across_z = extent_z // TILE_Z
-    lane = lax.broadcasted_iota(jnp.int32, (extent_y, extent_z), 1)
-    line = lax.broadcasted_iota(jnp.int32, (extent_y, extent_z), 0)
-    copy = pltpu.make_async_copy(gas_hbm, gas, sems.at[fields])
-    copy.start()
-    copy.wait()
-
-    def sent(f):
-        return pltpu.make_async_copy(diffused.at[f], diffused_hbm.at[f], sems.at[f])
-
-    def per_field(f, carry):
-        for x in range(extent_x):
-            centre = gas[f, x]
-            beside = jnp.where(line == 0, 0.0, roll(centre, 1, 0))
-            beside += jnp.where(line == extent_y - 1, 0.0, roll(centre, -1, 0))
-            beside += jnp.where(lane == 0, 0.0, roll(centre, 1, 1))
-            beside += jnp.where(lane == extent_z - 1, 0.0, roll(centre, -1, 1))
-            if x > 0:
-                beside += gas[f, x - 1]
-            if x < extent_x - 1:
-                beside += gas[f, x + 1]
-            diffused[f, x * extent_y : (x + 1) * extent_y, :] = centre + DIFFUSION * (beside - 6.0 * centre)
-        sent(f).start()
-        return carry
-
-    lax.fori_loop(0, fields, per_field, 0)
 
     def per_a(a, carry):
         for f in range(FLOWS):
@@ -163,8 +131,6 @@
         return carry
 
     lax.fori_loop(0, extent_x // TILE_X, per_a, 0)
-    for f in range(fields):
-        sent(f).wait()
 
 
 def paired(ref, member, stride, offset, capacity):
@@ -267,8 +233,8 @@
 
 
 def deposit_kernel(
-    ids_vmem, message, result, diffused, from_x0, from_x1, from_y0, from_y1, gas_next,
-    total, source, ids, work, sems, *, rows, capacity
+    ids_vmem, message, result, gas_hbm, from_x0, from_x1, from_y0, from_y1, gas_next,
+    total, source, ids, gas, work, sems, *, rows, capacity
 ):
     fields, extent_x, extent_z = from_y0.shape
     extent_y = from_x0.shape[1]
@@ -280,7 +246,7 @@
     across_i = result.shape[0]
     copy = pltpu.make_async_copy(ids_vmem, ids, sems.at[0])
     copy.start()
-    fetch = pltpu.make_async_copy(diffused, work, sems.at[1])
+    fetch = pltpu.make_async_copy(gas_hbm, gas, sems.at[1])
     fetch.start()
     total[...] = jnp.zeros(total.shape, total.dtype)
 
@@ -347,16 +313,22 @@
     lax.fori_loop(0, blocks // unroll, per_step, 0)
 
     fetch.wait()
-    last_x = (extent_x - 1) * extent_y
-    for f in range(fields):
-        work[f, 0:extent_y, :] += DIFFUSION * from_x0[f]
-        work[f, last_x : last_x + extent_y, :] += DIFFUSION * from_x1[f]
-        for h in range(extent_z // LANES):
-            lanes = slice(h * LANES, (h + 1) * LANES)
-            for line, face in ((0, from_y0), (extent_y - 1, from_y1)):
-                for x in range(extent_x):
-                    spot = x * extent_y + line
-                    work[f, spot : spot + 1, lanes] += DIFFUSION * face[f, x : x + 1, lanes]
+    lane = lax.broadcasted_iota(jnp.int32, (extent_y, extent_z), 1)
+    line = lax.broadcasted_iota(jnp.int32, (extent_y, extent_z), 0)
+
+    def per_field(f, carry):
+        for x in range(extent_x):
+            centre = gas[f, x]
+            beside = from_x0[f] if x == 0 else gas[f, x - 1]
+            beside += from_x1[f] if x == extent_x - 1 else gas[f, x + 1]
+            beside += jnp.where(line == 0, from_y0[f, x : x + 1, :], roll(centre, 1, 0))
+            beside += jnp.where(line == extent_y - 1, from_y1[f, x : x + 1, :], roll(centre, -1, 0))
+            beside += jnp.where(lane == 0, 0.0, roll(centre, 1, 1))
+            beside += jnp.where(lane == extent_z - 1, 0.0, roll(centre, -1, 1))
+            work[f, x * extent_y : (x + 1) * extent_y, :] = centre + DIFFUSION * (beside - 6.0 * centre)
+        return carry
+
+    lax.fori_loop(0, fields, per_field, 0)
 
     def sent(a):
         place = pl.ds(pl.multiple_of(a * TILE_X * extent_y, SUB), TILE_X * extent_y)
@@ -491,8 +463,8 @@
     side = shape(fields, extent_y, extent_z)
     whole = vmem(gas_state.shape, f32)
     flat = (fields, extent_x * extent_y, extent_z)
-    face_x0, face_x1, face_y0, face_y1 = call(
-        faces_kernel, (side, side, face, face), scratch=[whole, dma(())], ins=[hbm], outs=[vmem] * 4
+    table, face_x0, face_x1, face_y0, face_y1 = call(
+        table_kernel, (shape(FLOWS, tiles, LANES), side, side, face, face), flops=10**7
     )(gas_state)
 
     def shifted(value, axis, step):
@@ -503,16 +475,6 @@
     halo = (
         shifted(face_x1, "gx", 1), shifted(face_x0, "gx", -1), shifted(face_y1, "yz", 1), shifted(face_y0, "yz", -1)
     )
-    table, diffused = call(
-        local_kernel,
-        (shape(FLOWS, tiles, LANES), shape(*flat)),
-        scratch=[whole, vmem(flat, f32), dma((fields + 1,))],
-        flops=10**7,
-        ins=[hbm],
-        outs=[vmem, hbm],
-    )(gas_state)
-    message, table, diffused = lax.optimization_barrier((message, table, diffused))
-
     returned, result, ids = call(
         functools.partial(update_kernel, rows=rows, capacity=capacity),
         (
@@ -539,13 +501,14 @@
             vmem((tiles * SUB, LANES), f32),
             vmem((blocks * SUB, LANES), f32),
             pltpu.SMEM((devices, LANES), i32),
+            whole,
             vmem(flat, f32),
             dma((2 + extent_x // TILE_X,)),
         ],
         flops=3 * 10**7,
         ins=[vmem, vmem, vmem, hbm] + [vmem] * 4,
         outs=[hbm],
-    )(ids, message, result, diffused, *halo)
+    )(ids, message, result, gas_state, *halo)
     speed_next, mass_next = call(
         unpack_kernel,
         (shape(devices, vector, 1, LANES), shape(devices, capacity, 1, LANES)),

time: 57.9 us -> 57.3 us (0.990)
  Pallas kernels: 16.2 us -> 13.4 us
  waiting for transfers between devices: 19.1 us -> 21.4 us
    pallas_call x6 -> x5, Pallas kernels: 16.2 us -> 13.4 us  [with_spaces(): return called(*values)]
    all_to_all x1, waiting for transfers between devices: 14.3 us -> 16.7 us  [step(): lax.all_to_all(message.reshape(devices, rows, 1, LANES), SENT, split_axis...]
  transfers between devices with their start and end apart: 6 -> 6, of which waited for: 3 -> 3; matrix products, arithmetic and copies ran while one was open for 0% -> 0% of each run, Pallas kernels for 19% -> 14%
where the time goes in v8:
time: 57.3 us; the launch traced here: 56.9 us
  starting transfers between devices  21.4 us (37%)
  waiting for transfers between devices  21.4 us (37%)
  Pallas kernels  13.4 us (23%)
  between operations  0.75 us (1%)
    all_to_all x1, waiting for transfers between devices, step(): lax.all_to_all(message.reshape(devices, rows, 1, LANES), SENT, split_axis...  16.7 us
    pallas_call x5, Pallas kernels, with_spaces(): return called(*values)  13.4 us
    ppermute x4, starting transfers between devices, shifted(): return lax.ppermute(value, axis, pairs)  11.4 us
    all_to_all x1, starting transfers between devices, step(): lax.all_to_all(message.reshape(devices, rows, 1, LANES), SENT, split_axis...  6.08 us
    ppermute x4, waiting for transfers between devices, shifted(): return lax.ppermute(value, axis, pairs)  4.74 us
    all_to_all x1, starting transfers between devices, step(): lax.all_to_all(returned.reshape(devices, capacity * FLOWS, 1, LANES), RET...  3.89 us
  transfers between devices with their start and end apart: 6, of which 3 were waited for; matrix products, arithmetic and copies ran while one was open for 0% of the time, Pallas kernels for 14%

profile of v8, /device:TPU:6, one launch (start us, length us, event | category | flops | bytes accessed | tf_op | source)
XLA Modules:
  0.0 56.9 jit_solution(5388071772652477066)
XLA Ops:
  0.6 0.0 copy-start
  0.6 2.1 %shard_map.94 = f32[1312,128]{1,0:T(8,128)} custom-call(f32[4,96,128]{2,1,0:T(8,128)} %bitcast.35, f32[4,32,128]{2,1,0:T(8,128)} %bitcast.38, f32[4,96,128]{2,1,0:T(8,128)} %bitcast.36, s32[4,96,128]{2,1,0:T(8,128)} %bitcast.37, s32[4,32]{1,0:T(4,128)} %bitcast.39, s32[1,32]{1,0:T(1,128)} %bitcast.40), custom_call_target="tpu_custom_call" | custom-call | tf_op jit(solution)/shard_map/pallas_call | solution.py:409
  2.7 6.1 %all-to-all-start = ((f32[32,41,1,128]{3,2,1,0:T(1,128)}), f32[32,41,1,128]{3,2,1,0:T(1,128)S(1)}, u32[]{:S(2)}, u32[]{:S(2)}) async-start(f32[32,41,1,128]{3,2,1,0:T(1,128)} %bitcast.32), calls=%async_computation | async-start | bytes 1343488 | tf_op jit(solution)/shard_map/all_to_all | solution.py:459
  8.8 0.0 copy-done
  8.8 1.2 %shard_map.95 = (f32[4,512,128]{2,1,0:T(8,128)S(1)}, f32[5,16,256]{2,1,0:T(8,128)S(1)}, f32[5,16,256]{2,1,0:T(8,128)S(1)}, f32[5,16,256]{2,1,0:T(8,128)S(1)}, f32[5,16,256]{2,1,0:T(8,128)S(1)}) custom-call(f32[5,16,16,256]{3,2,1,0:T(8,128)S(1)} %copy-done), custom_call_target="tpu_custom_call" | custom-call | flops 10000000 | tf_op jit(solution)/shard_map/pallas_call | solution.py:409
  10.0 16.7 %all-to-all-done = f32[32,41,1,128]{3,2,1,0:T(1,128)S(1)} async-done(((f32[32,41,1,128]{3,2,1,0:T(1,128)}), f32[32,41,1,128]{3,2,1,0:T(1,128)S(1)}, u32[]{:S(2)}, u32[]{:S(2)}) %all-to-all-start) | async-done | bytes 671776 | tf_op jit(solution)/shard_map/all_to_all | solution.py:459
  26.7 2.4 %shard_map.96 = (f32[4,128,128]{2,1,0:T(8,128)}, f32[4,128,128]{2,1,0:T(8,128)S(1)}, s32[32,128]{1,0:T(8,128)S(1)}) custom-call(f32[1312,128]{1,0:T(8,128)S(1)} %bitcast.30, f32[4,512,128]{2,1,0:T(8,128)S(1)} %get-tuple-element.13.table), custom_call_target="tpu_custom_call" | custom-call | flops 10000000 | tf_op jit(solution)/shard_map/pallas_call | solution.py:409
  29.1 3.9 %all-to-all-start.1 = ((f32[32,16,1,128]{3,2,1,0:T(1,128)}), f32[32,16,1,128]{3,2,1,0:T(1,128)S(1)}, u32[]{:S(2)}, u32[]{:S(2)}) async-start(f32[32,16,1,128]{3,2,1,0:T(1,128)} %bitcast.34), calls=%async_computation.1 | async-start | bytes 524288 | tf_op jit(solution)/shard_map/all_to_all | solution.py:494
  33.0 2.0 %collective-permute-start = (f32[5,16,256]{2,1,0:T(8,128)S(1)}, f32[5,16,256]{2,1,0:T(8,128)S(1)}, u32[]{:S(2)}, u32[]{:S(2)}) collective-permute-start(f32[5,16,256]{2,1,0:T(8,128)S(1)} %get-tuple-element.16), channel_id=1, source_target_pairs={{0,8},{8,16},{16,24},{1,9},{9,17},{17,25},{2,10},{10,18},{18,26},{... | collective-permute-start | bytes 245768 | tf_op jit(solution)/shard_map/ppermute | solution.py:473
  35.0 3.5 %collective-permute-start.1 = (f32[5,16,256]{2,1,0:T(8,128)S(1)}, f32[5,16,256]{2,1,0:T(8,128)S(1)}, u32[]{:S(2)}, u32[]{:S(2)}) collective-permute-start(f32[5,16,256]{2,1,0:T(8,128)S(1)} %get-tuple-element.17), channel_id=1, source_target_pairs={{8,0},{16,8},{24,16},{9,1},{17,9},{25,17},{10,2},{18,10},{26,18},{... | collective-permute-start | bytes 245768 | tf_op jit(solution)/shard_map/ppermute | solution.py:473
  38.6 3.4 %collective-permute-start.2 = (f32[5,16,256]{2,1,0:T(8,128)S(1)}, f32[5,16,256]{2,1,0:T(8,128)S(1)}, u32[]{:S(2)}, u32[]{:S(2)}) collective-permute-start(f32[5,16,256]{2,1,0:T(8,128)S(1)} %get-tuple-element.18), channel_id=1, source_target_pairs={{0,1},{1,2},{2,3},{3,4},{4,5},{5,6},{6,7},{8,9},{9,10},{10,11},{11... | collective-permute-start | bytes 245768 | tf_op jit(solution)/shard_map/ppermute | solution.py:473
  42.0 2.5 %collective-permute-start.3 = (f32[5,16,256]{2,1,0:T(8,128)S(1)}, f32[5,16,256]{2,1,0:T(8,128)S(1)}, u32[]{:S(2)}, u32[]{:S(2)}) collective-permute-start(f32[5,16,256]{2,1,0:T(8,128)S(1)} %get-tuple-element.19), channel_id=1, source_target_pairs={{1,0},{2,1},{3,2},{4,3},{5,4},{6,5},{7,6},{9,8},{10,9},{11,10},{12... | collective-permute-start | bytes 245768 | tf_op jit(solution)/shard_map/ppermute | solution.py:473
  44.4 0.0 collective-permute-done.from_x0
  44.4 0.0 collective-permute-done.1.from_x1
  44.5 0.5 collective-permute-done.2.from_y0
  44.9 4.3 %collective-permute-done.3.from_y1 = f32[5,16,256]{2,1,0:T(8,128)S(1)} collective-permute-done((f32[5,16,256]{2,1,0:T(8,128)S(1)}, f32[5,16,256]{2,1,0:T(8,128)S(1)}, u32[]{:S(2)}, u32[]{:S(2)}) %collective-permute-start.3) | collective-permute-done | bytes 81952 | tf_op jit(solution)/shard_map/ppermute | solution.py:473
  49.2 7.0 %shard_map.97 = f32[5,256,256]{2,1,0:T(8,128)} custom-call(s32[32,128]{1,0:T(8,128)S(1)} %get-tuple-element.14.ids_vmem, f32[1312,128]{1,0:T(8,128)S(1)} %bitcast.31, f32[4,128,128]{2,1,0:T(8,128)S(1)} %get-tuple-element.15.result, f32[5,16,16,256]{3,2,1,0:T(8,128)} %gas_hbm.1, f32[5,16,256]{2,1,0:T(8,128)S(1)} %collective-permute-done.from_x0, ...), custom_call_target="tpu_custom_call" | custom-call | flops 30000000 | tf_op jit(solution)/shard_map/pallas_call | solution.py:409
  56.2 0.0 all-to-all-done.1.result
  56.2 0.7 %shard_map.98 = (f32[32,12,1,128]{3,2,1,0:T(1,128)}, f32[32,4,1,128]{3,2,1,0:T(1,128)}) custom-call(f32[32,16,1,128]{3,2,1,0:T(1,128)S(1)} %all-to-all-done.1.result), custom_call_target="tpu_custom_call" | custom-call | tf_op jit(solution)/shard_map/pallas_call | solution.py:409
Async XLA Ops:
  0.6 8.2 %copy-start = (f32[5,16,16,256]{3,2,1,0:T(8,128)S(1)}, f32[5,16,16,256]{3,2,1,0:T(8,128)}, u32[]{:S(2)}) copy-start(f32[5,16,16,256]{3,2,1,0:T(8,128)} %gas_hbm.1) | copy-start | bytes 3932164
  2.7 23.9 %all-to-all-start = ((f32[32,41,1,128]{3,2,1,0:T(1,128)}), f32[32,41,1,128]{3,2,1,0:T(1,128)S(1)}, u32[]{:S(2)}, u32[]{:S(2)}) async-start(f32[32,41,1,128]{3,2,1,0:T(1,128)} %bitcast.32), calls=%async_computation | async-start | bytes 1343488 | tf_op jit(solution)/shard_map/all_to_all | solution.py:459
  29.1 27.1 %all-to-all-start.1 = ((f32[32,16,1,128]{3,2,1,0:T(1,128)}), f32[32,16,1,128]{3,2,1,0:T(1,128)S(1)}, u32[]{:S(2)}, u32[]{:S(2)}) async-start(f32[32,16,1,128]{3,2,1,0:T(1,128)} %bitcast.34), calls=%async_computation.1 | async-start | bytes 524288 | tf_op jit(solution)/shard_map/all_to_all | solution.py:494
  33.0 11.4 %collective-permute-start = (f32[5,16,256]{2,1,0:T(8,128)S(1)}, f32[5,16,256]{2,1,0:T(8,128)S(1)}, u32[]{:S(2)}, u32[]{:S(2)}) collective-permute-start(f32[5,16,256]{2,1,0:T(8,128)S(1)} %get-tuple-element.16), channel_id=1, source_target_pairs={{0,8},{8,16},{16,24},{1,9},{9,17},{17,25},{2,10},{10,18},{18,26},{... | collective-permute-start | bytes 245768 | tf_op jit(solution)/shard_map/ppermute | solution.py:473
  35.0 9.4 %collective-permute-start.1 = (f32[5,16,256]{2,1,0:T(8,128)S(1)}, f32[5,16,256]{2,1,0:T(8,128)S(1)}, u32[]{:S(2)}, u32[]{:S(2)}) collective-permute-start(f32[5,16,256]{2,1,0:T(8,128)S(1)} %get-tuple-element.17), channel_id=1, source_target_pairs={{8,0},{16,8},{24,16},{9,1},{17,9},{25,17},{10,2},{18,10},{26,18},{... | collective-permute-start | bytes 245768 | tf_op jit(solution)/shard_map/ppermute | solution.py:473
  38.6 6.3 %collective-permute-start.2 = (f32[5,16,256]{2,1,0:T(8,128)S(1)}, f32[5,16,256]{2,1,0:T(8,128)S(1)}, u32[]{:S(2)}, u32[]{:S(2)}) collective-permute-start(f32[5,16,256]{2,1,0:T(8,128)S(1)} %get-tuple-element.18), channel_id=1, source_target_pairs={{0,1},{1,2},{2,3},{3,4},{4,5},{5,6},{6,7},{8,9},{9,10},{10,11},{11... | collective-permute-start | bytes 245768 | tf_op jit(solution)/shard_map/ppermute | solution.py:473
  42.0 7.2 %collective-permute-start.3 = (f32[5,16,256]{2,1,0:T(8,128)S(1)}, f32[5,16,256]{2,1,0:T(8,128)S(1)}, u32[]{:S(2)}, u32[]{:S(2)}) collective-permute-start(f32[5,16,256]{2,1,0:T(8,128)S(1)} %get-tuple-element.19), channel_id=1, source_target_pairs={{1,0},{2,1},{3,2},{4,3},{5,4},{6,5},{7,6},{9,8},{10,9},{11,10},{12... | collective-permute-start | bytes 245768 | tf_op jit(solution)/shard_map/ppermute | solution.py:473

commit v9 on v8

--- a/solution.py
+++ b/solution.py
@@ -144,7 +144,7 @@
 
 
 def update_kernel(
-    message, table, result_hbm, result, ids_vmem, products, turned, sems, *, rows, capacity
+    message, table, result_hbm, result, ids_vmem, turned, sems, *, rows, capacity
 ):
     devices = message.shape[0] // rows
     group = SUB * rows
@@ -180,6 +180,7 @@
 
             first = ((both(6) * TILE_Y + both(7)) * TILE_Z + both(8)).astype(jnp.int32)
             alive = jnp.zeros((SUB, LANES), jnp.int32)
+            made = [[] for _ in range(FLOWS)]
             for j in range(2 * capacity):
                 i, k = 2 * step + j // capacity, j % capacity
                 base = i * rows
@@ -196,14 +197,18 @@
                 for f in range(FLOWS):
                     held = jnp.broadcast_to(table[f, pl.ds(safe, 1), :], (SUB, LANES))
                     found = jnp.take_along_axis(held, index, axis=1, mode="promise_in_bounds")
-                    products[(f * SUB + j) * SUB : (f * SUB + j + 1) * SUB, :] = found * weight
+                    made[f].append(found * weight)
             live = alive >= 0
             sampled = []
-            for f in range(FLOWS):
-                total = products[pl.ds(f * SUB * SUB, SUB, stride=SUB), :]
-                for c in range(1, SUB):
-                    total = total + products[pl.ds(f * SUB * SUB + c, SUB, stride=SUB), :]
-                sampled.append(total)
+            for level in made:
+                for size in (4, 2, 1):
+                    keep = (row & size) == 0
+                    half = len(level) // 2
+                    level = [
+                        jnp.where(keep, x, roll(y, size, 0)) + jnp.where(keep, roll(x, -size, 0), y)
+                        for x, y in zip(level[:half], level[half:])
+                    ]
+                sampled.append(level[0])
 
             mass_old = both(9)
             radius = jnp.exp(jnp.log(mass_old) * (1.0 / 3.0))
@@ -223,7 +228,7 @@
         returned(g).start()
         return carry
 
-    lax.fori_loop(0, devices // SUB, per_group, 0)
+    lax.fori_loop(0, devices // SUB, per_group, 0, unroll=4)
     for g in range(devices // SUB):
         returned(g).wait()
 
@@ -483,7 +488,6 @@
             shape(devices, LANES, dtype=i32),
         ),
         scratch=[
-            vmem((FLOWS * SUB * SUB, LANES), f32),
             vmem((capacity, devices, LANES), i32),
             dma((devices // SUB,)),
         ],

time: 57.3 us -> 56.7 us (0.990)
  Pallas kernels: 13.4 us -> 12.8 us
where the time goes in v9:
time: 56.7 us; the launch traced here: 56.4 us
  starting transfers between devices  21.4 us (38%)
  waiting for transfers between devices  21.4 us (38%)
  Pallas kernels  12.8 us (23%)
  between operations  0.75 us (1%)
    all_to_all x1, waiting for transfers between devices, step(): lax.all_to_all(message.reshape(devices, rows, 1, LANES), SENT, split_axis...  16.7 us
    pallas_call x5, Pallas kernels, with_spaces(): return called(*values)  12.8 us
    ppermute x4, starting transfers between devices, shifted(): return lax.ppermute(value, axis, pairs)  11.4 us
    all_to_all x1, starting transfers between devices, step(): lax.all_to_all(message.reshape(devices, rows, 1, LANES), SENT, split_axis...  6.08 us
    ppermute x4, waiting for transfers between devices, shifted(): return lax.ppermute(value, axis, pairs)  4.74 us
    all_to_all x1, starting transfers between devices, step(): lax.all_to_all(returned.reshape(devices, capacity * FLOWS, 1, LANES), RET...  3.89 us
  transfers between devices with their start and end apart: 6, of which 3 were waited for; matrix products, arithmetic and copies ran while one was open for 0% of the time, Pallas kernels for 14%

profile of v9, /device:TPU:6, one launch (start us, length us, event | category | flops | bytes accessed | tf_op | source)
XLA Modules:
  0.0 56.4 jit_solution(14731392546917798384)
XLA Ops:
  0.6 0.0 copy-start
  0.6 2.1 %shard_map.94 = f32[1312,128]{1,0:T(8,128)} custom-call(f32[4,96,128]{2,1,0:T(8,128)} %bitcast.35, f32[4,32,128]{2,1,0:T(8,128)} %bitcast.38, f32[4,96,128]{2,1,0:T(8,128)} %bitcast.36, s32[4,96,128]{2,1,0:T(8,128)} %bitcast.37, s32[4,32]{1,0:T(4,128)} %bitcast.39, s32[1,32]{1,0:T(1,128)} %bitcast.40), custom_call_target="tpu_custom_call" | custom-call | tf_op jit(solution)/shard_map/pallas_call | solution.py:414
  2.7 6.1 %all-to-all-start = ((f32[32,41,1,128]{3,2,1,0:T(1,128)}), f32[32,41,1,128]{3,2,1,0:T(1,128)S(1)}, u32[]{:S(2)}, u32[]{:S(2)}) async-start(f32[32,41,1,128]{3,2,1,0:T(1,128)} %bitcast.32), calls=%async_computation | async-start | bytes 1343488 | tf_op jit(solution)/shard_map/all_to_all | solution.py:464
  8.8 0.0 copy-done
  8.8 1.2 %shard_map.95 = (f32[4,512,128]{2,1,0:T(8,128)S(1)}, f32[5,16,256]{2,1,0:T(8,128)S(1)}, f32[5,16,256]{2,1,0:T(8,128)S(1)}, f32[5,16,256]{2,1,0:T(8,128)S(1)}, f32[5,16,256]{2,1,0:T(8,128)S(1)}) custom-call(f32[5,16,16,256]{3,2,1,0:T(8,128)S(1)} %copy-done), custom_call_target="tpu_custom_call" | custom-call | flops 10000000 | tf_op jit(solution)/shard_map/pallas_call | solution.py:414
  10.0 16.7 %all-to-all-done = f32[32,41,1,128]{3,2,1,0:T(1,128)S(1)} async-done(((f32[32,41,1,128]{3,2,1,0:T(1,128)}), f32[32,41,1,128]{3,2,1,0:T(1,128)S(1)}, u32[]{:S(2)}, u32[]{:S(2)}) %all-to-all-start) | async-done | bytes 671776 | tf_op jit(solution)/shard_map/all_to_all | solution.py:464
  26.7 1.9 %shard_map.96 = (f32[4,128,128]{2,1,0:T(8,128)}, f32[4,128,128]{2,1,0:T(8,128)S(1)}, s32[32,128]{1,0:T(8,128)S(1)}) custom-call(f32[1312,128]{1,0:T(8,128)S(1)} %bitcast.30, f32[4,512,128]{2,1,0:T(8,128)S(1)} %get-tuple-element.13.table), custom_call_target="tpu_custom_call" | custom-call | flops 10000000 | tf_op jit(solution)/shard_map/pallas_call | solution.py:414
  28.6 3.9 %all-to-all-start.1 = ((f32[32,16,1,128]{3,2,1,0:T(1,128)}), f32[32,16,1,128]{3,2,1,0:T(1,128)S(1)}, u32[]{:S(2)}, u32[]{:S(2)}) async-start(f32[32,16,1,128]{3,2,1,0:T(1,128)} %bitcast.34), calls=%async_computation.1 | async-start | bytes 524288 | tf_op jit(solution)/shard_map/all_to_all | solution.py:498
  32.5 2.0 %collective-permute-start = (f32[5,16,256]{2,1,0:T(8,128)S(1)}, f32[5,16,256]{2,1,0:T(8,128)S(1)}, u32[]{:S(2)}, u32[]{:S(2)}) collective-permute-start(f32[5,16,256]{2,1,0:T(8,128)S(1)} %get-tuple-element.16), channel_id=1, source_target_pairs={{0,8},{8,16},{16,24},{1,9},{9,17},{17,25},{2,10},{10,18},{18,26},{... | collective-permute-start | bytes 245768 | tf_op jit(solution)/shard_map/ppermute | solution.py:478
  34.5 3.5 %collective-permute-start.1 = (f32[5,16,256]{2,1,0:T(8,128)S(1)}, f32[5,16,256]{2,1,0:T(8,128)S(1)}, u32[]{:S(2)}, u32[]{:S(2)}) collective-permute-start(f32[5,16,256]{2,1,0:T(8,128)S(1)} %get-tuple-element.17), channel_id=1, source_target_pairs={{8,0},{16,8},{24,16},{9,1},{17,9},{25,17},{10,2},{18,10},{26,18},{... | collective-permute-start | bytes 245768 | tf_op jit(solution)/shard_map/ppermute | solution.py:478
  38.0 3.4 %collective-permute-start.2 = (f32[5,16,256]{2,1,0:T(8,128)S(1)}, f32[5,16,256]{2,1,0:T(8,128)S(1)}, u32[]{:S(2)}, u32[]{:S(2)}) collective-permute-start(f32[5,16,256]{2,1,0:T(8,128)S(1)} %get-tuple-element.18), channel_id=1, source_target_pairs={{0,1},{1,2},{2,3},{3,4},{4,5},{5,6},{6,7},{8,9},{9,10},{10,11},{11... | collective-permute-start | bytes 245768 | tf_op jit(solution)/shard_map/ppermute | solution.py:478
  41.4 2.5 %collective-permute-start.3 = (f32[5,16,256]{2,1,0:T(8,128)S(1)}, f32[5,16,256]{2,1,0:T(8,128)S(1)}, u32[]{:S(2)}, u32[]{:S(2)}) collective-permute-start(f32[5,16,256]{2,1,0:T(8,128)S(1)} %get-tuple-element.19), channel_id=1, source_target_pairs={{1,0},{2,1},{3,2},{4,3},{5,4},{6,5},{7,6},{9,8},{10,9},{11,10},{12... | collective-permute-start | bytes 245768 | tf_op jit(solution)/shard_map/ppermute | solution.py:478
  43.9 0.0 collective-permute-done.from_x0
  43.9 0.0 collective-permute-done.1.from_x1
  43.9 0.5 collective-permute-done.2.from_y0
  44.4 4.3 %collective-permute-done.3.from_y1 = f32[5,16,256]{2,1,0:T(8,128)S(1)} collective-permute-done((f32[5,16,256]{2,1,0:T(8,128)S(1)}, f32[5,16,256]{2,1,0:T(8,128)S(1)}, u32[]{:S(2)}, u32[]{:S(2)}) %collective-permute-start.3) | collective-permute-done | bytes 81952 | tf_op jit(solution)/shard_map/ppermute | solution.py:478
  48.6 7.0 %shard_map.97 = f32[5,256,256]{2,1,0:T(8,128)} custom-call(s32[32,128]{1,0:T(8,128)S(1)} %get-tuple-element.14.ids_vmem, f32[1312,128]{1,0:T(8,128)S(1)} %bitcast.31, f32[4,128,128]{2,1,0:T(8,128)S(1)} %get-tuple-element.15.result, f32[5,16,16,256]{3,2,1,0:T(8,128)} %gas_hbm.1, f32[5,16,256]{2,1,0:T(8,128)S(1)} %collective-permute-done.from_x0, ...), custom_call_target="tpu_custom_call" | custom-call | flops 30000000 | tf_op jit(solution)/shard_map/pallas_call | solution.py:414
  55.6 0.0 all-to-all-done.1.result
  55.7 0.7 %shard_map.98 = (f32[32,12,1,128]{3,2,1,0:T(1,128)}, f32[32,4,1,128]{3,2,1,0:T(1,128)}) custom-call(f32[32,16,1,128]{3,2,1,0:T(1,128)S(1)} %all-to-all-done.1.result), custom_call_target="tpu_custom_call" | custom-call | tf_op jit(solution)/shard_map/pallas_call | solution.py:414
Async XLA Ops:
  0.6 8.2 %copy-start = (f32[5,16,16,256]{3,2,1,0:T(8,128)S(1)}, f32[5,16,16,256]{3,2,1,0:T(8,128)}, u32[]{:S(2)}) copy-start(f32[5,16,16,256]{3,2,1,0:T(8,128)} %gas_hbm.1) | copy-start | bytes 3932164
  2.7 23.9 %all-to-all-start = ((f32[32,41,1,128]{3,2,1,0:T(1,128)}), f32[32,41,1,128]{3,2,1,0:T(1,128)S(1)}, u32[]{:S(2)}, u32[]{:S(2)}) async-start(f32[32,41,1,128]{3,2,1,0:T(1,128)} %bitcast.32), calls=%async_computation | async-start | bytes 1343488 | tf_op jit(solution)/shard_map/all_to_all | solution.py:464
  28.6 27.1 %all-to-all-start.1 = ((f32[32,16,1,128]{3,2,1,0:T(1,128)}), f32[32,16,1,128]{3,2,1,0:T(1,128)S(1)}, u32[]{:S(2)}, u32[]{:S(2)}) async-start(f32[32,16,1,128]{3,2,1,0:T(1,128)} %bitcast.34), calls=%async_computation.1 | async-start | bytes 524288 | tf_op jit(solution)/shard_map/all_to_all | solution.py:498
  32.5 11.4 %collective-permute-start = (f32[5,16,256]{2,1,0:T(8,128)S(1)}, f32[5,16,256]{2,1,0:T(8,128)S(1)}, u32[]{:S(2)}, u32[]{:S(2)}) collective-permute-start(f32[5,16,256]{2,1,0:T(8,128)S(1)} %get-tuple-element.16), channel_id=1, source_target_pairs={{0,8},{8,16},{16,24},{1,9},{9,17},{17,25},{2,10},{10,18},{18,26},{... | collective-permute-start | bytes 245768 | tf_op jit(solution)/shard_map/ppermute | solution.py:478
  34.5 9.4 %collective-permute-start.1 = (f32[5,16,256]{2,1,0:T(8,128)S(1)}, f32[5,16,256]{2,1,0:T(8,128)S(1)}, u32[]{:S(2)}, u32[]{:S(2)}) collective-permute-start(f32[5,16,256]{2,1,0:T(8,128)S(1)} %get-tuple-element.17), channel_id=1, source_target_pairs={{8,0},{16,8},{24,16},{9,1},{17,9},{25,17},{10,2},{18,10},{26,18},{... | collective-permute-start | bytes 245768 | tf_op jit(solution)/shard_map/ppermute | solution.py:478
  38.0 6.3 %collective-permute-start.2 = (f32[5,16,256]{2,1,0:T(8,128)S(1)}, f32[5,16,256]{2,1,0:T(8,128)S(1)}, u32[]{:S(2)}, u32[]{:S(2)}) collective-permute-start(f32[5,16,256]{2,1,0:T(8,128)S(1)} %get-tuple-element.18), channel_id=1, source_target_pairs={{0,1},{1,2},{2,3},{3,4},{4,5},{5,6},{6,7},{8,9},{9,10},{10,11},{11... | collective-permute-start | bytes 245768 | tf_op jit(solution)/shard_map/ppermute | solution.py:478
  41.4 7.2 %collective-permute-start.3 = (f32[5,16,256]{2,1,0:T(8,128)S(1)}, f32[5,16,256]{2,1,0:T(8,128)S(1)}, u32[]{:S(2)}, u32[]{:S(2)}) collective-permute-start(f32[5,16,256]{2,1,0:T(8,128)S(1)} %get-tuple-element.19), channel_id=1, source_target_pairs={{1,0},{2,1},{3,2},{4,3},{5,4},{6,5},{7,6},{9,8},{10,9},{11,10},{12... | collective-permute-start | bytes 245768 | tf_op jit(solution)/shard_map/ppermute | solution.py:478
